TPU v7x, 128 devices: a whole 4x4x4 slice. The times are simulated.
128 devices in a mesh: aa: 8 (over x, core), ba: 16 (over z, y).
Axes of the slice: x: 4, y: 4, z: 4, core: 2. Of those that a mesh axis runs over, the one named last changes fastest.
Arguments:
- initial_dictionary_matrix: bfloat16 [65536, 3584], P('ba', 'aa'), may hold values from -60 to 60
- decoder_two: bfloat16 [65536, 3584], P('ba', 'aa'), may hold values from -60 to 60
- route_one: int32 [16, 16], replicated, may hold values from 0 to 7
- route_two: int32 [16, 16], replicated, may hold values from 0 to 7
- candidate_pair_slots: int32 [16, 24, 2], P('ba'), may hold values from 0 to 15
Outputs:
- leading_logarithmic_factor: float32 [65536], P('ba')
- col_log_scale: float32 [65536], P('ba')
All inputs are finite; a program needn't handle non-finite values.
Results may differ from a plain program's by a relative error of at most 0.00046.
Values may be sent and summed in bfloat16 or wider, within the bound.
No kernel may reach another device: no remote copies, remote signals or barrier semaphores. Data moves between devices by JAX's collectives and lax.ppermute only.
A program may use at most 128 MiB of HBM per device.

v0:
```python
import jax
import jax.numpy as jnp
from jax import lax
from jax.sharding import Mesh
from jax.sharding import PartitionSpec as P

BS = 512
SWEEPS = 4
BA = ("ba_0", "ba_1")
AA = ("aa_0", "aa_1")


smoothing_regularizer = 0.02
norm_floor = 1e-06


def split_up(x, dim, size):
    lengths = x.shape
    parts = x.reshape(*lengths[:dim], size, lengths[dim] // size, *lengths[dim + 1 :])
    return jnp.moveaxis(parts, dim, 0)


def summed_on_arrival(x, axis, dim):
    parts = split_up(x, dim, lax.axis_size(axis))
    arrived = lax.all_to_all(parts, axis, split_axis=0, concat_axis=0, tiled=True)
    return arrived.sum(axis=0)


def summed_rows(x, axes, dim):
    far, near = axes
    own = summed_on_arrival(split_up(x, dim, lax.axis_size(far)), near, dim + 1)
    return jnp.sum(lax.all_to_all(own, far, 0, 0, tiled=True), axis=0)


def rows_for(lines, size):
    spare = -len(lines) % size
    return jnp.pad(lines, [(0, spare)] + [(0, 0)] * (lines.ndim - 1))


def from_everyone(x, axis):
    size = lax.axis_size(axis)
    return lax.all_to_all(jnp.broadcast_to(x[None], (size, *x.shape)), axis, 0, 0, tiled=True)


def laid_out(parts, dim):
    lengths = list(parts.shape[1:])
    lengths[dim] *= parts.shape[0]
    return jnp.moveaxis(parts, 0, dim).reshape(lengths)


def gathered_by_axis(x, axes, dim):
    far, near = axes
    parts = from_everyone(from_everyone(x, far), near)
    return laid_out(parts.swapaxes(0, 1).reshape(-1, *x.shape), dim)


def nested_sum(x, axes):
    lines = x.reshape(-1, x.shape[-1])
    own = summed_rows(rows_for(lines, lax.axis_size(axes[0]) * lax.axis_size(axes[1])), axes, 0)
    whole = gathered_by_axis(own, axes, 0)
    return whole[: len(lines)].reshape(x.shape)


def taken_together(x, axis):
    return from_everyone(x, axis).sum(axis=0)


def packed_total(arrays, axis):
    ends = [0]
    for a in arrays:
        ends.append(ends[-1] + a.size)
    running = taken_together(jnp.concatenate([a.ravel() for a in arrays]), axis)
    return tuple((running[b:e].reshape(a.shape) for a, b, e in zip(arrays, ends, ends[1:])))


def in_one_piece(arrays, axis, split_dim, concat_dim, along):
    ends, at = ([], 0)
    for a in arrays[:-1]:
        at += a.shape[along]
        ends.append(at)
    both = jnp.concatenate(arrays, axis=along)
    return tuple(
        jnp.split(
            lax.all_to_all(both, axis, split_axis=split_dim, concat_axis=concat_dim, tiled=True),
            ends,
            axis=along,
        )
    )


def converge_balancing(partial_totals):
    totals = nested_sum(partial_totals, (("aa_0", "aa_1", "ba_0"), "ba_1"))
    return 1.0 / (1.0 + totals)


def per_device(initial_dictionary_matrix, decoder_two, route_one, route_two, candidate_pair_slots):
    column = lax.axis_index(BA)
    depth = lax.axis_size(AA)
    depth_index = lax.axis_index(AA)
    owners = lax.axis_size(BA)
    width = initial_dictionary_matrix.shape[1]
    blocks_dev = initial_dictionary_matrix.shape[0] // BS
    nblocks = blocks_dev * owners
    sum_one = jnp.sum(jnp.square(initial_dictionary_matrix.astype(jnp.float32)), axis=1)
    sum_two = jnp.sum(jnp.square(decoder_two.astype(jnp.float32)), axis=1)
    sum_one, sum_two = packed_total((sum_one, sum_two), AA)
    unit_one = (
        initial_dictionary_matrix.astype(jnp.float32) * lax.rsqrt(sum_one + norm_floor)[:, None]
    ).astype(jnp.bfloat16)
    unit_two = (decoder_two.astype(jnp.float32) * lax.rsqrt(sum_two + norm_floor)[:, None]).astype(
        jnp.bfloat16
    )
    send_one = jnp.take(unit_one.reshape(blocks_dev, BS, width), route_one[column], axis=0)
    second_seed_sender = jnp.take(
        unit_two.reshape(blocks_dev, BS, width), route_two[column], axis=0
    )
    got_one, got_two = in_one_piece((send_one, second_seed_sender), BA, 0, 0, 1)
    column_pairs = candidate_pair_slots[0]
    whole_pairs = column_pairs.shape[0]
    owned = whole_pairs // depth
    left = jnp.take(got_one, column_pairs[:, 0], axis=0)
    right = jnp.take(got_two, column_pairs[:, 1], axis=0)
    angular_agreement = lax.psum_scatter(
        jnp.einsum("qid,qjd->qij", left, right, preferred_element_type=jnp.float32),
        AA,
        scatter_dimension=0,
        tiled=True,
    )
    exponential_affinity = jnp.exp(angular_agreement / smoothing_regularizer)
    my_pairs = lax.dynamic_slice_in_dim(column_pairs, depth_index * owned, owned, 0)
    row_ids = my_pairs[:, 0] * blocks_dev + route_one[:, column][my_pairs[:, 0]]
    col_ids = my_pairs[:, 1] * blocks_dev + route_two[:, column][my_pairs[:, 1]]
    block_ids = jnp.arange(nblocks, dtype=jnp.int32)
    row_hot = (row_ids[:, None] == block_ids[None, :]).astype(jnp.float32)
    col_hot = (col_ids[:, None] == block_ids[None, :]).astype(jnp.float32)
    col_scale = jnp.ones((nblocks, BS), jnp.float32)
    row_scale = jnp.ones((nblocks, BS), jnp.float32)
    for sweep_index in range(SWEEPS):
        row_terms = jnp.einsum(
            "qij,qj->qi",
            exponential_affinity,
            jnp.take(col_scale, col_ids, axis=0),
            precision=lax.Precision.HIGHEST,
        )
        row_scale = converge_balancing(
            jnp.einsum("qb,qi->bi", row_hot, row_terms, precision=lax.Precision.HIGHEST)
        )
        col_terms = jnp.einsum(
            "qij,qi->qj",
            exponential_affinity,
            jnp.take(row_scale, row_ids, axis=0),
            precision=lax.Precision.HIGHEST,
        )
        col_scale = converge_balancing(
            jnp.einsum("qb,qj->bj", col_hot, col_terms, precision=lax.Precision.HIGHEST)
        )
    row_mine = lax.dynamic_slice_in_dim(row_scale, column * blocks_dev, blocks_dev, 0)
    column_local_part = lax.dynamic_slice_in_dim(col_scale, column * blocks_dev, blocks_dev, 0)
    return (jnp.log(row_mine).reshape(-1), jnp.log(column_local_part).reshape(-1))


def solution(mesh):
    torus = Mesh(mesh.devices.reshape(4, 2, 4, 4), ("aa_0", "aa_1", "ba_0", "ba_1"))
    in_specs = (P(BA, AA), P(BA, AA), P(), P(), P(BA, None, None))
    out_specs = (P(BA), P(BA))
    return jax.shard_map(
        per_device, mesh=torus, in_specs=in_specs, out_specs=out_specs, check_vma=False
    )
```

profile of v0, /device:TPU:0, one launch (start us, length us, event | category | flops | bytes accessed | tf_op | source)
XLA Modules:
  0.0 868.7 jit_solution(10147820323653711560)
XLA Ops:
  60.2 9.8 %pad_maximum_fusion = bf16[16,1024,448]{1,2,0:T(8,128)(2,1)} fusion(bf16[16,512,448]{1,2,0:T(8,128)(2,1)S(1)} %copy-done.1, bf16[16,512,448]{1,2,0:T(8,128)(2,1)} %broadcast_select_fusion.1), kind=kLoop, calls=%fused_computation.14 | loop fusion | flops 29360128 | bytes 29360128 | tf_op jit(solution)/shard_map/concatenate | solution.py:81
  78.5 216.1 %all-to-all-done.1 = bf16[16,1024,448]{1,2,0:T(8,128)(2,1)} async-done(((bf16[16,1024,448]{1,2,0:T(8,128)(2,1)}), bf16[16,1024,448]{1,2,0:T(8,128)(2,1)}, u32[]{:S(2)}, u32[]{:S(2)}) %all-to-all-start.1) | async-done | bytes 14680096 | tf_op jit(solution)/shard_map/all_to_all | solution.py:84
  294.6 10.3 %fusion.76 = (bf16[16,512,448]{1,2,0:T(8,128)(2,1)}, bf16[16,512,448]{1,2,0:T(8,128)(2,1)}) fusion(bf16[16,1024,448]{1,2,0:T(8,128)(2,1)} %all-to-all-done.1), kind=kLoop, calls=%fused_computation.170 | loop fusion | bytes 29360128 | tf_op jit(solution)/shard_map/split | solution.py:83
  324.0 19.9 %fusion = f32[24,512,512]{2,1,0:T(8,128)} fusion(bf16[24,512,448]{1,2,0:T(8,128)(2,1)} %gather_fusion.5, bf16[24,512,448]{1,2,0:T(8,128)(2,1)} %gather_fusion.4, pred[24]{0:T(512)(128)(4,1)S(1)} %get-tuple-element.25, pred[24]{0:T(512)(128)(4,1)S(1)} %get-tuple-element.9), kind=kOutput, calls=%fused_computation.15 | convolution fusion | flops 5648154624 | bytes 47185968 | tf_op jit(solution)/shard_map/qid,qjd->qij/dot_general | solution.py:124
  346.2 127.0 %reduce-scatter.2.cloned.1.call-done = f32[3,512,512]{2,1,0:T(8,128)} async-done(((f32[24,512,512]{2,1,0:T(8,128)}), f32[3,512,512]{2,1,0:T(8,128)}) %reduce-scatter.2.cloned.1.call-update) | async-done | bytes 3145744 | tf_op jit(solution)/shard_map/reduce_scatter | solution.py:123
  480.5 10.8 %all_to_all.171 = f32[4,32,1,512]{3,1,2,0:T(8,128)S(1)} all-to-all(f32[4,32,1,512]{3,1,2,0:T(8,128)S(1)} %bitcast.183), channel_id=1, replica_groups=mesh['aa_0'=4,'aa_1'=2,'ba_0'=4,'ba_1'=4] {'ba_1'}, dimensions={0} | all-to-all | bytes 524288 | tf_op jit(solution)/shard_map/all_to_all | solution.py:25
  491.3 13.3 %all_to_all.172 = f32[32,1,512]{2,1,0:T(1,128)S(1)} all-to-all(f32[32,1,512]{2,1,0:T(1,128)S(1)} %reduce_sum.191), channel_id=1, replica_groups=mesh['aa_0'=4,'aa_1'=2,'ba_0'=4,'ba_1'=4] {'aa_0','aa_1','ba_0'}, dimensions={0} | all-to-all | bytes 131072 | tf_op jit(solution)/shard_map/all_to_all | solution.py:32
  504.7 10.9 %all_to_all.173 = f32[32,1,512]{2,1,0:T(1,128)S(1)} all-to-all(f32[32,1,512]{2,1,0:T(1,128)S(1)} %broadcast_in_dim.78), channel_id=1, replica_groups=mesh['aa_0'=4,'aa_1'=2,'ba_0'=4,'ba_1'=4] {'aa_0','aa_1','ba_0'}, dimensions={0} | all-to-all | bytes 131072 | tf_op jit(solution)/shard_map/all_to_all | solution.py:42
  543.3 10.5 %all_to_all.175 = f32[32,1,512]{2,1,0:T(1,128)S(1)} all-to-all(f32[32,1,512]{2,1,0:T(1,128)S(1)} %reduce_sum.194), channel_id=1, replica_groups=mesh['aa_0'=4,'aa_1'=2,'ba_0'=4,'ba_1'=4] {'aa_0','aa_1','ba_0'}, dimensions={0} | all-to-all | bytes 131072 | tf_op jit(solution)/shard_map/all_to_all | solution.py:32
  553.9 10.9 %all_to_all.176 = f32[32,1,512]{2,1,0:T(1,128)S(1)} all-to-all(f32[32,1,512]{2,1,0:T(1,128)S(1)} %broadcast_in_dim.81), channel_id=1, replica_groups=mesh['aa_0'=4,'aa_1'=2,'ba_0'=4,'ba_1'=4] {'aa_0','aa_1','ba_0'}, dimensions={0} | all-to-all | bytes 131072 | tf_op jit(solution)/shard_map/all_to_all | solution.py:42
  564.9 9.6 %all_to_all.177 = f32[4,32,1,512]{3,1,2,0:T(8,128)S(1)} all-to-all(f32[4,32,1,512]{3,1,2,0:T(8,128)S(1)} %broadcast_in_dim.83), channel_id=1, replica_groups=mesh['aa_0'=4,'aa_1'=2,'ba_0'=4,'ba_1'=4] {'ba_1'}, dimensions={0} | all-to-all | bytes 524288 | tf_op jit(solution)/shard_map/all_to_all | solution.py:42
  591.5 10.5 %all_to_all.179 = f32[32,1,512]{2,1,0:T(1,128)S(1)} all-to-all(f32[32,1,512]{2,1,0:T(1,128)S(1)} %reduce_sum.197), channel_id=1, replica_groups=mesh['aa_0'=4,'aa_1'=2,'ba_0'=4,'ba_1'=4] {'aa_0','aa_1','ba_0'}, dimensions={0} | all-to-all | bytes 131072 | tf_op jit(solution)/shard_map/all_to_all | solution.py:32
  602.1 10.9 %all_to_all.180 = f32[32,1,512]{2,1,0:T(1,128)S(1)} all-to-all(f32[32,1,512]{2,1,0:T(1,128)S(1)} %broadcast_in_dim.84), channel_id=1, replica_groups=mesh['aa_0'=4,'aa_1'=2,'ba_0'=4,'ba_1'=4] {'aa_0','aa_1','ba_0'}, dimensions={0} | all-to-all | bytes 131072 | tf_op jit(solution)/shard_map/all_to_all | solution.py:42
  638.6 10.6 %all_to_all.183 = f32[32,1,512]{2,1,0:T(1,128)S(1)} all-to-all(f32[32,1,512]{2,1,0:T(1,128)S(1)} %reduce_sum.200), channel_id=1, replica_groups=mesh['aa_0'=4,'aa_1'=2,'ba_0'=4,'ba_1'=4] {'aa_0','aa_1','ba_0'}, dimensions={0} | all-to-all | bytes 131072 | tf_op jit(solution)/shard_map/all_to_all | solution.py:32
  649.3 10.9 %all_to_all.184 = f32[32,1,512]{2,1,0:T(1,128)S(1)} all-to-all(f32[32,1,512]{2,1,0:T(1,128)S(1)} %broadcast_in_dim.87), channel_id=1, replica_groups=mesh['aa_0'=4,'aa_1'=2,'ba_0'=4,'ba_1'=4] {'aa_0','aa_1','ba_0'}, dimensions={0} | all-to-all | bytes 131072 | tf_op jit(solution)/shard_map/all_to_all | solution.py:42
  686.8 10.5 %all_to_all.187 = f32[32,1,512]{2,1,0:T(1,128)S(1)} all-to-all(f32[32,1,512]{2,1,0:T(1,128)S(1)} %reduce_sum.203), channel_id=1, replica_groups=mesh['aa_0'=4,'aa_1'=2,'ba_0'=4,'ba_1'=4] {'aa_0','aa_1','ba_0'}, dimensions={0} | all-to-all | bytes 131072 | tf_op jit(solution)/shard_map/all_to_all | solution.py:32
  697.4 10.9 %all_to_all.188 = f32[32,1,512]{2,1,0:T(1,128)S(1)} all-to-all(f32[32,1,512]{2,1,0:T(1,128)S(1)} %broadcast_in_dim.90), channel_id=1, replica_groups=mesh['aa_0'=4,'aa_1'=2,'ba_0'=4,'ba_1'=4] {'aa_0','aa_1','ba_0'}, dimensions={0} | all-to-all | bytes 131072 | tf_op jit(solution)/shard_map/all_to_all | solution.py:42
  733.9 10.5 %all_to_all.191 = f32[32,1,512]{2,1,0:T(1,128)S(1)} all-to-all(f32[32,1,512]{2,1,0:T(1,128)S(1)} %reduce_sum.206), channel_id=1, replica_groups=mesh['aa_0'=4,'aa_1'=2,'ba_0'=4,'ba_1'=4] {'aa_0','aa_1','ba_0'}, dimensions={0} | all-to-all | bytes 131072 | tf_op jit(solution)/shard_map/all_to_all | solution.py:32
  744.5 10.9 %all_to_all.192 = f32[32,1,512]{2,1,0:T(1,128)S(1)} all-to-all(f32[32,1,512]{2,1,0:T(1,128)S(1)} %broadcast_in_dim.93), channel_id=1, replica_groups=mesh['aa_0'=4,'aa_1'=2,'ba_0'=4,'ba_1'=4] {'aa_0','aa_1','ba_0'}, dimensions={0} | all-to-all | bytes 131072 | tf_op jit(solution)/shard_map/all_to_all | solution.py:42
  755.5 9.8 %all_to_all.193 = f32[4,32,1,512]{3,1,2,0:T(8,128)S(1)} all-to-all(f32[4,32,1,512]{3,1,2,0:T(8,128)S(1)} %broadcast_in_dim.171), channel_id=1, replica_groups=mesh['aa_0'=4,'aa_1'=2,'ba_0'=4,'ba_1'=4] {'ba_1'}, dimensions={0} | all-to-all | bytes 524288 | tf_op jit(solution)/shard_map/all_to_all | solution.py:42
  782.3 10.5 %all_to_all.195 = f32[32,1,512]{2,1,0:T(1,128)S(1)} all-to-all(f32[32,1,512]{2,1,0:T(1,128)S(1)} %reduce_sum.209), channel_id=1, replica_groups=mesh['aa_0'=4,'aa_1'=2,'ba_0'=4,'ba_1'=4] {'aa_0','aa_1','ba_0'}, dimensions={0} | all-to-all | bytes 131072 | tf_op jit(solution)/shard_map/all_to_all | solution.py:32
  792.9 10.9 %all_to_all.196 = f32[32,1,512]{2,1,0:T(1,128)S(1)} all-to-all(f32[32,1,512]{2,1,0:T(1,128)S(1)} %broadcast_in_dim.172), channel_id=1, replica_groups=mesh['aa_0'=4,'aa_1'=2,'ba_0'=4,'ba_1'=4] {'aa_0','aa_1','ba_0'}, dimensions={0} | all-to-all | bytes 131072 | tf_op jit(solution)/shard_map/all_to_all | solution.py:42
  827.8 10.5 %all_to_all.199 = f32[32,1,512]{2,1,0:T(1,128)S(1)} all-to-all(f32[32,1,512]{2,1,0:T(1,128)S(1)} %reduce_sum.212), channel_id=1, replica_groups=mesh['aa_0'=4,'aa_1'=2,'ba_0'=4,'ba_1'=4] {'aa_0','aa_1','ba_0'}, dimensions={0} | all-to-all | bytes 131072 | tf_op jit(solution)/shard_map/all_to_all | solution.py:32
  838.4 10.9 %all_to_all.200 = f32[32,1,512]{2,1,0:T(1,128)S(1)} all-to-all(f32[32,1,512]{2,1,0:T(1,128)S(1)} %broadcast_in_dim.175), channel_id=1, replica_groups=mesh['aa_0'=4,'aa_1'=2,'ba_0'=4,'ba_1'=4] {'aa_0','aa_1','ba_0'}, dimensions={0} | all-to-all | bytes 131072 | tf_op jit(solution)/shard_map/all_to_all | solution.py:42
  (189 shorter events, 266.4 us)
Async XLA Ops:
  7.2 10.0 %copy-start.3 = (s32[16,16]{1,0:T(8,128)S(1)}, s32[16,16]{1,0:T(8,128)}, u32[]{:S(2)}) copy-start(s32[16,16]{1,0:T(8,128)} %param.14) | copy-start | bytes 3076
  7.2 10.0 %copy-start.4 = (s32[16,16]{1,0:T(8,128)S(1)}, s32[16,16]{1,0:T(8,128)}, u32[]{:S(2)}) copy-start(s32[16,16]{1,0:T(8,128)} %param.13) | copy-start | bytes 3076
  12.7 11.9 %all-to-all-start = ((f32[8,1,8192]{2,1,0:T(1,128)}), f32[8,1,8192]{2,1,0:T(1,128)S(1)}, u32[]{:S(2)}, u32[]{:S(2)}) async-start(f32[8,1,8192]{2,1,0:T(1,128)} %broadcast_in_dim.77), calls=%async_computation | async-start | bytes 524288 | tf_op jit(solution)/shard_map/all_to_all | solution.py:42
  27.8 3.4 copy-start.2
  53.2 7.0 copy-start.1
  69.9 8.5 copy-start.5
  69.9 224.7 %all-to-all-start.1 = ((bf16[16,1024,448]{1,2,0:T(8,128)(2,1)}), bf16[16,1024,448]{1,2,0:T(8,128)(2,1)}, u32[]{:S(2)}, u32[]{:S(2)}) async-start(bf16[16,1024,448]{1,2,0:T(8,128)(2,1)} %pad_maximum_fusion), calls=%async_computation.1 | async-start | bytes 29360128 | tf_op jit(solution)/shard_map/all_to_all | solution.py:84
  78.2 395.0 %reduce-scatter.2.cloned.1.call-start = ((), (), s32[]{:S(2)}) async-start(), calls=%async_computation.35 | async-start | bytes 28311552 | tf_op jit(solution)/shard_map/reduce_scatter | solution.py:123
  473.2 56.8 %copy-start = (f32[3,512,512]{2,1,0:T(8,128)S(1)}, f32[3,512,512]{2,1,0:T(8,128)}, u32[]{:S(2)}) copy-start(f32[3,512,512]{2,1,0:T(8,128)} %reduce-scatter.2.cloned.1.call-done) | copy-start | bytes 9437188
  516.4 11.0 %all-to-all-start.5 = ((f32[4,32,1,512]{3,1,2,0:T(8,128)}), f32[4,32,1,512]{3,1,2,0:T(8,128)S(1)}, u32[]{:S(2)}, u32[]{:S(2)}) async-start(f32[4,32,1,512]{3,1,2,0:T(8,128)} %broadcast_in_dim.80), calls=%async_computation.6 | async-start | bytes 524288 | tf_op jit(solution)/shard_map/all_to_all | solution.py:42
  850.0 10.6 %all-to-all-start.33 = ((f32[4,32,1,512]{3,1,2,0:T(8,128)}), f32[4,32,1,512]{3,1,2,0:T(8,128)S(1)}, u32[]{:S(2)}, u32[]{:S(2)}) async-start(f32[4,32,1,512]{3,1,2,0:T(8,128)} %broadcast_in_dim.177), calls=%async_computation.34 | async-start | bytes 524288 | tf_op jit(solution)/shard_map/all_to_all | solution.py:42
Sparse Core Ops, SparseCore 0:
  344.0 129.1 reduce-scatter.1
where the time goes:
time: 877 us; the launch traced here: 869 us
  waiting for transfers between devices  364 us (42%)
  blocking collectives  306 us (35%)
  local copies, waits for them, and re-layouts  84.5 us (10%)
  matrix products  45.2 us (5%)
  other arithmetic  34.1 us (4%)
  starting transfers between devices  20.1 us (2%)
  between operations  14.9 us (2%)
    all_to_all x1, waiting for transfers between devices, in_one_piece(): lax.all_to_all(both, axis, split_axis=split_dim, concat_axis=concat_dim,...  216 us
    all_to_all x14, blocking collectives, from_everyone(): lax.all_to_all(jnp.broadcast_to(x[None], (size, *x.shape)), axis, 0, 0, t...  145 us
    reduce_scatter x1, waiting for transfers between devices, per_device(): lax.psum_scatter(jnp.einsum('qid,qjd->qij', left, right, preferred_elemen...  127 us
    all_to_all x8, blocking collectives, summed_rows(): return jnp.sum(lax.all_to_all(own, far, 0, 0, tiled=True), axis=0)  86.8 us
    all_to_all x8, blocking collectives, summed_on_arrival(): lax.all_to_all(parts, axis, split_axis=0, concat_axis=0, tiled=True)  74.2 us
    all_to_all x3, waiting for transfers between devices, from_everyone(): lax.all_to_all(jnp.broadcast_to(x[None], (size, *x.shape)), axis, 0, 0, t...  20.4 us
    dot_general x1, matrix products, per_device(): jnp.einsum('qid,qjd->qij', left, right, preferred_element_type=jnp.float32)  19.9 us
  transfers between devices with their start and end apart: 5, of which 5 were waited for; matrix products, arithmetic and copies ran while one was open for 0% of the time, Pallas kernels for 0%

commit v1 on v0

v1 whole, which is shorter than its diff:
```python
import functools

import jax
import jax.numpy as jnp
from jax import lax
from jax.experimental import pallas as pl
from jax.experimental.pallas import tpu as pltpu
from jax.sharding import Mesh
from jax.sharding import PartitionSpec as P

BS = 512
SWEEPS = 4
BA = ("ba_0", "ba_1")
AA = ("aa_0", "aa_1")
ALL = AA + BA
LANES = 128
TILES = BS // LANES
HALF = BS // 2
FIXED = 32000.0
IDS = 16

smoothing_regularizer = 0.02
norm_floor = 1e-06

f32, bf16, i16, i32 = jnp.float32, jnp.bfloat16, jnp.int16, jnp.int32


def call(kernel, out_shape, grid_spec, flops, bytes_accessed, args):
    return pl.pallas_call(
        kernel,
        out_shape=out_shape,
        grid_spec=grid_spec,
        compiler_params=pltpu.CompilerParams(vmem_limit_bytes=24 * 2**20),
        cost_estimate=pl.CostEstimate(
            flops=flops, bytes_accessed=bytes_accessed, transcendentals=0
        ),
    )(*args)


def pack_first_kernel(one_ref, two_ref, a_ref, b_ref, inv_a_ref, inv_b_ref, out_ref):
    out_ref[0, :, :BS] = (b_ref[...].astype(f32) * inv_b_ref[...]).astype(bf16)
    out_ref[0, :, BS:] = (a_ref[...].astype(f32) * inv_a_ref[...]).astype(bf16)


def pack_second_kernel(one_ref, a_ref, inv_a_ref, ids_ref, out_ref):
    width = a_ref.shape[0]
    out_ref[0, :width, :] = (a_ref[...].astype(f32) * inv_a_ref[...]).astype(bf16)
    out_ref[0, width:, :] = ids_ref[...]


def pack_first(one, two, a, b, inv_a, inv_b):
    width, owners = a.shape[0], one.shape[0]
    spec = pltpu.PrefetchScalarGridSpec(
        num_scalar_prefetch=2,
        grid=(owners,),
        in_specs=[
            pl.BlockSpec((width, HALF), lambda o, r1, r2: (0, 2 * r1[o])),
            pl.BlockSpec((width, BS), lambda o, r1, r2: (0, r2[o])),
            pl.BlockSpec((1, HALF), lambda o, r1, r2: (0, 2 * r1[o])),
            pl.BlockSpec((1, BS), lambda o, r1, r2: (0, r2[o])),
        ],
        out_specs=pl.BlockSpec((1, width, BS + HALF), lambda o, r1, r2: (o, 0, 0)),
    )
    shape = jax.ShapeDtypeStruct((owners, width, BS + HALF), bf16)
    size = owners * width * (BS + HALF)
    return call(
        pack_first_kernel, shape, spec, 2 * size, 4 * size, (one, two, a, b, inv_a, inv_b)
    )


def pack_second(one, a, inv_a, ids):
    width, owners = a.shape[0], one.shape[0]
    spec = pltpu.PrefetchScalarGridSpec(
        num_scalar_prefetch=1,
        grid=(owners,),
        in_specs=[
            pl.BlockSpec((width, HALF), lambda o, r1: (0, 2 * r1[o] + 1)),
            pl.BlockSpec((1, HALF), lambda o, r1: (0, 2 * r1[o] + 1)),
            pl.BlockSpec((IDS, HALF), lambda o, r1: (0, 0)),
        ],
        out_specs=pl.BlockSpec((1, width + IDS, HALF), lambda o, r1: (o, 0, 0)),
    )
    shape = jax.ShapeDtypeStruct((owners, width + IDS, HALF), bf16)
    size = owners * width * HALF
    return call(pack_second_kernel, shape, spec, 2 * size, 4 * size, (one, a, inv_a, ids))


def cosine_kernel(s_ref, r_ref, a_ref, b_ref, out_ref):
    partial = lax.dot_general(
        a_ref[0], b_ref[0], (((0,), (0,)), ((), ())), preferred_element_type=f32
    )
    out_ref[0] = jnp.floor(partial * FIXED + 0.5).astype(i32).astype(i16)


def cosines(slots, a, a_at, b, width):
    pairs = slots.shape[0]
    spec = pltpu.PrefetchScalarGridSpec(
        num_scalar_prefetch=2,
        grid=(pairs,),
        in_specs=[
            pl.BlockSpec((1, width, HALF), lambda q, s, r: (s[q], 0, a_at)),
            pl.BlockSpec((1, width, BS), lambda q, s, r: (r[q], 0, 0)),
        ],
        out_specs=pl.BlockSpec((1, HALF, BS), lambda q, s, r: (q, 0, 0)),
    )
    shape = jax.ShapeDtypeStruct((pairs, HALF, BS), i16)
    flops = 2 * pairs * HALF * BS * width
    moved = pairs * (width * (HALF + BS) + HALF * BS) * 2
    return call(cosine_kernel, shape, spec, flops, moved, (slots[:, 0], slots[:, 1], a, b))


def both_cores_kernel(x_ref, *refs):
    ins, outs = refs[:8], refs[8:]
    for d in range(4):
        total = ins[d][...].astype(i32) + ins[4 + d][...].astype(i32)
        outs[d][...] = total.astype(i16)


def both_cores(chip, own, other):
    each = own.shape[0] // 4
    block = (1, HALF, BS)

    def at(d):
        return pl.BlockSpec(block, lambda k, x: (lax.rem(x[0] + d, 4) * each + k, 0, 0))

    spec = pltpu.PrefetchScalarGridSpec(
        num_scalar_prefetch=1,
        grid=(each,),
        in_specs=[at(d) for d in range(4)] * 2,
        out_specs=[pl.BlockSpec(block, lambda k, x: (k, 0, 0))] * 4,
    )
    shape = [jax.ShapeDtypeStruct((each, HALF, BS), i16)] * 4
    size = own.size
    return call(
        both_cores_kernel, shape, spec, size, 6 * size, (chip, *([own] * 4), *([other] * 4))
    )


def affinity_kernel(a_ref, b_ref, c_ref, d_ref, out_ref, turned_ref):
    total = a_ref[0].astype(i32) + b_ref[0].astype(i32)
    total = total + c_ref[0].astype(i32) + d_ref[0].astype(i32)
    value = jnp.exp(total.astype(f32) * (1.0 / (FIXED * smoothing_regularizer)))
    out_ref[0] = value
    turned_ref[0] = value.T


def affinity(parts):
    each = parts[0].shape[0]
    spec = pl.GridSpec(
        grid=(each,),
        in_specs=[pl.BlockSpec((1, HALF, BS), lambda k: (k, 0, 0))] * 4,
        out_specs=[
            pl.BlockSpec((1, HALF, BS), lambda k: (k, 0, 0)),
            pl.BlockSpec((1, BS, HALF), lambda k: (k, 0, 0)),
        ],
    )
    shape = [
        jax.ShapeDtypeStruct((each, HALF, BS), f32),
        jax.ShapeDtypeStruct((each, BS, HALF), f32),
    ]
    size = each * HALF * BS
    return call(affinity_kernel, shape, spec, 8 * size, 16 * size, tuple(parts))


def emit_rows(rows, fine, out_ref, scratch):
    pad = scratch.shape[0] - len(rows)
    tile = jnp.concatenate(rows + [jnp.zeros((pad, LANES), f32)], axis=0)
    high = tile.astype(bf16)
    if fine:
        low = (tile - high.astype(f32)).astype(bf16)
        high = jnp.concatenate([high, low], axis=0)
    out_ref[...] = jnp.broadcast_to(high[None], out_ref.shape)


def times_rows(mats, scale):
    turned = None if scale is None else scale.T
    rows = []
    for k in range(mats[0].shape[0]):
        if len(mats) == 2 and mats[0].shape[1] == HALF:
            total = None
            for j in range(TILES):
                part = mats[j // 2][k, (j % 2) * LANES : (j % 2 + 1) * LANES, :]
                if turned is not None:
                    part = part * turned[:, TILES * k + j : TILES * k + j + 1]
                part = jnp.sum(part, axis=0, keepdims=True)
                total = part if total is None else total + part
            rows += [total[:, j * LANES : (j + 1) * LANES] for j in range(TILES)]
        else:
            for m in mats:
                total = None
                for j in range(TILES):
                    part = m[k, j * LANES : (j + 1) * LANES, :]
                    if turned is not None:
                        part = part * turned[:, TILES * k + j : TILES * k + j + 1]
                    part = jnp.sum(part, axis=0, keepdims=True)
                    total = part if total is None else total + part
                rows += [total[:, j * LANES : (j + 1) * LANES] for j in range(TILES // 2)]
    return rows


def start_kernel(first_ref, second_ref, out_ref, scratch):
    emit_rows(times_rows((first_ref, second_ref), None), False, out_ref, scratch)


def totals_of(hot, got_ref):
    got = got_ref[...].reshape(-1, LANES)
    return jnp.dot(hot, got, preferred_element_type=f32)


def step_kernel(fine, got_ref, hot_ref, first_ref, second_ref, out_ref, scratch):
    scale = 1.0 / (1.0 + totals_of(hot_ref[...], got_ref))
    padded = jnp.concatenate([scale, jnp.zeros((LANES - scale.shape[0], LANES), f32)], axis=0)
    emit_rows(times_rows((first_ref, second_ref), padded), fine, out_ref, scratch)


def log_kernel(got_ref, hot_ref, log_ref):
    log_ref[...] = jnp.log(1.0 / (1.0 + totals_of(hot_ref[...], got_ref)))


def on_chip(kernel, out_shape, flops, args, scratch=()):
    return pl.pallas_call(
        kernel,
        out_shape=out_shape,
        in_specs=[pl.BlockSpec(memory_space=pltpu.VMEM)] * len(args),
        out_specs=pl.BlockSpec(memory_space=pltpu.VMEM),
        scratch_shapes=list(scratch),
        compiler_params=pltpu.CompilerParams(vmem_limit_bytes=24 * 2**20),
        cost_estimate=pl.CostEstimate(flops=flops, bytes_accessed=flops, transcendentals=0),
    )(*args)


ROWS = 16


def step(got, hot, mats, fine, devices):
    out = jax.ShapeDtypeStruct((devices, 2 * ROWS if fine else ROWS, LANES), bf16)
    scratch = [pltpu.VMEM((ROWS, LANES), f32)]
    flops = 4 * mats[0].size
    if got is None:
        return on_chip(start_kernel, out, flops, tuple(mats), scratch)
    return on_chip(
        functools.partial(step_kernel, fine), out, flops, (got, hot, *mats), scratch
    )


def exchanged(x):
    return lax.all_to_all(x, ALL, 0, 0, tiled=True)


def hot_rows(wanted, present, fine):
    devices, pairs = present.shape
    col = jnp.full((devices, ROWS // TILES), -1, i32).at[:, :pairs].set(present)
    col_id = jnp.broadcast_to(col[:, :, None], (devices, ROWS // TILES, TILES))
    col_tile = jnp.broadcast_to(jnp.arange(TILES)[None, None, :], col_id.shape)
    if fine:
        col_id = jnp.concatenate([col_id, col_id], axis=1)
        col_tile = jnp.concatenate([col_tile, col_tile], axis=1)
    row_id = jnp.repeat(wanted, TILES)
    row_tile = jnp.tile(jnp.arange(TILES), wanted.shape[0])
    same = (row_id[:, None] == col_id.reshape(-1)[None, :]) & (
        row_tile[:, None] == col_tile.reshape(-1)[None, :]
    )
    return same.astype(bf16)


def per_device(initial_dictionary_matrix, decoder_two, route_one, route_two, candidate_pair_slots):
    column = lax.axis_index(BA)
    chip = lax.axis_index("aa_0")
    core = lax.axis_index("aa_1")
    owners = lax.axis_size(BA)
    depth = lax.axis_size(AA)
    devices = owners * depth
    blocks_dev = initial_dictionary_matrix.shape[0] // BS
    width = initial_dictionary_matrix.shape[1]

    one_t, two_t = initial_dictionary_matrix.T, decoder_two.T
    sums = jnp.concatenate(
        [jnp.sum(jnp.square(t.astype(f32)), axis=0) for t in (one_t, two_t)]
    )
    sums = sums.reshape(8, -1)
    sums = lax.all_to_all(
        jnp.broadcast_to(sums[None], (depth, *sums.shape)), AA, 0, 0, tiled=True
    ).sum(axis=0)
    inverse = lax.rsqrt(sums + norm_floor).reshape(2, 1, -1)

    my_one = lax.dynamic_index_in_dim(route_one, column, 0, False)
    my_two = lax.dynamic_index_in_dim(route_two, column, 0, False)
    slots = candidate_pair_slots[0]
    pairs = slots.shape[0]
    ids = jnp.zeros((IDS, HALF), bf16).at[:2, :pairs].set(slots.T.astype(bf16))
    first = pack_first(my_one, my_two, one_t, two_t, inverse[0], inverse[1])
    second = pack_second(my_one, one_t, inverse[0], ids)
    first = lax.all_to_all(first, BA, 0, 0, tiled=True)

    mine = pairs // 2
    own_slots = lax.dynamic_slice_in_dim(slots, core * mine, mine, 0)
    other_slots = lax.dynamic_slice_in_dim(slots, (1 - core) * mine, mine, 0)
    swap = [(0, 1), (1, 0)]
    chip_list = chip.reshape(1).astype(i32)

    def summed(a, a_at):
        other = cosines(other_slots, a, a_at, first, width)
        other = lax.ppermute(other, "aa_1", swap)
        own = cosines(own_slots, a, a_at, first, width)
        parts = both_cores(chip_list, own, other)
        return [parts[0]] + [
            lax.ppermute(parts[d], "aa_0", [(x, (x + d) % 4) for x in range(4)])
            for d in range(1, 4)
        ]

    upper = summed(first, 2)
    second = lax.all_to_all(second, BA, 0, 0, tiled=True)
    lower = summed(second, 0)
    k_upper, t_upper = affinity(upper)
    k_lower, t_lower = affinity(lower)

    every = second[:, width : width + 2, :pairs].astype(i32)
    owner_ids = jnp.arange(owners)[:, None]
    s_all, r_all = every[:, 0], every[:, 1]
    row_all = s_all * blocks_dev + route_one[s_all, owner_ids]
    col_all = r_all * blocks_dev + route_two[r_all, owner_ids]
    each = pairs // depth

    def by_device(x):
        x = x.reshape(owners, 2, 4, each)
        return x.transpose(2, 1, 0, 3).reshape(devices, each)

    row_dev, col_dev = by_device(row_all), by_device(col_all)
    me = (chip * 2 + core) * owners + column
    my_rows = lax.dynamic_index_in_dim(row_dev, me, 0, False)
    my_cols = lax.dynamic_index_in_dim(col_dev, me, 0, False)
    pad = jnp.full((ROWS // TILES - each,), -2, i32)
    my_rows = jnp.concatenate([my_rows, pad])
    my_cols = jnp.concatenate([my_cols, pad])
    own_blocks = column * blocks_dev + jnp.arange(blocks_dev)
    row_hot = hot_rows(my_rows, row_dev, False)
    col_hot = hot_rows(my_cols, col_dev, False)
    row_hot_fine = hot_rows(my_rows, row_dev, True)
    row_hot_own = hot_rows(own_blocks, row_dev, True)
    col_hot_own = hot_rows(own_blocks, col_dev, True)

    by_row, by_col = (t_upper, t_lower), (k_upper, k_lower)
    got = exchanged(step(None, None, by_row, False, devices))
    for sweep in range(SWEEPS - 1):
        got = exchanged(step(got, row_hot, by_col, False, devices))
        got = exchanged(step(got, col_hot, by_row, sweep == SWEEPS - 2, devices))
    logs = jax.ShapeDtypeStruct((blocks_dev * TILES, LANES), f32)
    last = exchanged(step(got, row_hot_fine, by_col, True, devices))
    row_log = on_chip(log_kernel, logs, 2**20, (got, row_hot_own))
    col_log = on_chip(log_kernel, logs, 2**20, (last, col_hot_own))
    return row_log.reshape(-1), col_log.reshape(-1)


def solution(mesh):
    torus = Mesh(mesh.devices.reshape(4, 2, 4, 4), ("aa_0", "aa_1", "ba_0", "ba_1"))
    in_specs = (P(BA, AA), P(BA, AA), P(), P(), P(BA, None, None))
    out_specs = (P(BA), P(BA))
    return jax.shard_map(
        per_device, mesh=torus, in_specs=in_specs, out_specs=out_specs, check_vma=False
    )
```

time: 877 us -> 552 us (0.63)
  blocking collectives: 306 us -> 89.2 us
  Pallas kernels: 0 us -> 71.5 us
  waiting for transfers between devices: 364 us -> 299 us
  local copies, waits for them, and re-layouts: 84.5 us -> 36.6 us
  matrix products: 45.2 us -> 0 us
  other arithmetic: 34.1 us -> 7.07 us
  starting transfers between devices: 20.1 us -> 45.1 us
  between operations: 14.9 us -> 1.21 us
    all_to_all x30 -> x5, blocking collectives: 306 us -> 89.2 us  [exchanged(): return lax.all_to_all(x, ALL, 0, 0, tiled=True)]
    reduce_scatter x1 -> x0, waiting for transfers between devices: 127 us -> none  [per_device(): lax.psum_scatter(jnp.einsum('qid,qjd->qij', left, right, preferred_elemen...]
    pallas_call x0 -> x20, Pallas kernels: none -> 71.5 us  [the longest x10 60.2 us: call(): pl.pallas_call(kernel, out_shape=out_shape, grid_spec=grid_spec, compiler...]
    ppermute x0 -> x8, waiting for transfers between devices: none -> 52.5 us  [the longest x6 52.5 us: summed(): lax.ppermute(parts[d], 'aa_0', [(x, (x + d) % 4) for x in range(4)])]
    dot_general x17 -> x0, matrix products: 45.2 us -> none  [the longest x1 19.9 us: per_device(): jnp.einsum('qid,qjd->qij', left, right, preferred_element_type=jnp.float32)]
    gather x14 -> x6, local copies, waits for them, and re-layouts: 43.6 us -> 6.52 us  [the longest x3 3.26 us: per_device(): col_all = r_all * blocks_dev + route_two[r_all, owner_ids]]
    unnamed x24 -> x49, local copies, waits for them, and re-layouts: 3.17 us -> 21.2 us
    all_to_all x4 -> x6, starting transfers between devices: 19.8 us -> 36.2 us  [the longest x3 17.7 us: exchanged(): return lax.all_to_all(x, ALL, 0, 0, tiled=True)]
  transfers between devices with their start and end apart: 5 -> 14, of which waited for: 5 -> 10; matrix products, arithmetic and copies ran while one was open for 0% -> 3% of each run, Pallas kernels for 0% -> 10%
where the time goes in v1:
time: 552 us; the launch traced here: 550 us
  waiting for transfers between devices  299 us (54%)
  blocking collectives  89.2 us (16%)
  Pallas kernels  71.5 us (13%)
  starting transfers between devices  45.1 us (8%)
  local copies, waits for them, and re-layouts  36.6 us (7%)
  other arithmetic  7.07 us (1%)
    all_to_all x1, waiting for transfers between devices, per_device(): first = lax.all_to_all(first, BA, 0, 0, tiled=True)  156 us
    all_to_all x5, blocking collectives, exchanged(): return lax.all_to_all(x, ALL, 0, 0, tiled=True)  89.2 us
    pallas_call x10, Pallas kernels, call(): pl.pallas_call(kernel, out_shape=out_shape, grid_spec=grid_spec, compiler...  60.2 us
    ppermute x6, waiting for transfers between devices, summed(): lax.ppermute(parts[d], 'aa_0', [(x, (x + d) % 4) for x in range(4)])  52.5 us
    all_to_all x1, waiting for transfers between devices, per_device(): second = lax.all_to_all(second, BA, 0, 0, tiled=True)  41.8 us
    all_to_all x3, waiting for transfers between devices, exchanged(): return lax.all_to_all(x, ALL, 0, 0, tiled=True)  41.4 us
    unnamed x49, local copies, waits for them, and re-layouts  21.2 us
    all_to_all x3, starting transfers between devices, exchanged(): return lax.all_to_all(x, ALL, 0, 0, tiled=True)  17.7 us
  transfers between devices with their start and end apart: 14, of which 10 were waited for; matrix products, arithmetic and copies ran while one was open for 3% of the time, Pallas kernels for 10%

profile of v1, /device:TPU:0, one launch (start us, length us, event | category | flops | bytes accessed | tf_op | source)
XLA Modules:
  0.0 549.6 jit_solution(7030127094776656774)
XLA Ops:
  11.5 7.5 %all-to-all-done = f32[8,8,1024]{2,1,0:T(8,128)S(1)} async-done(((f32[8,8,1024]{2,1,0:T(8,128)}), f32[8,8,1024]{2,1,0:T(8,128)S(1)}, u32[]{:S(2)}, u32[]{:S(2)}) %all-to-all-start) | async-done | bytes 262176 | tf_op jit(solution)/shard_map/all_to_all | solution.py:281
  30.9 8.1 %all-to-all-start.1 = ((bf16[16,448,768]{2,1,0:T(8,128)(2,1)}), bf16[16,448,768]{2,1,0:T(8,128)(2,1)}, u32[]{:S(2)}, u32[]{:S(2)}) async-start(bf16[16,448,768]{2,1,0:T(8,128)(2,1)} %copy-done.2), calls=%async_computation.1 | async-start | bytes 22020096 | tf_op jit(solution)/shard_map/all_to_all | solution.py:293
  45.0 155.7 %all-to-all-done.1.a_ref.b_ref = bf16[16,448,768]{2,1,0:T(8,128)(2,1)} async-done(((bf16[16,448,768]{2,1,0:T(8,128)(2,1)}), bf16[16,448,768]{2,1,0:T(8,128)(2,1)}, u32[]{:S(2)}, u32[]{:S(2)}) %all-to-all-start.1) | async-done | bytes 11010080 | tf_op jit(solution)/shard_map/all_to_all | solution.py:293
  200.7 6.0 %all-to-all-start.2 = ((bf16[16,464,256]{2,1,0:T(8,128)(2,1)}), bf16[16,464,256]{2,1,0:T(8,128)(2,1)}, u32[]{:S(2)}, u32[]{:S(2)}) async-start(bf16[16,464,256]{2,1,0:T(8,128)(2,1)} %copy-done.9), calls=%async_computation.2 | async-start | bytes 7602176 | tf_op jit(solution)/shard_map/all_to_all | solution.py:312
  206.8 11.4 %shard_map.70 = s16[12,256,512]{2,1,0:T(8,128)(2,1)} custom-call(s32[12]{0:T(128)S(1)} %get-tuple-element.95.s_ref, s32[12]{0:T(128)S(1)} %get-tuple-element.94.r_ref, bf16[16,448,768]{2,1,0:T(8,128)(2,1)} %all-to-all-done.1.a_ref.b_ref, bf16[16,448,768]{2,1,0:T(8,128)(2,1)} %all-to-all-done.1.a_ref.b_ref), custom_call_target="tpu_custom_call" | custom-call | flops 1409286144 | bytes 11403264 | tf_op jit(solution)/shard_map/pallas_call | solution.py:29
  218.2 41.8 %all-to-all-done.2.a_ref = bf16[16,464,256]{2,1,0:T(8,128)(2,1)} async-done(((bf16[16,464,256]{2,1,0:T(8,128)(2,1)}), bf16[16,464,256]{2,1,0:T(8,128)(2,1)}, u32[]{:S(2)}, u32[]{:S(2)}) %all-to-all-start.2) | async-done | bytes 3801120 | tf_op jit(solution)/shard_map/all_to_all | solution.py:312
  259.9 11.4 %shard_map.75 = s16[12,256,512]{2,1,0:T(8,128)(2,1)} custom-call(s32[12]{0:T(128)S(1)} %get-tuple-element.95.s_ref, s32[12]{0:T(128)S(1)} %get-tuple-element.94.r_ref, bf16[16,464,256]{2,1,0:T(8,128)(2,1)} %all-to-all-done.2.a_ref, bf16[16,448,768]{2,1,0:T(8,128)(2,1)} %all-to-all-done.1.a_ref.b_ref), custom_call_target="tpu_custom_call" | custom-call | flops 1409286144 | bytes 11403264 | tf_op jit(solution)/shard_map/pallas_call | solution.py:29
  272.5 10.1 %shard_map.69.refs_0_.refs_1_.refs_2_.refs_3_ = s16[12,256,512]{2,1,0:T(8,128)(2,1)S(1)} custom-call(s32[12]{0:T(128)S(1)} %get-tuple-element.102.s_ref, s32[12]{0:T(128)S(1)} %get-tuple-element.103.r_ref, bf16[16,448,768]{2,1,0:T(8,128)(2,1)} %all-to-all-done.1.a_ref.b_ref, bf16[16,448,768]{2,1,0:T(8,128)(2,1)} %all-to-all-done.1.a_ref.b_ref), custom_call_target="tpu_custom_call" | custom-call | flops 1409286144 | bytes 11403264 | tf_op jit(solution)/shard_map/pallas_call | solution.py:29
  291.7 10.1 %shard_map.74.refs_0_.refs_1_.refs_2_.refs_3_ = s16[12,256,512]{2,1,0:T(8,128)(2,1)S(1)} custom-call(s32[12]{0:T(128)S(1)} %get-tuple-element.102.s_ref, s32[12]{0:T(128)S(1)} %get-tuple-element.103.r_ref, bf16[16,464,256]{2,1,0:T(8,128)(2,1)} %all-to-all-done.2.a_ref, bf16[16,448,768]{2,1,0:T(8,128)(2,1)} %all-to-all-done.1.a_ref.b_ref), custom_call_target="tpu_custom_call" | custom-call | flops 1409286144 | bytes 11403264 | tf_op jit(solution)/shard_map/pallas_call | solution.py:29
  317.7 8.5 %collective-permute-done.2.c_ref = s16[3,256,512]{2,1,0:T(8,128)(2,1)} collective-permute-done((s16[3,256,512]{2,1,0:T(8,128)(2,1)}, s16[3,256,512]{2,1,0:T(8,128)(2,1)}, u32[]{:S(2)}, u32[]{:S(2)}) %collective-permute-start.2) | collective-permute-done | bytes 786464 | tf_op jit(solution)/shard_map/ppermute | solution.py:307
  326.2 14.8 %collective-permute-done.3.d_ref = s16[3,256,512]{2,1,0:T(8,128)(2,1)} collective-permute-done((s16[3,256,512]{2,1,0:T(8,128)(2,1)}, s16[3,256,512]{2,1,0:T(8,128)(2,1)}, u32[]{:S(2)}, u32[]{:S(2)}) %collective-permute-start.3) | collective-permute-done | bytes 786464 | tf_op jit(solution)/shard_map/ppermute | solution.py:307
  344.7 15.0 %collective-permute-done.6.c_ref = s16[3,256,512]{2,1,0:T(8,128)(2,1)} collective-permute-done((s16[3,256,512]{2,1,0:T(8,128)(2,1)}, s16[3,256,512]{2,1,0:T(8,128)(2,1)}, u32[]{:S(2)}, u32[]{:S(2)}) %collective-permute-start.6) | collective-permute-done | bytes 786464 | tf_op jit(solution)/shard_map/ppermute | solution.py:307
  359.7 14.3 %collective-permute-done.7.d_ref = s16[3,256,512]{2,1,0:T(8,128)(2,1)} collective-permute-done((s16[3,256,512]{2,1,0:T(8,128)(2,1)}, s16[3,256,512]{2,1,0:T(8,128)(2,1)}, u32[]{:S(2)}, u32[]{:S(2)}) %collective-permute-start.7) | collective-permute-done | bytes 786464 | tf_op jit(solution)/shard_map/ppermute | solution.py:307
  381.0 7.4 %all-to-all-start.3 = ((bf16[128,16,128]{2,1,0:T(8,128)(2,1)}), bf16[128,16,128]{2,1,0:T(8,128)(2,1)}, u32[]{:S(2)}, u32[]{:S(2)}) async-start(bf16[128,16,128]{2,1,0:T(8,128)(2,1)} %copy-done.13), calls=%async_computation.3 | async-start | bytes 1048576 | tf_op jit(solution)/shard_map/all_to_all | solution.py:247
  389.5 11.9 %all-to-all-done.3.got_ref = bf16[128,16,128]{2,1,0:T(8,128)(2,1)} async-done(((bf16[128,16,128]{2,1,0:T(8,128)(2,1)}), bf16[128,16,128]{2,1,0:T(8,128)(2,1)}, u32[]{:S(2)}, u32[]{:S(2)}) %all-to-all-start.3) | async-done | bytes 524320 | tf_op jit(solution)/shard_map/all_to_all | solution.py:247
  403.4 17.8 %all_to_all.55.got_ref = bf16[128,16,128]{2,1,0:T(8,128)(2,1)S(1)} all-to-all(bf16[128,16,128]{2,1,0:T(8,128)(2,1)S(1)} %shard_map.79), channel_id=1, replica_groups=mesh['aa_0'=4,'aa_1'=2,'ba_0'=4,'ba_1'=4] {'aa_0','aa_1','ba_0','ba_1'}, dimensions={0} | all-to-all | bytes 1048576 | tf_op jit(solution)/shard_map/all_to_all | solution.py:247
  422.0 17.8 %all_to_all.56.got_ref = bf16[128,16,128]{2,1,0:T(8,128)(2,1)S(1)} all-to-all(bf16[128,16,128]{2,1,0:T(8,128)(2,1)S(1)} %shard_map.80), channel_id=1, replica_groups=mesh['aa_0'=4,'aa_1'=2,'ba_0'=4,'ba_1'=4] {'aa_0','aa_1','ba_0','ba_1'}, dimensions={0} | all-to-all | bytes 1048576 | tf_op jit(solution)/shard_map/all_to_all | solution.py:247
  440.6 17.8 %all_to_all.57.got_ref = bf16[128,16,128]{2,1,0:T(8,128)(2,1)S(1)} all-to-all(bf16[128,16,128]{2,1,0:T(8,128)(2,1)S(1)} %shard_map.81), channel_id=1, replica_groups=mesh['aa_0'=4,'aa_1'=2,'ba_0'=4,'ba_1'=4] {'aa_0','aa_1','ba_0','ba_1'}, dimensions={0} | all-to-all | bytes 1048576 | tf_op jit(solution)/shard_map/all_to_all | solution.py:247
  459.3 17.8 %all_to_all.58.got_ref = bf16[128,16,128]{2,1,0:T(8,128)(2,1)S(1)} all-to-all(bf16[128,16,128]{2,1,0:T(8,128)(2,1)S(1)} %shard_map.82), channel_id=1, replica_groups=mesh['aa_0'=4,'aa_1'=2,'ba_0'=4,'ba_1'=4] {'aa_0','aa_1','ba_0','ba_1'}, dimensions={0} | all-to-all | bytes 1048576 | tf_op jit(solution)/shard_map/all_to_all | solution.py:247
  477.9 17.8 %all_to_all.59.got_ref = bf16[128,16,128]{2,1,0:T(8,128)(2,1)S(1)} all-to-all(bf16[128,16,128]{2,1,0:T(8,128)(2,1)S(1)} %shard_map.83), channel_id=1, replica_groups=mesh['aa_0'=4,'aa_1'=2,'ba_0'=4,'ba_1'=4] {'aa_0','aa_1','ba_0','ba_1'}, dimensions={0} | all-to-all | bytes 1048576 | tf_op jit(solution)/shard_map/all_to_all | solution.py:247
  497.6 5.8 %all-to-all-start.9 = ((bf16[128,32,128]{2,1,0:T(8,128)(2,1)}), bf16[128,32,128]{2,1,0:T(8,128)(2,1)}, u32[]{:S(2)}, u32[]{:S(2)}) async-start(bf16[128,32,128]{2,1,0:T(8,128)(2,1)} %copy-done.12), calls=%async_computation.9 | async-start | bytes 2097152 | tf_op jit(solution)/shard_map/all_to_all | solution.py:247
  508.2 13.7 %all-to-all-done.9.got_ref = bf16[128,32,128]{2,1,0:T(8,128)(2,1)} async-done(((bf16[128,32,128]{2,1,0:T(8,128)(2,1)}), bf16[128,32,128]{2,1,0:T(8,128)(2,1)}, u32[]{:S(2)}, u32[]{:S(2)}) %all-to-all-start.9) | async-done | bytes 1048608 | tf_op jit(solution)/shard_map/all_to_all | solution.py:247
  525.1 4.6 all-to-all-start.10
  532.9 15.8 %all-to-all-done.10.got_ref = bf16[128,32,128]{2,1,0:T(8,128)(2,1)S(1)} async-done(((bf16[128,32,128]{2,1,0:T(8,128)(2,1)}), bf16[128,32,128]{2,1,0:T(8,128)(2,1)S(1)}, u32[]{:S(2)}, u32[]{:S(2)}) %all-to-all-start.10) | async-done | bytes 1048608 | tf_op jit(solution)/shard_map/all_to_all | solution.py:247
  (153 shorter events, 85.6 us)
Async XLA Ops:
  0.6 10.9 %copy-start = (s32[16,16]{1,0:T(8,128)S(1)}, s32[16,16]{1,0:T(8,128)}, u32[]{:S(2)}) copy-start(s32[16,16]{1,0:T(8,128)} %param.20) | copy-start | bytes 3076
  0.6 10.8 %copy-start.20 = (s32[16,16]{1,0:T(8,128)S(1)}, s32[16,16]{1,0:T(8,128)}, u32[]{:S(2)}) copy-start(s32[16,16]{1,0:T(8,128)} %param.19) | copy-start | bytes 3076
  7.1 11.9 %all-to-all-start = ((f32[8,8,1024]{2,1,0:T(8,128)}), f32[8,8,1024]{2,1,0:T(8,128)S(1)}, u32[]{:S(2)}, u32[]{:S(2)}) async-start(f32[8,8,1024]{2,1,0:T(8,128)} %broadcast_in_dim.24), calls=%async_computation | async-start | bytes 524288 | tf_op jit(solution)/shard_map/all_to_all | solution.py:281
  19.1 2.0 copy-start.3
  26.8 4.1 copy-start.2
  30.9 8.1 %copy-start.21 = (s32[1,24,2]{1,2,0:T(2,128)S(1)}, s32[1,24,2]{1,2,0:T(2,128)}, u32[]{:S(2)}) copy-start(s32[1,24,2]{1,2,0:T(2,128)} %param.21) | copy-start | bytes 580
  30.9 169.8 %all-to-all-start.1 = ((bf16[16,448,768]{2,1,0:T(8,128)(2,1)}), bf16[16,448,768]{2,1,0:T(8,128)(2,1)}, u32[]{:S(2)}, u32[]{:S(2)}) async-start(bf16[16,448,768]{2,1,0:T(8,128)(2,1)} %copy-done.2), calls=%async_computation.1 | async-start | bytes 22020096 | tf_op jit(solution)/shard_map/all_to_all | solution.py:293
  200.7 59.2 %all-to-all-start.2 = ((bf16[16,464,256]{2,1,0:T(8,128)(2,1)}), bf16[16,464,256]{2,1,0:T(8,128)(2,1)}, u32[]{:S(2)}, u32[]{:S(2)}) async-start(bf16[16,464,256]{2,1,0:T(8,128)(2,1)} %copy-done.9), calls=%async_computation.2 | async-start | bytes 7602176 | tf_op jit(solution)/shard_map/all_to_all | solution.py:312
  218.2 64.4 %collective-permute-start = (s16[12,256,512]{2,1,0:T(8,128)(2,1)}, s16[12,256,512]{2,1,0:T(8,128)(2,1)}, u32[]{:S(2)}, u32[]{:S(2)}) collective-permute-start(s16[12,256,512]{2,1,0:T(8,128)(2,1)} %shard_map.70), channel_id=1, source_target_pairs={{0,16},{16,0},{1,17},{17,1},{2,18},{18,2},{3,19},{19,3},{4,20},{20... | collective-permute-start | bytes 9437192 | tf_op jit(solution)/shard_map/ppermute | solution.py:303
  271.3 35.6 %collective-permute-start.4 = (s16[12,256,512]{2,1,0:T(8,128)(2,1)}, s16[12,256,512]{2,1,0:T(8,128)(2,1)S(1)}, u32[]{:S(2)}, u32[]{:S(2)}) collective-permute-start(s16[12,256,512]{2,1,0:T(8,128)(2,1)} %shard_map.75), channel_id=1, source_target_pairs={{0,16},{16,0},{1,17},{17,1},{2,18},{18,2},{3,19},{19,3},{4,20},{20... | collective-permute-start | bytes 9437192 | tf_op jit(solution)/shard_map/ppermute | solution.py:303
  287.7 23.6 %collective-permute-start.1 = (s16[3,256,512]{2,1,0:T(8,128)(2,1)}, s16[3,256,512]{2,1,0:T(8,128)(2,1)}, u32[]{:S(2)}, u32[]{:S(2)}) collective-permute-start(s16[3,256,512]{2,1,0:T(8,128)(2,1)} %get-tuple-element.75), channel_id=1, source_target_pairs={{0,32},{32,64},{64,96},{96,0},{1,33},{33,65},{65,97},{97,1},{2,34}... | collective-permute-start | bytes 2359304 | tf_op jit(solution)/shard_map/ppermute | solution.py:307
  301.8 24.4 %collective-permute-start.2 = (s16[3,256,512]{2,1,0:T(8,128)(2,1)}, s16[3,256,512]{2,1,0:T(8,128)(2,1)}, u32[]{:S(2)}, u32[]{:S(2)}) collective-permute-start(s16[3,256,512]{2,1,0:T(8,128)(2,1)} %get-tuple-element.76), channel_id=1, source_target_pairs={{0,64},{32,96},{64,0},{96,32},{1,65},{33,97},{65,1},{97,33},{2,66}... | collective-permute-start | bytes 2359304 | tf_op jit(solution)/shard_map/ppermute | solution.py:307
  304.2 36.8 %collective-permute-start.3 = (s16[3,256,512]{2,1,0:T(8,128)(2,1)}, s16[3,256,512]{2,1,0:T(8,128)(2,1)}, u32[]{:S(2)}, u32[]{:S(2)}) collective-permute-start(s16[3,256,512]{2,1,0:T(8,128)(2,1)} %get-tuple-element.77), channel_id=1, source_target_pairs={{0,96},{32,0},{64,32},{96,64},{1,97},{33,1},{65,33},{97,65},{2,98}... | collective-permute-start | bytes 2359304 | tf_op jit(solution)/shard_map/ppermute | solution.py:307
  309.8 34.0 %collective-permute-start.5 = (s16[3,256,512]{2,1,0:T(8,128)(2,1)}, s16[3,256,512]{2,1,0:T(8,128)(2,1)S(1)}, u32[]{:S(2)}, u32[]{:S(2)}) collective-permute-start(s16[3,256,512]{2,1,0:T(8,128)(2,1)} %get-tuple-element.80), channel_id=1, source_target_pairs={{0,32},{32,64},{64,96},{96,0},{1,33},{33,65},{65,97},{97,1},{2,34}... | collective-permute-start | bytes 2359304 | tf_op jit(solution)/shard_map/ppermute | solution.py:307
  309.8 49.9 %collective-permute-start.6 = (s16[3,256,512]{2,1,0:T(8,128)(2,1)}, s16[3,256,512]{2,1,0:T(8,128)(2,1)}, u32[]{:S(2)}, u32[]{:S(2)}) collective-permute-start(s16[3,256,512]{2,1,0:T(8,128)(2,1)} %get-tuple-element.81), channel_id=1, source_target_pairs={{0,64},{32,96},{64,0},{96,32},{1,65},{33,97},{65,1},{97,33},{2,66}... | collective-permute-start | bytes 2359304 | tf_op jit(solution)/shard_map/ppermute | solution.py:307
  311.3 62.7 %collective-permute-start.7 = (s16[3,256,512]{2,1,0:T(8,128)(2,1)}, s16[3,256,512]{2,1,0:T(8,128)(2,1)}, u32[]{:S(2)}, u32[]{:S(2)}) collective-permute-start(s16[3,256,512]{2,1,0:T(8,128)(2,1)} %get-tuple-element.82), channel_id=1, source_target_pairs={{0,96},{32,0},{64,32},{96,64},{1,97},{33,1},{65,33},{97,65},{2,98}... | collective-permute-start | bytes 2359304 | tf_op jit(solution)/shard_map/ppermute | solution.py:307
  313.5 27.5 %copy-start.15 = (s16[3,256,512]{2,1,0:T(8,128)(2,1)S(1)}, s16[3,256,512]{2,1,0:T(8,128)(2,1)}, u32[]{:S(2)}) copy-start(s16[3,256,512]{2,1,0:T(8,128)(2,1)} %copy-done.14) | copy-start | bytes 2359300
  343.8 35.1 %copy-start.5 = (f32[3,512,256]{2,1,0:T(8,128)}, f32[3,512,256]{2,1,0:T(8,128)S(1)}, u32[]{:S(2)}) copy-start(f32[3,512,256]{2,1,0:T(8,128)S(1)} %get-tuple-element.78.first_ref) | copy-start | bytes 4718596
  381.0 20.3 %all-to-all-start.3 = ((bf16[128,16,128]{2,1,0:T(8,128)(2,1)}), bf16[128,16,128]{2,1,0:T(8,128)(2,1)}, u32[]{:S(2)}, u32[]{:S(2)}) async-start(bf16[128,16,128]{2,1,0:T(8,128)(2,1)} %copy-done.13), calls=%async_computation.3 | async-start | bytes 1048576 | tf_op jit(solution)/shard_map/all_to_all | solution.py:247
  401.4 19.8 %copy-start.6 = (f32[3,512,256]{2,1,0:T(8,128)S(1)}, f32[3,512,256]{2,1,0:T(8,128)}, u32[]{:S(2)}) copy-start(f32[3,512,256]{2,1,0:T(8,128)} %copy-done.5) | copy-start | bytes 4718596
  401.4 19.8 %copy-start.8 = (f32[3,512,256]{2,1,0:T(8,128)S(1)}, f32[3,512,256]{2,1,0:T(8,128)}, u32[]{:S(2)}) copy-start(f32[3,512,256]{2,1,0:T(8,128)} %copy-done.7) | copy-start | bytes 4718596
  497.6 24.4 %all-to-all-start.9 = ((bf16[128,32,128]{2,1,0:T(8,128)(2,1)}), bf16[128,32,128]{2,1,0:T(8,128)(2,1)}, u32[]{:S(2)}, u32[]{:S(2)}) async-start(bf16[128,32,128]{2,1,0:T(8,128)(2,1)} %copy-done.12), calls=%async_computation.9 | async-start | bytes 2097152 | tf_op jit(solution)/shard_map/all_to_all | solution.py:247
  521.9 27.7 %copy-start.1 = (s32[16,16]{1,0:T(8,128)S(1)}, s32[16,16]{1,0:T(8,128)}, u32[]{:S(2)}) copy-start(s32[16,16]{1,0:T(8,128)} %param.20) | copy-start | bytes 3076
  525.1 23.7 %all-to-all-start.10 = ((bf16[128,32,128]{2,1,0:T(8,128)(2,1)}), bf16[128,32,128]{2,1,0:T(8,128)(2,1)S(1)}, u32[]{:S(2)}, u32[]{:S(2)}) async-start(bf16[128,32,128]{2,1,0:T(8,128)(2,1)} %copy-done.11), calls=%async_computation.10 | async-start | bytes 2097152 | tf_op jit(solution)/shard_map/all_to_all | solution.py:247
  (12 other events, 14.8 us)

commit v2 on v1

v2 whole, which is shorter than its diff:
```python
import jax
import jax.numpy as jnp
from jax import lax
from jax.experimental import pallas as pl
from jax.experimental.pallas import tpu as pltpu
from jax.sharding import Mesh
from jax.sharding import PartitionSpec as P

BS = 512
SWEEPS = 4
BA = ("ba_0", "ba_1")
AA = ("aa_0", "aa_1")
ALL = AA + BA
LANES = 128
TILES = BS // LANES
HALF = BS // 2
FIXED = 32000.0
IDS = 16

smoothing_regularizer = 0.02
norm_floor = 1e-06

f32, bf16, i16, i32 = jnp.float32, jnp.bfloat16, jnp.int16, jnp.int32


def call(kernel, out_shape, grid_spec, flops, bytes_accessed, args):
    return pl.pallas_call(
        kernel,
        out_shape=out_shape,
        grid_spec=grid_spec,
        compiler_params=pltpu.CompilerParams(vmem_limit_bytes=8 * 2**20),
        cost_estimate=pl.CostEstimate(
            flops=flops, bytes_accessed=bytes_accessed, transcendentals=0
        ),
    )(*args)


def pack_kernel(one_ref, two_ref, a_ref, b_ref, inv_a_ref, inv_b_ref, ids_ref, first_ref, second_ref):
    width = a_ref.shape[0]
    unit_a = (a_ref[...].astype(f32) * inv_a_ref[...]).astype(bf16)
    first_ref[0, :, :BS] = (b_ref[...].astype(f32) * inv_b_ref[...]).astype(bf16)
    first_ref[0, :, BS:] = unit_a[:, :HALF]
    second_ref[0, :width, :] = unit_a[:, HALF:]
    second_ref[0, width:, :] = ids_ref[...]


def pack(one, two, a, b, inv_a, inv_b, ids):
    width, owners = a.shape[0], one.shape[0]
    spec = pltpu.PrefetchScalarGridSpec(
        num_scalar_prefetch=2,
        grid=(owners,),
        in_specs=[
            pl.BlockSpec((width, BS), lambda o, r1, r2: (0, r1[o])),
            pl.BlockSpec((width, BS), lambda o, r1, r2: (0, r2[o])),
            pl.BlockSpec((1, BS), lambda o, r1, r2: (0, r1[o])),
            pl.BlockSpec((1, BS), lambda o, r1, r2: (0, r2[o])),
            pl.BlockSpec((IDS, HALF), lambda o, r1, r2: (0, 0)),
        ],
        out_specs=[
            pl.BlockSpec((1, width, BS + HALF), lambda o, r1, r2: (o, 0, 0)),
            pl.BlockSpec((1, width + IDS, HALF), lambda o, r1, r2: (o, 0, 0)),
        ],
    )
    shape = [
        jax.ShapeDtypeStruct((owners, width, BS + HALF), bf16),
        jax.ShapeDtypeStruct((owners, width + IDS, HALF), bf16),
    ]
    size = owners * width * 2 * BS
    return call(pack_kernel, shape, spec, 2 * size, 4 * size, (one, two, a, b, inv_a, inv_b, ids))


def cosine_kernel(s_ref, r_ref, a_ref, b_ref, out_ref):
    partial = lax.dot_general(
        a_ref[0], b_ref[0], (((0,), (0,)), ((), ())), preferred_element_type=f32
    )
    out_ref[0] = jnp.floor(partial * FIXED + 0.5).astype(i32).astype(i16)


def cosines(sources, a, a_at, b, width):
    pairs = sources[0].shape[0]
    spec = pltpu.PrefetchScalarGridSpec(
        num_scalar_prefetch=2,
        grid=(pairs,),
        in_specs=[
            pl.BlockSpec((1, width, HALF), lambda q, s, r: (s[q], 0, a_at)),
            pl.BlockSpec((1, width, BS), lambda q, s, r: (r[q], 0, 0)),
        ],
        out_specs=pl.BlockSpec((1, HALF, BS), lambda q, s, r: (q, 0, 0)),
    )
    shape = jax.ShapeDtypeStruct((pairs, HALF, BS), i16)
    flops = 2 * pairs * HALF * BS * width
    moved = pairs * (width * (HALF + BS) + HALF * BS) * 2
    return call(cosine_kernel, shape, spec, flops, moved, (*sources, a, b))


def both_cores_kernel(x_ref, *refs):
    ins, outs = refs[:8], refs[8:]
    for d in range(4):
        total = ins[d][...].astype(i32) + ins[4 + d][...].astype(i32)
        outs[d][...] = total.astype(i16)


def both_cores(chip, own, other):
    each = own.shape[0] // 4
    block = (1, HALF, BS)

    def at(d):
        return pl.BlockSpec(block, lambda k, x: (lax.rem(x[0] + d, 4) * each + k, 0, 0))

    spec = pltpu.PrefetchScalarGridSpec(
        num_scalar_prefetch=1,
        grid=(each,),
        in_specs=[at(d) for d in range(4)] * 2,
        out_specs=[pl.BlockSpec(block, lambda k, x: (k, 0, 0))] * 4,
    )
    shape = [jax.ShapeDtypeStruct((each, HALF, BS), i16)] * 4
    size = own.size
    return call(
        both_cores_kernel, shape, spec, size, 6 * size, (chip, *([own] * 4), *([other] * 4))
    )


def affinity_kernel(a_ref, b_ref, c_ref, d_ref, out_ref, turned_ref):
    total = a_ref[0].astype(i32) + b_ref[0].astype(i32)
    total = total + c_ref[0].astype(i32) + d_ref[0].astype(i32)
    value = jnp.exp(total.astype(f32) * (1.0 / (FIXED * smoothing_regularizer)))
    out_ref[0] = value
    turned_ref[0] = value.T


def affinity(parts):
    each = parts[0].shape[0]
    spec = pl.GridSpec(
        grid=(each,),
        in_specs=[pl.BlockSpec((1, HALF, BS), lambda k: (k, 0, 0))] * 4,
        out_specs=[
            pl.BlockSpec((1, HALF, BS), lambda k: (k, 0, 0)),
            pl.BlockSpec((1, BS, HALF), lambda k: (k, 0, 0)),
        ],
    )
    shape = [
        jax.ShapeDtypeStruct((each, HALF, BS), f32),
        jax.ShapeDtypeStruct((each, BS, HALF), f32),
    ]
    size = each * HALF * BS
    return call(affinity_kernel, shape, spec, 8 * size, 16 * size, tuple(parts))


def emit_rows(rows, out_ref):
    high = [r.astype(bf16).astype(f32) for r in rows]
    low = [r - h for r, h in zip(rows, high)]
    tile = jnp.concatenate(high + low, axis=0).astype(bf16)
    out_ref[...] = jnp.broadcast_to(tile[None], out_ref.shape)


def times_rows(mats, scale):
    turned = None if scale is None else scale.T
    rows = []
    for k in range(mats[0].shape[0]):
        if len(mats) == 2 and mats[0].shape[1] == HALF:
            total = None
            for j in range(TILES):
                part = mats[j // 2][k, (j % 2) * LANES : (j % 2 + 1) * LANES, :]
                if turned is not None:
                    part = part * turned[:, TILES * k + j : TILES * k + j + 1]
                part = jnp.sum(part, axis=0, keepdims=True)
                total = part if total is None else total + part
            rows += [total[:, j * LANES : (j + 1) * LANES] for j in range(TILES)]
        else:
            for m in mats:
                total = None
                for j in range(TILES):
                    part = m[k, j * LANES : (j + 1) * LANES, :]
                    if turned is not None:
                        part = part * turned[:, TILES * k + j : TILES * k + j + 1]
                    part = jnp.sum(part, axis=0, keepdims=True)
                    total = part if total is None else total + part
                rows += [total[:, j * LANES : (j + 1) * LANES] for j in range(TILES // 2)]
    return rows


def start_kernel(first_ref, second_ref, out_ref):
    emit_rows(times_rows((first_ref, second_ref), None), out_ref)


def totals_of(hot, got_ref):
    got = got_ref[...].reshape(-1, LANES)
    return jnp.dot(hot, got, preferred_element_type=f32)


def step_kernel(got_ref, hot_ref, first_ref, second_ref, out_ref):
    scale = 1.0 / (1.0 + totals_of(hot_ref[...], got_ref))
    padded = jnp.concatenate([scale, jnp.zeros((LANES - scale.shape[0], LANES), f32)], axis=0)
    emit_rows(times_rows((first_ref, second_ref), padded), out_ref)


def log_kernel(got_ref, hot_ref, log_ref):
    log_ref[...] = jnp.log(1.0 / (1.0 + totals_of(hot_ref[...], got_ref)))


def on_chip(kernel, out_shape, flops, args):
    return pl.pallas_call(
        kernel,
        out_shape=out_shape,
        in_specs=[pl.BlockSpec(memory_space=pltpu.VMEM)] * len(args),
        out_specs=pl.BlockSpec(memory_space=pltpu.VMEM),
        compiler_params=pltpu.CompilerParams(vmem_limit_bytes=8 * 2**20),
        cost_estimate=pl.CostEstimate(flops=flops, bytes_accessed=flops, transcendentals=0),
    )(*args)


def step(got, hot, mats, devices):
    rows = 2 * TILES * mats[0].shape[0]
    out = jax.ShapeDtypeStruct((devices, rows, LANES), bf16)
    flops = 4 * mats[0].size
    if got is None:
        return on_chip(start_kernel, out, flops, tuple(mats))
    return on_chip(step_kernel, out, flops, (got, hot, *mats))


def exchanged(x):
    return lax.all_to_all(x, ALL, 0, 0, tiled=True)


def hot_rows(wanted, present):
    devices, pairs = present.shape
    shape = (devices, 2, pairs, TILES)
    col_id = jnp.broadcast_to(present[:, None, :, None], shape).reshape(1, -1)
    col_tile = lax.broadcasted_iota(i32, shape, 3).reshape(1, -1)
    row_id = jnp.repeat(wanted, TILES)[:, None]
    row_tile = jnp.tile(jnp.arange(TILES), wanted.shape[0])[:, None]
    return ((row_id == col_id) & (row_tile == col_tile)).astype(bf16)


tied = lax.optimization_barrier


def per_device(initial_dictionary_matrix, decoder_two, route_one, route_two, candidate_pair_slots):
    column = lax.axis_index(BA)
    chip = lax.axis_index("aa_0")
    core = lax.axis_index("aa_1")
    owners = lax.axis_size(BA)
    depth = lax.axis_size(AA)
    devices = owners * depth
    blocks_dev = initial_dictionary_matrix.shape[0] // BS
    width = initial_dictionary_matrix.shape[1]

    one_t, two_t = initial_dictionary_matrix.T, decoder_two.T
    sums = jnp.concatenate(
        [jnp.sum(jnp.square(t.astype(f32)), axis=0) for t in (one_t, two_t)]
    )
    sums = sums.reshape(8, -1)
    my_one = lax.dynamic_index_in_dim(route_one, column, 0, False)
    my_two = lax.dynamic_index_in_dim(route_two, column, 0, False)
    slots = candidate_pair_slots[0]
    pairs = slots.shape[0]
    ids = jnp.zeros((IDS, HALF), bf16).at[:2, :pairs].set(slots.T.astype(bf16))
    mine = pairs // 2

    def of_core(which):
        return [lax.dynamic_slice_in_dim(slots[:, i], which * mine, mine, 0) for i in range(2)]

    own_slots, other_slots = of_core(core), of_core(1 - core)
    chip_list = chip.reshape(1).astype(i32)
    small = (my_one, my_two, ids, own_slots, other_slots, chip_list)
    sums, small = tied((sums, small))
    my_one, my_two, ids, own_slots, other_slots, chip_list = small
    sums = lax.all_to_all(
        jnp.broadcast_to(sums[None], (depth, *sums.shape)), AA, 0, 0, tiled=True
    ).sum(axis=0)
    inverse = lax.rsqrt(sums + norm_floor).reshape(2, 1, -1)

    first, second = pack(my_one, my_two, one_t, two_t, inverse[0], inverse[1], ids)
    first, second = tied((first, second))
    first = lax.all_to_all(first, BA, 0, 0, tiled=True)
    first, second = tied((first, second))
    swap = [(0, 1), (1, 0)]

    def by_chip(a, a_at):
        other = cosines(other_slots, a, a_at, first, width)
        other = lax.ppermute(other, "aa_1", swap)
        own = cosines(own_slots, a, a_at, first, width)
        return both_cores(chip_list, own, other)

    def to_chips(parts):
        return [parts[0]] + [
            lax.ppermute(parts[d], "aa_0", [(x, (x + d) % 4) for x in range(4)])
            for d in range(1, 4)
        ]

    parts = by_chip(first, 2)
    parts, second = tied((parts, second))
    upper = to_chips(parts)
    second = lax.all_to_all(second, BA, 0, 0, tiled=True)
    parts, second = tied((by_chip(second, 0), second))
    lower = to_chips(parts)
    k_upper, t_upper = affinity(upper)
    k_lower, t_lower = affinity(lower)

    def masks():
        every = second[:, width : width + 2, :pairs].astype(i32)
        s_all, r_all = every[:, 0], every[:, 1]

        def block_of(source, route):
            chosen = source[:, :, None] == jnp.arange(owners)[None, None, :]
            return source * blocks_dev + jnp.sum(jnp.where(chosen, route.T[:, None, :], 0), axis=2)

        each = pairs // depth

        def by_device(x):
            x = x.reshape(owners, 2, 4, each)
            return x.transpose(2, 1, 0, 3).reshape(devices, each)

        row_dev, col_dev = by_device(block_of(s_all, route_one)), by_device(block_of(r_all, route_two))
        me = (chip * 2 + core) * owners + column
        pad = jnp.full((4 - each,), -2, i32)
        my_rows = jnp.concatenate([lax.dynamic_index_in_dim(row_dev, me, 0, False), pad])
        my_cols = jnp.concatenate([lax.dynamic_index_in_dim(col_dev, me, 0, False), pad])
        own_blocks = column * blocks_dev + jnp.arange(blocks_dev)
        return [
            hot_rows(my_rows, row_dev),
            hot_rows(my_cols, col_dev),
            hot_rows(own_blocks, row_dev),
            hot_rows(own_blocks, col_dev),
        ]

    hot = masks()

    mats, hot = tied(((k_upper, k_lower, t_upper, t_lower), hot))
    by_row, by_col = mats[2:], mats[:2]
    got = exchanged(step(None, None, by_row, devices))
    for _ in range(SWEEPS - 1):
        got = exchanged(step(got, hot[0], by_col, devices))
        got = exchanged(step(got, hot[1], by_row, devices))
    last = exchanged(step(got, hot[0], by_col, devices))
    got, last = tied((got, last))
    logs = jax.ShapeDtypeStruct((blocks_dev * TILES, LANES), f32)
    row_log = on_chip(log_kernel, logs, 2**20, (got, hot[2]))
    col_log = on_chip(log_kernel, logs, 2**20, (last, hot[3]))
    return row_log.reshape(-1), col_log.reshape(-1)


def solution(mesh):
    torus = Mesh(mesh.devices.reshape(4, 2, 4, 4), ("aa_0", "aa_1", "ba_0", "ba_1"))
    in_specs = (P(BA, AA), P(BA, AA), P(), P(), P(BA, None, None))
    out_specs = (P(BA), P(BA))
    return jax.shard_map(
        per_device, mesh=torus, in_specs=in_specs, out_specs=out_specs, check_vma=False
    )
```

time: 552 us -> 511 us (0.926)
  blocking collectives: 89.2 us -> 358 us
  waiting for transfers between devices: 299 us -> 66.6 us
  starting transfers between devices: 45.1 us -> 7.4 us
  Pallas kernels: 71.5 us -> 43.5 us
  local copies, waits for them, and re-layouts: 36.6 us -> 25.6 us
    all_to_all x6 -> x0, waiting for transfers between devices: 246 us -> none  [the longest x1 156 us: per_device(): first = lax.all_to_all(first, BA, 0, 0, tiled=True)]
    all_to_all x0 -> x3, blocking collectives: none -> 194 us  [the longest x1 131 us: per_device(): first = lax.all_to_all(first, BA, 0, 0, tiled=True)]
    all_to_all x5 -> x8, blocking collectives: 89.2 us -> 165 us  [exchanged(): return lax.all_to_all(x, ALL, 0, 0, tiled=True)]
    all_to_all x6 -> x0, starting transfers between devices: 36.2 us -> none  [the longest x3 17.7 us: exchanged(): return lax.all_to_all(x, ALL, 0, 0, tiled=True)]
    pallas_call x10 -> x9, Pallas kernels: 60.2 us -> 35.5 us  [call(): pl.pallas_call(kernel, out_shape=out_shape, grid_spec=grid_spec, compiler...]
    ppermute x8, waiting for transfers between devices: 52.5 us -> 66.6 us  [the longest x6 66.6 us: to_chips(): lax.ppermute(parts[d], 'aa_0', [(x, (x + d) % 4) for x in range(4)])]
    gather x6 -> x0, local copies, waits for them, and re-layouts: 6.52 us -> none  [the longest x3 3.26 us: per_device(): col_all = r_all * blocks_dev + route_two[r_all, owner_ids]]
    unnamed x49 -> x41, local copies, waits for them, and re-layouts: 21.2 us -> 18.2 us
  transfers between devices with their start and end apart: 14 -> 8, of which waited for: 10 -> 4; matrix products, arithmetic and copies ran while one was open for 3% -> 1% of each run, Pallas kernels for 10% -> 3%
where the time goes in v2:
time: 511 us; the launch traced here: 509 us
  blocking collectives  358 us (70%)
  waiting for transfers between devices  66.6 us (13%)
  Pallas kernels  43.5 us (9%)
  local copies, waits for them, and re-layouts  25.6 us (5%)
  starting transfers between devices  7.4 us (1%)
  other arithmetic  7.03 us (1%)
    all_to_all x8, blocking collectives, exchanged(): return lax.all_to_all(x, ALL, 0, 0, tiled=True)  165 us
    all_to_all x1, blocking collectives, per_device(): first = lax.all_to_all(first, BA, 0, 0, tiled=True)  131 us
    ppermute x6, waiting for transfers between devices, to_chips(): lax.ppermute(parts[d], 'aa_0', [(x, (x + d) % 4) for x in range(4)])  66.6 us
    all_to_all x1, blocking collectives, per_device(): second = lax.all_to_all(second, BA, 0, 0, tiled=True)  50.5 us
    pallas_call x9, Pallas kernels, call(): pl.pallas_call(kernel, out_shape=out_shape, grid_spec=grid_spec, compiler...  35.5 us
    unnamed x41, local copies, waits for them, and re-layouts  18.2 us
    all_to_all x1, blocking collectives, per_device(): lax.all_to_all(jnp.broadcast_to(sums[None], (depth, *sums.shape)), AA, 0,...  11.7 us
  transfers between devices with their start and end apart: 8, of which 4 were waited for; matrix products, arithmetic and copies ran while one was open for 1% of the time, Pallas kernels for 3%

profile of v2, /device:TPU:0, one launch (start us, length us, event | category | flops | bytes accessed | tf_op | source)
XLA Modules:
  0.0 509.5 jit_solution(13782709351362952084)
XLA Ops:
  3.6 2.8 multiply_reduce_fusion.1
  6.4 2.8 multiply_reduce_fusion
  9.3 11.7 %all_to_all.55 = f32[8,8,1024]{2,1,0:T(8,128)S(1)} all-to-all(f32[8,8,1024]{2,1,0:T(8,128)S(1)} %broadcast_in_dim.30), channel_id=1, replica_groups=mesh['aa_0'=4,'aa_1'=2,'ba_0'=4,'ba_1'=4] {'aa_0','aa_1'}, dimensions={0} | all-to-all | bytes 524288 | tf_op jit(solution)/shard_map/all_to_all | solution.py:268
  25.2 4.3 shard_map.68
  29.5 131.4 %all_to_all.56.a_ref.b_ref = bf16[16,448,768]{2,1,0:T(8,128)(2,1)S(1)} all-to-all(bf16[16,448,768]{2,1,0:T(8,128)(2,1)S(1)} %get-tuple-element.66), channel_id=1, replica_groups=mesh['aa_0'=4,'aa_1'=2,'ba_0'=4,'ba_1'=4] {'ba_0','ba_1'}, dimensions={0} | all-to-all | bytes 22020096 | tf_op jit(solution)/shard_map/all_to_all | solution.py:275
  160.9 5.7 %shard_map.70 = s16[12,256,512]{2,1,0:T(8,128)(2,1)S(1)} custom-call(s32[12]{0:T(128)S(1)} %get-tuple-element.69.s_ref, s32[12]{0:T(128)S(1)} %get-tuple-element.70.r_ref, bf16[16,448,768]{2,1,0:T(8,128)(2,1)S(1)} %all_to_all.56.a_ref.b_ref, bf16[16,448,768]{2,1,0:T(8,128)(2,1)S(1)} %all_to_all.56.a_ref.b_ref), custom_call_target="tpu_custom_call" | custom-call | flops 1409286144 | bytes 11403264 | tf_op jit(solution)/shard_map/pallas_call | solution.py:27
  166.7 5.7 %shard_map.69.refs_0_.refs_1_.refs_2_.refs_3_ = s16[12,256,512]{2,1,0:T(8,128)(2,1)S(1)} custom-call(s32[12]{0:T(128)S(1)} %get-tuple-element.60.s_ref, s32[12]{0:T(128)S(1)} %get-tuple-element.61.r_ref, bf16[16,448,768]{2,1,0:T(8,128)(2,1)S(1)} %all_to_all.56.a_ref.b_ref, bf16[16,448,768]{2,1,0:T(8,128)(2,1)S(1)} %all_to_all.56.a_ref.b_ref), custom_call_target="tpu_custom_call" | custom-call | flops 1409286144 | bytes 11403264 | tf_op jit(solution)/shard_map/pallas_call | solution.py:27
  175.4 50.5 %all_to_all.57.a_ref = bf16[16,464,256]{2,1,0:T(8,128)(2,1)S(1)} all-to-all(bf16[16,464,256]{2,1,0:T(8,128)(2,1)S(1)} %get-tuple-element.81), channel_id=1, replica_groups=mesh['aa_0'=4,'aa_1'=2,'ba_0'=4,'ba_1'=4] {'ba_0','ba_1'}, dimensions={0} | all-to-all | bytes 7602176 | tf_op jit(solution)/shard_map/all_to_all | solution.py:294
  225.8 7.9 %shard_map.74 = s16[12,256,512]{2,1,0:T(8,128)(2,1)} custom-call(s32[12]{0:T(128)S(1)} %get-tuple-element.69.s_ref, s32[12]{0:T(128)S(1)} %get-tuple-element.70.r_ref, bf16[16,464,256]{2,1,0:T(8,128)(2,1)S(1)} %all_to_all.57.a_ref, bf16[16,448,768]{2,1,0:T(8,128)(2,1)S(1)} %all_to_all.56.a_ref.b_ref), custom_call_target="tpu_custom_call" | custom-call | flops 1409286144 | bytes 11403264 | tf_op jit(solution)/shard_map/pallas_call | solution.py:27
  239.9 32.2 %collective-permute-done.1.b_ref = s16[3,256,512]{2,1,0:T(8,128)(2,1)} collective-permute-done((s16[3,256,512]{2,1,0:T(8,128)(2,1)}, s16[3,256,512]{2,1,0:T(8,128)(2,1)}, u32[]{:S(2)}, u32[]{:S(2)}) %collective-permute-start.1) | collective-permute-done | bytes 786464 | tf_op jit(solution)/shard_map/ppermute | solution.py:287
  273.8 2.8 shard_map.72
  278.9 4.1 copy-done.1
  285.1 5.4 %shard_map.73.refs_0_.refs_1_.refs_2_.refs_3_ = s16[12,256,512]{2,1,0:T(8,128)(2,1)S(1)} custom-call(s32[12]{0:T(128)S(1)} %get-tuple-element.60.s_ref, s32[12]{0:T(128)S(1)} %get-tuple-element.61.r_ref, bf16[16,464,256]{2,1,0:T(8,128)(2,1)S(1)} %copy-done.3, bf16[16,448,768]{2,1,0:T(8,128)(2,1)S(1)} %copy-done.1), custom_call_target="tpu_custom_call" | custom-call | flops 1409286144 | bytes 11403264 | tf_op jit(solution)/shard_map/pallas_call | solution.py:27
  298.1 3.6 collective-permute-start.6
  302.0 16.3 %collective-permute-done.5.b_ref = s16[3,256,512]{2,1,0:T(8,128)(2,1)S(1)} collective-permute-done((s16[3,256,512]{2,1,0:T(8,128)(2,1)}, s16[3,256,512]{2,1,0:T(8,128)(2,1)S(1)}, u32[]{:S(2)}, u32[]{:S(2)}) %collective-permute-start.5) | collective-permute-done | bytes 786464 | tf_op jit(solution)/shard_map/ppermute | solution.py:287
  318.4 17.5 %collective-permute-done.6.c_ref = s16[3,256,512]{2,1,0:T(8,128)(2,1)S(1)} collective-permute-done((s16[3,256,512]{2,1,0:T(8,128)(2,1)}, s16[3,256,512]{2,1,0:T(8,128)(2,1)S(1)}, u32[]{:S(2)}, u32[]{:S(2)}) %collective-permute-start.6) | collective-permute-done | bytes 786464 | tf_op jit(solution)/shard_map/ppermute | solution.py:287
  336.9 21.7 %all_to_all.58.got_ref = bf16[128,24,128]{2,1,0:T(8,128)(2,1)S(1)} all-to-all(bf16[128,24,128]{2,1,0:T(8,128)(2,1)S(1)} %shard_map.77), channel_id=1, replica_groups=mesh['aa_0'=4,'aa_1'=2,'ba_0'=4,'ba_1'=4] {'aa_0','aa_1','ba_0','ba_1'}, dimensions={0} | all-to-all | bytes 1572864 | tf_op jit(solution)/shard_map/all_to_all | solution.py:222
  359.5 20.5 %all_to_all.59.got_ref = bf16[128,24,128]{2,1,0:T(8,128)(2,1)S(1)} all-to-all(bf16[128,24,128]{2,1,0:T(8,128)(2,1)S(1)} %shard_map.78), channel_id=1, replica_groups=mesh['aa_0'=4,'aa_1'=2,'ba_0'=4,'ba_1'=4] {'aa_0','aa_1','ba_0','ba_1'}, dimensions={0} | all-to-all | bytes 1572864 | tf_op jit(solution)/shard_map/all_to_all | solution.py:222
  380.8 20.4 %all_to_all.60.got_ref = bf16[128,24,128]{2,1,0:T(8,128)(2,1)S(1)} all-to-all(bf16[128,24,128]{2,1,0:T(8,128)(2,1)S(1)} %shard_map.79), channel_id=1, replica_groups=mesh['aa_0'=4,'aa_1'=2,'ba_0'=4,'ba_1'=4] {'aa_0','aa_1','ba_0','ba_1'}, dimensions={0} | all-to-all | bytes 1572864 | tf_op jit(solution)/shard_map/all_to_all | solution.py:222
  402.1 20.4 %all_to_all.61.got_ref = bf16[128,24,128]{2,1,0:T(8,128)(2,1)S(1)} all-to-all(bf16[128,24,128]{2,1,0:T(8,128)(2,1)S(1)} %shard_map.80), channel_id=1, replica_groups=mesh['aa_0'=4,'aa_1'=2,'ba_0'=4,'ba_1'=4] {'aa_0','aa_1','ba_0','ba_1'}, dimensions={0} | all-to-all | bytes 1572864 | tf_op jit(solution)/shard_map/all_to_all | solution.py:222
  423.4 20.4 %all_to_all.62.got_ref = bf16[128,24,128]{2,1,0:T(8,128)(2,1)S(1)} all-to-all(bf16[128,24,128]{2,1,0:T(8,128)(2,1)S(1)} %shard_map.81), channel_id=1, replica_groups=mesh['aa_0'=4,'aa_1'=2,'ba_0'=4,'ba_1'=4] {'aa_0','aa_1','ba_0','ba_1'}, dimensions={0} | all-to-all | bytes 1572864 | tf_op jit(solution)/shard_map/all_to_all | solution.py:222
  444.7 20.4 %all_to_all.63.got_ref = bf16[128,24,128]{2,1,0:T(8,128)(2,1)S(1)} all-to-all(bf16[128,24,128]{2,1,0:T(8,128)(2,1)S(1)} %shard_map.82), channel_id=1, replica_groups=mesh['aa_0'=4,'aa_1'=2,'ba_0'=4,'ba_1'=4] {'aa_0','aa_1','ba_0','ba_1'}, dimensions={0} | all-to-all | bytes 1572864 | tf_op jit(solution)/shard_map/all_to_all | solution.py:222
  466.1 20.4 %all_to_all.64.got_ref = bf16[128,24,128]{2,1,0:T(8,128)(2,1)S(1)} all-to-all(bf16[128,24,128]{2,1,0:T(8,128)(2,1)S(1)} %shard_map.83), channel_id=1, replica_groups=mesh['aa_0'=4,'aa_1'=2,'ba_0'=4,'ba_1'=4] {'aa_0','aa_1','ba_0','ba_1'}, dimensions={0} | all-to-all | bytes 1572864 | tf_op jit(solution)/shard_map/all_to_all | solution.py:222
  487.3 20.4 %all_to_all.65.got_ref = bf16[128,24,128]{2,1,0:T(8,128)(2,1)S(1)} all-to-all(bf16[128,24,128]{2,1,0:T(8,128)(2,1)S(1)} %shard_map.84), channel_id=1, replica_groups=mesh['aa_0'=4,'aa_1'=2,'ba_0'=4,'ba_1'=4] {'aa_0','aa_1','ba_0','ba_1'}, dimensions={0} | all-to-all | bytes 1572864 | tf_op jit(solution)/shard_map/all_to_all | solution.py:222
  (123 shorter events, 39.1 us)
Async XLA Ops:
  21.1 2.0 copy-start.8
  23.2 2.0 copy-start.9
  160.9 64.9 %copy-start = (bf16[16,448,768]{2,1,0:T(8,128)(2,1)}, bf16[16,448,768]{2,1,0:T(8,128)(2,1)S(1)}, u32[]{:S(2)}) copy-start(bf16[16,448,768]{2,1,0:T(8,128)(2,1)S(1)} %all_to_all.56.a_ref.b_ref) | copy-start | bytes 33030148
  166.6 5.8 %collective-permute-start = (s16[12,256,512]{2,1,0:T(8,128)(2,1)S(1)}, s16[12,256,512]{2,1,0:T(8,128)(2,1)S(1)}, u32[]{:S(2)}, u32[]{:S(2)}) collective-permute-start(s16[12,256,512]{2,1,0:T(8,128)(2,1)S(1)} %shard_map.70), channel_id=1, source_target_pairs={{0,16},{16,0},{1,17},{17,1},{2,18},{18,2},{3,19},{19,3},{4,20},{20... | collective-permute-start | bytes 9437192 | tf_op jit(solution)/shard_map/ppermute | solution.py:281
  225.8 7.9 %copy-start.2 = (bf16[16,464,256]{2,1,0:T(8,128)(2,1)}, bf16[16,464,256]{2,1,0:T(8,128)(2,1)S(1)}, u32[]{:S(2)}) copy-start(bf16[16,464,256]{2,1,0:T(8,128)(2,1)S(1)} %all_to_all.57.a_ref) | copy-start | bytes 11403268
  225.8 11.4 %copy-start.17 = (s32[16,16]{1,0:T(8,128)S(1)}, s32[16,16]{1,0:T(8,128)}, u32[]{:S(2)}) copy-start(s32[16,16]{1,0:T(8,128)} %param.9) | copy-start | bytes 3076
  225.8 11.4 %copy-start.18 = (s32[16,16]{1,0:T(8,128)S(1)}, s32[16,16]{1,0:T(8,128)}, u32[]{:S(2)}) copy-start(s32[16,16]{1,0:T(8,128)} %param.10) | copy-start | bytes 3076
  233.7 56.8 %collective-permute-start.4 = (s16[12,256,512]{2,1,0:T(8,128)(2,1)}, s16[12,256,512]{2,1,0:T(8,128)(2,1)S(1)}, u32[]{:S(2)}, u32[]{:S(2)}) collective-permute-start(s16[12,256,512]{2,1,0:T(8,128)(2,1)} %shard_map.74), channel_id=1, source_target_pairs={{0,16},{16,0},{1,17},{17,1},{2,18},{18,2},{3,19},{19,3},{4,20},{20... | collective-permute-start | bytes 9437192 | tf_op jit(solution)/shard_map/ppermute | solution.py:281
  233.7 38.3 %collective-permute-start.1 = (s16[3,256,512]{2,1,0:T(8,128)(2,1)}, s16[3,256,512]{2,1,0:T(8,128)(2,1)}, u32[]{:S(2)}, u32[]{:S(2)}) collective-permute-start(s16[3,256,512]{2,1,0:T(8,128)(2,1)} %get-tuple-element.77), channel_id=1, source_target_pairs={{0,32},{32,64},{64,96},{96,0},{1,33},{33,65},{65,97},{97,1},{2,34}... | collective-permute-start | bytes 2359304 | tf_op jit(solution)/shard_map/ppermute | solution.py:287
  234.3 37.8 %collective-permute-start.2 = (s16[3,256,512]{2,1,0:T(8,128)(2,1)}, s16[3,256,512]{2,1,0:T(8,128)(2,1)}, u32[]{:S(2)}, u32[]{:S(2)}) collective-permute-start(s16[3,256,512]{2,1,0:T(8,128)(2,1)} %get-tuple-element.78), channel_id=1, source_target_pairs={{0,64},{32,96},{64,0},{96,32},{1,65},{33,97},{65,1},{97,33},{2,66}... | collective-permute-start | bytes 2359304 | tf_op jit(solution)/shard_map/ppermute | solution.py:287
  236.3 36.3 %collective-permute-start.3 = (s16[3,256,512]{2,1,0:T(8,128)(2,1)}, s16[3,256,512]{2,1,0:T(8,128)(2,1)}, u32[]{:S(2)}, u32[]{:S(2)}) collective-permute-start(s16[3,256,512]{2,1,0:T(8,128)(2,1)} %get-tuple-element.79), channel_id=1, source_target_pairs={{0,96},{32,0},{64,32},{96,64},{1,97},{33,1},{65,33},{97,65},{2,98}... | collective-permute-start | bytes 2359304 | tf_op jit(solution)/shard_map/ppermute | solution.py:287
  272.7 1.1 copy-start.13
  276.6 1.1 copy-start.4
  277.7 1.1 copy-start.6
  278.9 4.1 copy-start.1
  283.0 2.1 copy-start.3
  291.4 0.9 copy-start.10
  292.3 0.9 copy-start.14
  295.0 41.7 %copy-start.7 = (f32[3,512,256]{2,1,0:T(8,128)S(1)}, f32[3,512,256]{2,1,0:T(8,128)}, u32[]{:S(2)}) copy-start(f32[3,512,256]{2,1,0:T(8,128)} %copy-done.6) | copy-start | bytes 4718596
  295.0 40.9 %copy-start.11 = (s16[3,256,512]{2,1,0:T(8,128)(2,1)S(1)}, s16[3,256,512]{2,1,0:T(8,128)(2,1)}, u32[]{:S(2)}) copy-start(s16[3,256,512]{2,1,0:T(8,128)(2,1)} %copy-done.10) | copy-start | bytes 2359300
  297.8 20.5 %collective-permute-start.5 = (s16[3,256,512]{2,1,0:T(8,128)(2,1)}, s16[3,256,512]{2,1,0:T(8,128)(2,1)S(1)}, u32[]{:S(2)}, u32[]{:S(2)}) collective-permute-start(s16[3,256,512]{2,1,0:T(8,128)(2,1)} %copy-done.16), channel_id=1, source_target_pairs={{0,32},{32,64},{64,96},{96,0},{1,33},{33,65},{65,97},{97,1},{2,34}... | collective-permute-start | bytes 2359304 | tf_op jit(solution)/shard_map/ppermute | solution.py:287
  298.1 37.8 %collective-permute-start.6 = (s16[3,256,512]{2,1,0:T(8,128)(2,1)}, s16[3,256,512]{2,1,0:T(8,128)(2,1)S(1)}, u32[]{:S(2)}, u32[]{:S(2)}) collective-permute-start(s16[3,256,512]{2,1,0:T(8,128)(2,1)} %copy-done.15), channel_id=1, source_target_pairs={{0,64},{32,96},{64,0},{96,32},{1,65},{33,97},{65,1},{97,33},{2,66}... | collective-permute-start | bytes 2359304 | tf_op jit(solution)/shard_map/ppermute | solution.py:287
  301.6 34.2 %collective-permute-start.7 = (s16[3,256,512]{2,1,0:T(8,128)(2,1)}, s16[3,256,512]{2,1,0:T(8,128)(2,1)S(1)}, u32[]{:S(2)}, u32[]{:S(2)}) collective-permute-start(s16[3,256,512]{2,1,0:T(8,128)(2,1)} %copy-done.14), channel_id=1, source_target_pairs={{0,96},{32,0},{64,32},{96,64},{1,97},{33,1},{65,33},{97,65},{2,98}... | collective-permute-start | bytes 2359304 | tf_op jit(solution)/shard_map/ppermute | solution.py:287
  302.0 56.6 %copy-start.5 = (f32[3,256,512]{2,1,0:T(8,128)S(1)}, f32[3,256,512]{2,1,0:T(8,128)}, u32[]{:S(2)}) copy-start(f32[3,256,512]{2,1,0:T(8,128)} %copy-done.4) | copy-start | bytes 4718596
  (3 other events, 2.6 us)

commit v3 on v2

v3 whole, which is shorter than its diff:
```python
import jax
import jax.numpy as jnp
from jax import lax
from jax.experimental import pallas as pl
from jax.experimental.pallas import tpu as pltpu
from jax.sharding import Mesh
from jax.sharding import PartitionSpec as P

BS = 512
SWEEPS = 4
BA = ("ba_0", "ba_1")
AA = ("aa_0", "aa_1")
ALL = AA + BA
LANES = 128
TILES = BS // LANES
UPPER = 3 * LANES
FIXED = 32000.0
IDS = 16


smoothing_regularizer = 0.02
norm_floor = 1e-06

f32, bf16, i16, i32 = jnp.float32, jnp.bfloat16, jnp.int16, jnp.int32


def call(kernel, out_shape, grid_spec, flops, bytes_accessed, args, mebibytes=8):
    return pl.pallas_call(
        kernel,
        out_shape=out_shape,
        grid_spec=grid_spec,
        compiler_params=pltpu.CompilerParams(vmem_limit_bytes=mebibytes * 2**20),
        cost_estimate=pl.CostEstimate(
            flops=flops, bytes_accessed=bytes_accessed, transcendentals=0
        ),
    )(*args)


def squares_kernel(one_ref, two_ref, sums_ref):
    for i, ref in enumerate((one_ref, two_ref)):
        total = jnp.sum(jnp.square(ref[...].astype(f32)), axis=0, keepdims=True)
        sums_ref[:, i : i + 1, :] = jnp.broadcast_to(total[None], (sums_ref.shape[0], 1, BS))


def squares(one, two, depth):
    width, rows = one.shape
    block = pl.BlockSpec((width, BS), lambda k: (0, k))
    spec = pl.GridSpec(
        grid=(rows // BS,),
        in_specs=[block, block],
        out_specs=pl.BlockSpec((depth, 2, BS), lambda k: (0, 0, k)),
    )
    shape = jax.ShapeDtypeStruct((depth, 2, rows), f32)
    return call(squares_kernel, shape, spec, 4 * one.size, 8 * one.size, (one, two), 60)


def pack_kernel(
    me_ref, one_ref, two_ref, a_ref, b_ref, inv_a_ref, inv_b_ref, slots_ref, first_ref, second_ref
):
    width, pairs = a_ref.shape[0], slots_ref.shape[1]
    unit_a = (a_ref[...].astype(f32) * inv_a_ref[0:1, :]).astype(bf16)
    first_ref[0, :, :BS] = (b_ref[...].astype(f32) * inv_b_ref[1:2, :]).astype(bf16)
    first_ref[0, :, BS:] = unit_a[:, :UPPER]
    second_ref[0, :width, :] = unit_a[:, UPPER:]
    second_ref[0, width:, :] = jnp.zeros((IDS, LANES), bf16)
    second_ref[0, width : width + 2, :pairs] = slots_ref[...].astype(f32).astype(bf16)


def pack(me, one, two, a, b, inverse, slots):
    width, owners = a.shape[0], one.shape[0]
    spec = pltpu.PrefetchScalarGridSpec(
        num_scalar_prefetch=3,
        grid=(owners,),
        in_specs=[
            pl.BlockSpec((width, BS), lambda o, me, r1, r2: (0, r1[me[0], o])),
            pl.BlockSpec((width, BS), lambda o, me, r1, r2: (0, r2[me[0], o])),
            pl.BlockSpec((2, BS), lambda o, me, r1, r2: (0, r1[me[0], o])),
            pl.BlockSpec((2, BS), lambda o, me, r1, r2: (0, r2[me[0], o])),
            pl.BlockSpec(slots.shape, lambda o, me, r1, r2: (0, 0)),
        ],
        out_specs=[
            pl.BlockSpec((1, width, BS + UPPER), lambda o, me, r1, r2: (o, 0, 0)),
            pl.BlockSpec((1, width + IDS, LANES), lambda o, me, r1, r2: (o, 0, 0)),
        ],
    )
    shape = [
        jax.ShapeDtypeStruct((owners, width, BS + UPPER), bf16),
        jax.ShapeDtypeStruct((owners, width + IDS, LANES), bf16),
    ]
    size = owners * width * 2 * BS
    args = (me, one, two, a, b, inverse, inverse, slots)
    return call(pack_kernel, shape, spec, 2 * size, 4 * size, args)


def cosine_kernel(core_ref, slots_ref, *refs):
    out_ref, b_ref, tiles = refs[-1], refs[-2], refs[:-2]
    for t, a_ref in enumerate(tiles):
        partial = lax.dot_general(
            a_ref[0], b_ref[0], (((0,), (0,)), ((), ())), preferred_element_type=f32
        )
        fixed = jnp.floor(partial * FIXED + 0.5).astype(i32).astype(i16)
        out_ref[0, t * LANES : (t + 1) * LANES, :] = fixed


def cosines(core, slots, a, tiles, b, width):
    pairs = slots.shape[1] // 2

    def tile(t):
        return pl.BlockSpec((1, width, LANES), lambda q, c, s: (s[0, c[0] * pairs + q], 0, t))

    rows = LANES * len(tiles)
    spec = pltpu.PrefetchScalarGridSpec(
        num_scalar_prefetch=2,
        grid=(pairs,),
        in_specs=[tile(t) for t in tiles]
        + [pl.BlockSpec((1, width, BS), lambda q, c, s: (s[1, c[0] * pairs + q], 0, 0))],
        out_specs=pl.BlockSpec((1, rows, BS), lambda q, c, s: (q, 0, 0)),
    )
    shape = jax.ShapeDtypeStruct((pairs, rows, BS), i16)
    flops = 2 * pairs * rows * BS * width
    moved = pairs * (width * (rows + BS) + rows * BS) * 2
    return call(cosine_kernel, shape, spec, flops, moved, (core, slots, *([a] * len(tiles)), b))


def both_cores_kernel(x_ref, *refs):
    ins, outs = refs[:8], refs[8:]
    for d in range(4):
        total = ins[d][...].astype(i32) + ins[4 + d][...].astype(i32)
        outs[d][...] = total.astype(i16)


def both_cores(chip, own, other):
    each = own.shape[0] // 4
    block = (1, *own.shape[1:])

    def at(d):
        return pl.BlockSpec(block, lambda k, x: (lax.rem(x[0] + d, 4) * each + k, 0, 0))

    spec = pltpu.PrefetchScalarGridSpec(
        num_scalar_prefetch=1,
        grid=(each,),
        in_specs=[at(d) for d in range(4)] * 2,
        out_specs=[pl.BlockSpec(block, lambda k, x: (k, 0, 0))] * 4,
    )
    shape = [jax.ShapeDtypeStruct((each, *own.shape[1:]), i16)] * 4
    size = own.size
    return call(
        both_cores_kernel, shape, spec, size, 6 * size, (chip, *([own] * 4), *([other] * 4))
    )


def affinity_kernel(a_ref, b_ref, c_ref, d_ref, out_ref, turned_ref):
    total = a_ref[0].astype(i32) + b_ref[0].astype(i32)
    total = total + c_ref[0].astype(i32) + d_ref[0].astype(i32)
    value = jnp.exp(total.astype(f32) * (1.0 / (FIXED * smoothing_regularizer)))
    out_ref[0] = value
    turned_ref[0] = value.T


def affinity(parts):
    each, rows, cols = parts[0].shape
    spec = pl.GridSpec(
        grid=(each,),
        in_specs=[pl.BlockSpec((1, rows, cols), lambda k: (k, 0, 0))] * 4,
        out_specs=[
            pl.BlockSpec((1, rows, cols), lambda k: (k, 0, 0)),
            pl.BlockSpec((1, cols, rows), lambda k: (k, 0, 0)),
        ],
    )
    shape = [
        jax.ShapeDtypeStruct((each, rows, cols), f32),
        jax.ShapeDtypeStruct((each, cols, rows), f32),
    ]
    size = each * rows * cols
    return call(affinity_kernel, shape, spec, 8 * size, 16 * size, tuple(parts))


def emit_rows(rows, out_ref):
    high = [r.astype(bf16).astype(f32) for r in rows]
    low = [r - h for r, h in zip(rows, high)]
    tile = jnp.concatenate(high + low, axis=0).astype(bf16)
    out_ref[...] = jnp.broadcast_to(tile[None], out_ref.shape)


def times_rows(mats, scale):
    turned = None if scale is None else scale.T

    def tile(m, at, k, j):
        part = m[k, at * LANES : (at + 1) * LANES, :]
        if turned is not None:
            part = part * turned[:, TILES * k + j : TILES * k + j + 1]
        return jnp.sum(part, axis=0, keepdims=True)

    rows = []
    for k in range(mats[0].shape[0]):
        if mats[0].shape[1] == BS:
            groups = [[tile(m, j, k, j) for j in range(TILES)] for m in mats]
        else:
            places = [(m, at) for m in mats for at in range(m.shape[1] // LANES)]
            groups = [[tile(m, at, k, j) for j, (m, at) in enumerate(places)]]
        for g in groups:
            total = (g[0] + g[1]) + (g[2] + g[3])
            rows += [total[:, t : t + LANES] for t in range(0, total.shape[1], LANES)]
    return rows


def start_kernel(first_ref, second_ref, out_ref):
    emit_rows(times_rows((first_ref, second_ref), None), out_ref)


def totals_of(hot, got_ref):
    got = got_ref[...].reshape(-1, LANES)
    return jnp.dot(hot, got, preferred_element_type=f32)


def step_kernel(got_ref, hot_ref, first_ref, second_ref, out_ref):
    scale = 1.0 / (1.0 + totals_of(hot_ref[...], got_ref))
    padded = jnp.concatenate([scale, jnp.zeros((LANES - scale.shape[0], LANES), f32)], axis=0)
    emit_rows(times_rows((first_ref, second_ref), padded), out_ref)


def log_kernel(row_got_ref, row_hot_ref, col_got_ref, col_hot_ref, row_log_ref, col_log_ref):
    row_log_ref[...] = jnp.log(1.0 / (1.0 + totals_of(row_hot_ref[...], row_got_ref)))
    col_log_ref[...] = jnp.log(1.0 / (1.0 + totals_of(col_hot_ref[...], col_got_ref)))


def on_chip(kernel, out_shape, flops, args):
    return pl.pallas_call(
        kernel,
        out_shape=out_shape,
        in_specs=[pl.BlockSpec(memory_space=pltpu.VMEM)] * len(args),
        out_specs=jax.tree.map(lambda _: pl.BlockSpec(memory_space=pltpu.VMEM), out_shape),
        compiler_params=pltpu.CompilerParams(vmem_limit_bytes=8 * 2**20),
        cost_estimate=pl.CostEstimate(flops=flops, bytes_accessed=flops, transcendentals=0),
    )(*args)


def step(got, hot, mats, devices):
    rows = 2 * TILES * mats[0].shape[0]
    out = jax.ShapeDtypeStruct((devices, rows, LANES), bf16)
    flops = 4 * mats[0].size
    if got is None:
        return on_chip(start_kernel, out, flops, tuple(mats))
    return on_chip(step_kernel, out, flops, (got, hot, *mats))


def exchanged(x):
    return lax.all_to_all(x, ALL, 0, 0, tiled=True)


def hot_rows(wanted, present):
    devices, pairs = present.shape
    shape = (devices, 2, pairs, TILES)
    col_id = jnp.broadcast_to(present[:, None, :, None], shape).reshape(1, -1)
    col_tile = lax.broadcasted_iota(i32, shape, 3).reshape(1, -1)
    row_id = jnp.repeat(wanted, TILES)[:, None]
    row_tile = jnp.tile(jnp.arange(TILES), wanted.shape[0])[:, None]
    return ((row_id == col_id) & (row_tile == col_tile)).astype(bf16)


tied = lax.optimization_barrier


def per_device(initial_dictionary_matrix, decoder_two, route_one, route_two, candidate_pair_slots):
    column = lax.axis_index(BA)
    chip = lax.axis_index("aa_0")
    core = lax.axis_index("aa_1")
    owners = lax.axis_size(BA)
    depth = lax.axis_size(AA)
    devices = owners * depth
    blocks_dev = initial_dictionary_matrix.shape[0] // BS
    width = initial_dictionary_matrix.shape[1]

    def scalar(x):
        return x.reshape(1).astype(i32)

    one_t, two_t = initial_dictionary_matrix.T, decoder_two.T
    sums = squares(one_t, two_t, depth)
    places = (scalar(column), scalar(chip), scalar(core), scalar(1 - core))
    sums, places = tied((sums, places))
    at_column, at_chip, at_core, at_other = places
    sums = lax.all_to_all(sums, AA, 0, 0, tiled=True).sum(axis=0)
    inverse = lax.rsqrt(sums + norm_floor)

    slots = candidate_pair_slots[0].T
    pairs = slots.shape[1]
    first, second = pack(at_column, route_one, route_two, one_t, two_t, inverse, slots)
    first, second = tied((first, second))
    first = lax.all_to_all(first, BA, 0, 0, tiled=True)
    first, second = tied((first, second))
    swap = [(0, 1), (1, 0)]

    def by_chip(a, tiles):
        other = cosines(at_other, slots, a, tiles, first, width)
        other = lax.ppermute(other, "aa_1", swap)
        own = cosines(at_core, slots, a, tiles, first, width)
        return both_cores(at_chip, own, other)

    def to_chips(parts):
        return [parts[0]] + [
            lax.ppermute(parts[d], "aa_0", [(x, (x + d) % 4) for x in range(4)])
            for d in range(1, 4)
        ]

    parts = by_chip(first, (4, 5, 6))
    parts, second = tied((parts, second))
    upper = to_chips(parts)
    second = lax.all_to_all(second, BA, 0, 0, tiled=True)
    parts, second = tied((by_chip(second, (0,)), second))
    lower = to_chips(parts)
    k_upper, t_upper = affinity(upper)
    k_lower, t_lower = affinity(lower)

    def masks():
        every = second[:, width : width + 2, :pairs].astype(i32)
        s_all, r_all = every[:, 0], every[:, 1]

        def block_of(source, route):
            chosen = source[:, :, None] == jnp.arange(owners)[None, None, :]
            return source * blocks_dev + jnp.sum(jnp.where(chosen, route.T[:, None, :], 0), axis=2)

        each = pairs // depth

        def by_device(x):
            x = x.reshape(owners, 2, 4, each)
            return x.transpose(2, 1, 0, 3).reshape(devices, each)

        row_dev, col_dev = by_device(block_of(s_all, route_one)), by_device(block_of(r_all, route_two))
        me = (chip * 2 + core) * owners + column
        pad = jnp.full((4 - each,), -2, i32)
        my_rows = jnp.concatenate([lax.dynamic_index_in_dim(row_dev, me, 0, False), pad])
        my_cols = jnp.concatenate([lax.dynamic_index_in_dim(col_dev, me, 0, False), pad])
        own_blocks = column * blocks_dev + jnp.arange(blocks_dev)
        return [
            hot_rows(my_rows, row_dev),
            hot_rows(my_cols, col_dev),
            hot_rows(own_blocks, row_dev),
            hot_rows(own_blocks, col_dev),
        ]

    hot = masks()

    mats, hot = tied(((k_upper, k_lower, t_upper, t_lower), hot))
    by_row, by_col = mats[2:], mats[:2]
    got = exchanged(step(None, None, by_row, devices))
    for _ in range(SWEEPS - 1):
        got = exchanged(step(got, hot[0], by_col, devices))
        got = exchanged(step(got, hot[1], by_row, devices))
    last = exchanged(step(got, hot[0], by_col, devices))
    got, last = tied((got, last))
    logs = [jax.ShapeDtypeStruct((blocks_dev * TILES, LANES), f32)] * 2
    row_log, col_log = on_chip(log_kernel, logs, 2**20, (got, hot[2], last, hot[3]))
    return row_log.reshape(-1), col_log.reshape(-1)


def solution(mesh):
    torus = Mesh(mesh.devices.reshape(4, 2, 4, 4), ("aa_0", "aa_1", "ba_0", "ba_1"))
    in_specs = (P(BA, AA), P(BA, AA), P(), P(), P(BA, None, None))
    out_specs = (P(BA), P(BA))
    return jax.shard_map(
        per_device, mesh=torus, in_specs=in_specs, out_specs=out_specs, check_vma=False
    )
```

time: 511 us -> 540 us (1.057)
  local copies, waits for them, and re-layouts: 25.6 us -> 50.6 us
  Pallas kernels: 43.5 us -> 52.5 us
    all_to_all x1, blocking collectives: 50.5 us -> 29.5 us  [per_device(): second = lax.all_to_all(second, BA, 0, 0, tiled=True)]
    all_to_all x1, blocking collectives: 131 us -> 151 us  [per_device(): first = lax.all_to_all(first, BA, 0, 0, tiled=True)]
    pallas_call x9 -> x10, Pallas kernels: 35.5 us -> 45.9 us  [call(): pl.pallas_call(kernel, out_shape=out_shape, grid_spec=grid_spec, compiler...]
    eq x8, local copies, waits for them, and re-layouts: 2.32 us -> 8.33 us  [hot_rows(): return ((row_id == col_id) & (row_tile == col_tile)).astype(bf16)]
    reduce_sum x3 -> x1, other arithmetic: 5.62 us -> 0.09 us  [per_device(): sums = lax.all_to_all(sums, AA, 0, 0, tiled=True).sum(axis=0)]
    unnamed x41 -> x38, local copies, waits for them, and re-layouts: 18.2 us -> 17.1 us
where the time goes in v3:
time: 540 us; the launch traced here: 538 us
  blocking collectives  357 us (66%)
  waiting for transfers between devices  62.3 us (12%)
  Pallas kernels  52.5 us (10%)
  local copies, waits for them, and re-layouts  50.6 us (9%)
  other arithmetic  7.43 us (1%)
  starting transfers between devices  6.83 us (1%)
    all_to_all x8, blocking collectives, exchanged(): return lax.all_to_all(x, ALL, 0, 0, tiled=True)  165 us
    all_to_all x1, blocking collectives, per_device(): first = lax.all_to_all(first, BA, 0, 0, tiled=True)  151 us
    ppermute x6, waiting for transfers between devices, to_chips(): lax.ppermute(parts[d], 'aa_0', [(x, (x + d) % 4) for x in range(4)])  61.9 us
    pallas_call x10, Pallas kernels, call(): pl.pallas_call(kernel, out_shape=out_shape, grid_spec=grid_spec, compiler...  45.9 us
    all_to_all x1, blocking collectives, per_device(): second = lax.all_to_all(second, BA, 0, 0, tiled=True)  29.5 us
    unnamed x38, local copies, waits for them, and re-layouts  17.1 us
    all_to_all x1, blocking collectives, per_device(): sums = lax.all_to_all(sums, AA, 0, 0, tiled=True).sum(axis=0)  11.9 us
  transfers between devices with their start and end apart: 8, of which 4 were waited for; matrix products, arithmetic and copies ran while one was open for 1% of the time, Pallas kernels for 3%

profile of v3, /device:TPU:0, one launch (start us, length us, event | category | flops | bytes accessed | tf_op | source)
XLA Modules:
  0.0 537.7 jit_solution(9819892049334860001)
XLA Ops:
  0.7 6.4 %shard_map.68 = f32[8,2,4096]{2,1,0:T(2,128)} custom-call(bf16[448,4096]{1,0:T(8,128)(2,1)} %bitcast.32, bf16[448,4096]{1,0:T(8,128)(2,1)} %bitcast.34), custom_call_target="tpu_custom_call" | custom-call | flops 7340032 | bytes 14680064 | tf_op jit(solution)/shard_map/pallas_call | solution.py:28
  7.0 11.9 %all_to_all.55 = f32[8,2,4096]{2,1,0:T(2,128)S(1)} all-to-all(f32[8,2,4096]{2,1,0:T(2,128)} %shard_map.68), channel_id=1, replica_groups=mesh['aa_0'=4,'aa_1'=2,'ba_0'=4,'ba_1'=4] {'aa_0','aa_1'}, dimensions={0} | all-to-all | bytes 524288 | tf_op jit(solution)/shard_map/all_to_all | solution.py:282
  23.2 5.0 shard_map.69
  28.2 151.1 %all_to_all.56.refs_0_.refs_1_.refs_2_.refs_3_ = bf16[16,448,896]{2,1,0:T(8,128)(2,1)S(1)} all-to-all(bf16[16,448,896]{2,1,0:T(8,128)(2,1)S(1)} %get-tuple-element.49), channel_id=1, replica_groups=mesh['aa_0'=4,'aa_1'=2,'ba_0'=4,'ba_1'=4] {'ba_0','ba_1'}, dimensions={0} | all-to-all | bytes 25690112 | tf_op jit(solution)/shard_map/all_to_all | solution.py:289
  179.2 7.5 %shard_map.71 = s16[12,384,512]{2,1,0:T(8,128)(2,1)S(1)} custom-call(s32[1]{0:T(128)} %bitcast.5.core_ref, s32[2,24]{1,0:T(2,128)S(1)} %bitcast.39, bf16[16,448,896]{2,1,0:T(8,128)(2,1)S(1)} %all_to_all.56.refs_0_.refs_1_.refs_2_.refs_3_, bf16[16,448,896]{2,1,0:T(8,128)(2,1)S(1)} %all_to_all.56.refs_0_.refs_1_.refs_2_.refs_3_, ...), custom_call_target="tpu_custom_call" | custom-call | flops 2113929216 | bytes 14352384 | tf_op jit(solution)/shard_map/pallas_call | solution.py:28
  186.8 7.5 %shard_map.70.refs_0_.refs_1_.refs_2_.refs_3_ = s16[12,384,512]{2,1,0:T(8,128)(2,1)S(1)} custom-call(s32[1]{0:T(128)} %bitcast.4.core_ref, s32[2,24]{1,0:T(2,128)S(1)} %bitcast.40, bf16[16,448,896]{2,1,0:T(8,128)(2,1)S(1)} %all_to_all.56.refs_0_.refs_1_.refs_2_.refs_3_, bf16[16,448,896]{2,1,0:T(8,128)(2,1)S(1)} %all_to_all.56.refs_0_.refs_1_.refs_2_.refs_3_, ...), custom_call_target="tpu_custom_call" | custom-call | flops 2113929216 | bytes 14352384 | tf_op jit(solution)/shard_map/pallas_call | solution.py:28
  194.7 2.5 shard_map.72
  197.2 29.5 %all_to_all.57.refs_0_ = bf16[16,464,128]{2,1,0:T(8,128)(2,1)S(1)} all-to-all(bf16[16,464,128]{2,1,0:T(8,128)(2,1)S(1)} %get-tuple-element.63), channel_id=1, replica_groups=mesh['aa_0'=4,'aa_1'=2,'ba_0'=4,'ba_1'=4] {'ba_0','ba_1'}, dimensions={0} | all-to-all | bytes 3801088 | tf_op jit(solution)/shard_map/all_to_all | solution.py:308
  226.6 6.7 %shard_map.75 = s16[12,128,512]{2,1,0:T(8,128)(2,1)} custom-call(s32[1]{0:T(128)} %bitcast.5.core_ref, s32[2,24]{1,0:T(2,128)S(1)} %bitcast.41, bf16[16,464,128]{2,1,0:T(8,128)(2,1)S(1)} %all_to_all.57.refs_0_, bf16[16,448,896]{2,1,0:T(8,128)(2,1)S(1)} %all_to_all.56.refs_0_.refs_1_.refs_2_.refs_3_), custom_call_target="tpu_custom_call" | custom-call | flops 704643072 | bytes 8454144 | tf_op jit(solution)/shard_map/pallas_call | solution.py:28
  242.4 46.0 %collective-permute-done.1.b_ref = s16[3,384,512]{2,1,0:T(8,128)(2,1)S(1)} collective-permute-done((s16[3,384,512]{2,1,0:T(8,128)(2,1)}, s16[3,384,512]{2,1,0:T(8,128)(2,1)S(1)}, u32[]{:S(2)}, u32[]{:S(2)}) %collective-permute-start.1) | collective-permute-done | bytes 1179680 | tf_op jit(solution)/shard_map/ppermute | solution.py:301
  293.1 2.7 shard_map.73
  297.2 4.6 copy-done.1
  301.8 4.6 shard_map.74.refs_0_.refs_1_.refs_2_.refs_3_
  306.5 2.5 shard_map.76
  343.3 2.5 collective-permute-start.6
  348.4 15.4 %collective-permute-done.5.b_ref = s16[3,128,512]{2,1,0:T(8,128)(2,1)S(1)} collective-permute-done((s16[3,128,512]{2,1,0:T(8,128)(2,1)}, s16[3,128,512]{2,1,0:T(8,128)(2,1)S(1)}, u32[]{:S(2)}, u32[]{:S(2)}) %collective-permute-start.5) | collective-permute-done | bytes 393248 | tf_op jit(solution)/shard_map/ppermute | solution.py:301
  366.6 21.5 %all_to_all.58.got_ref = bf16[128,24,128]{2,1,0:T(8,128)(2,1)S(1)} all-to-all(bf16[128,24,128]{2,1,0:T(8,128)(2,1)S(1)} %shard_map.78), channel_id=1, replica_groups=mesh['aa_0'=4,'aa_1'=2,'ba_0'=4,'ba_1'=4] {'aa_0','aa_1','ba_0','ba_1'}, dimensions={0} | all-to-all | bytes 1572864 | tf_op jit(solution)/shard_map/all_to_all | solution.py:248
  388.9 20.4 %all_to_all.59.got_ref = bf16[128,24,128]{2,1,0:T(8,128)(2,1)S(1)} all-to-all(bf16[128,24,128]{2,1,0:T(8,128)(2,1)S(1)} %shard_map.79), channel_id=1, replica_groups=mesh['aa_0'=4,'aa_1'=2,'ba_0'=4,'ba_1'=4] {'aa_0','aa_1','ba_0','ba_1'}, dimensions={0} | all-to-all | bytes 1572864 | tf_op jit(solution)/shard_map/all_to_all | solution.py:248
  410.1 20.5 %all_to_all.60.got_ref = bf16[128,24,128]{2,1,0:T(8,128)(2,1)S(1)} all-to-all(bf16[128,24,128]{2,1,0:T(8,128)(2,1)S(1)} %shard_map.80), channel_id=1, replica_groups=mesh['aa_0'=4,'aa_1'=2,'ba_0'=4,'ba_1'=4] {'aa_0','aa_1','ba_0','ba_1'}, dimensions={0} | all-to-all | bytes 1572864 | tf_op jit(solution)/shard_map/all_to_all | solution.py:248
  431.4 20.4 %all_to_all.61.got_ref = bf16[128,24,128]{2,1,0:T(8,128)(2,1)S(1)} all-to-all(bf16[128,24,128]{2,1,0:T(8,128)(2,1)S(1)} %shard_map.81), channel_id=1, replica_groups=mesh['aa_0'=4,'aa_1'=2,'ba_0'=4,'ba_1'=4] {'aa_0','aa_1','ba_0','ba_1'}, dimensions={0} | all-to-all | bytes 1572864 | tf_op jit(solution)/shard_map/all_to_all | solution.py:248
  452.6 20.4 %all_to_all.62.got_ref = bf16[128,24,128]{2,1,0:T(8,128)(2,1)S(1)} all-to-all(bf16[128,24,128]{2,1,0:T(8,128)(2,1)S(1)} %shard_map.82), channel_id=1, replica_groups=mesh['aa_0'=4,'aa_1'=2,'ba_0'=4,'ba_1'=4] {'aa_0','aa_1','ba_0','ba_1'}, dimensions={0} | all-to-all | bytes 1572864 | tf_op jit(solution)/shard_map/all_to_all | solution.py:248
  473.8 20.4 %all_to_all.63.got_ref = bf16[128,24,128]{2,1,0:T(8,128)(2,1)S(1)} all-to-all(bf16[128,24,128]{2,1,0:T(8,128)(2,1)S(1)} %shard_map.83), channel_id=1, replica_groups=mesh['aa_0'=4,'aa_1'=2,'ba_0'=4,'ba_1'=4] {'aa_0','aa_1','ba_0','ba_1'}, dimensions={0} | all-to-all | bytes 1572864 | tf_op jit(solution)/shard_map/all_to_all | solution.py:248
  495.1 20.4 %all_to_all.64.got_ref.row_got_ref = bf16[128,24,128]{2,1,0:T(8,128)(2,1)S(1)} all-to-all(bf16[128,24,128]{2,1,0:T(8,128)(2,1)S(1)} %shard_map.84), channel_id=1, replica_groups=mesh['aa_0'=4,'aa_1'=2,'ba_0'=4,'ba_1'=4] {'aa_0','aa_1','ba_0','ba_1'}, dimensions={0} | all-to-all | bytes 1572864 | tf_op jit(solution)/shard_map/all_to_all | solution.py:248
  516.3 20.4 %all_to_all.65.col_got_ref = bf16[128,24,128]{2,1,0:T(8,128)(2,1)S(1)} all-to-all(bf16[128,24,128]{2,1,0:T(8,128)(2,1)S(1)} %shard_map.85), channel_id=1, replica_groups=mesh['aa_0'=4,'aa_1'=2,'ba_0'=4,'ba_1'=4] {'aa_0','aa_1','ba_0','ba_1'}, dimensions={0} | all-to-all | bytes 1572864 | tf_op jit(solution)/shard_map/all_to_all | solution.py:248
  (107 shorter events, 65.7 us)
Async XLA Ops:
  0.6 18.4 %copy-start.12 = (s32[16,16]{1,0:T(8,128)S(1)}, s32[16,16]{1,0:T(8,128)}, u32[]{:S(2)}) copy-start(s32[16,16]{1,0:T(8,128)} %one_ref.1) | copy-start | bytes 3076
  0.6 18.4 %copy-start.13 = (s32[16,16]{1,0:T(8,128)S(1)}, s32[16,16]{1,0:T(8,128)}, u32[]{:S(2)}) copy-start(s32[16,16]{1,0:T(8,128)} %two_ref.1) | copy-start | bytes 3076
  0.7 18.4 %copy-start.14 = (s32[1,24,2]{1,2,0:T(2,128)S(1)}, s32[1,24,2]{1,2,0:T(2,128)}, u32[]{:S(2)}) copy-start(s32[1,24,2]{1,2,0:T(2,128)} %param.9) | copy-start | bytes 580
  19.1 2.0 copy-start.6
  21.1 2.0 copy-start.7
  179.2 47.4 %copy-start = (bf16[16,448,896]{2,1,0:T(8,128)(2,1)}, bf16[16,448,896]{2,1,0:T(8,128)(2,1)S(1)}, u32[]{:S(2)}) copy-start(bf16[16,448,896]{2,1,0:T(8,128)(2,1)S(1)} %all_to_all.56.refs_0_.refs_1_.refs_2_.refs_3_) | copy-start | bytes 38535172
  186.7 8.0 %collective-permute-start = (s16[12,384,512]{2,1,0:T(8,128)(2,1)S(1)}, s16[12,384,512]{2,1,0:T(8,128)(2,1)S(1)}, u32[]{:S(2)}, u32[]{:S(2)}) collective-permute-start(s16[12,384,512]{2,1,0:T(8,128)(2,1)S(1)} %shard_map.71), channel_id=1, source_target_pairs={{0,16},{16,0},{1,17},{17,1},{2,18},{18,2},{3,19},{19,3},{4,20},{20... | collective-permute-start | bytes 14155784 | tf_op jit(solution)/shard_map/ppermute | solution.py:295
  226.6 6.8 %copy-start.4 = (bf16[16,464,128]{2,1,0:T(8,128)(2,1)}, bf16[16,464,128]{2,1,0:T(8,128)(2,1)S(1)}, u32[]{:S(2)}) copy-start(bf16[16,464,128]{2,1,0:T(8,128)(2,1)S(1)} %all_to_all.57.refs_0_) | copy-start | bytes 5701636
  233.4 73.1 %collective-permute-start.4 = (s16[12,128,512]{2,1,0:T(8,128)(2,1)}, s16[12,128,512]{2,1,0:T(8,128)(2,1)}, u32[]{:S(2)}, u32[]{:S(2)}) collective-permute-start(s16[12,128,512]{2,1,0:T(8,128)(2,1)} %shard_map.75), channel_id=1, source_target_pairs={{0,16},{16,0},{1,17},{17,1},{2,18},{18,2},{3,19},{19,3},{4,20},{20... | collective-permute-start | bytes 4718600 | tf_op jit(solution)/shard_map/ppermute | solution.py:295
  233.4 55.1 %collective-permute-start.1 = (s16[3,384,512]{2,1,0:T(8,128)(2,1)}, s16[3,384,512]{2,1,0:T(8,128)(2,1)S(1)}, u32[]{:S(2)}, u32[]{:S(2)}) collective-permute-start(s16[3,384,512]{2,1,0:T(8,128)(2,1)} %get-tuple-element.59), channel_id=1, source_target_pairs={{0,32},{32,64},{64,96},{96,0},{1,33},{33,65},{65,97},{97,1},{2,34}... | collective-permute-start | bytes 3538952 | tf_op jit(solution)/shard_map/ppermute | solution.py:301
  234.0 55.5 %collective-permute-start.2 = (s16[3,384,512]{2,1,0:T(8,128)(2,1)}, s16[3,384,512]{2,1,0:T(8,128)(2,1)S(1)}, u32[]{:S(2)}, u32[]{:S(2)}) collective-permute-start(s16[3,384,512]{2,1,0:T(8,128)(2,1)} %get-tuple-element.60), channel_id=1, source_target_pairs={{0,64},{32,96},{64,0},{96,32},{1,65},{33,97},{65,1},{97,33},{2,66}... | collective-permute-start | bytes 3538952 | tf_op jit(solution)/shard_map/ppermute | solution.py:301
  236.0 54.5 %collective-permute-start.3 = (s16[3,384,512]{2,1,0:T(8,128)(2,1)}, s16[3,384,512]{2,1,0:T(8,128)(2,1)}, u32[]{:S(2)}, u32[]{:S(2)}) collective-permute-start(s16[3,384,512]{2,1,0:T(8,128)(2,1)} %get-tuple-element.61), channel_id=1, source_target_pairs={{0,96},{32,0},{64,32},{96,64},{1,97},{33,1},{65,33},{97,65},{2,98}... | collective-permute-start | bytes 3538952 | tf_op jit(solution)/shard_map/ppermute | solution.py:301
  242.4 54.8 %copy-start.15 = (s32[1,24,2]{1,2,0:T(2,128)S(1)}, s32[1,24,2]{1,2,0:T(2,128)}, u32[]{:S(2)}) copy-start(s32[1,24,2]{1,2,0:T(2,128)} %param.9) | copy-start | bytes 580
  242.4 54.8 %copy-start.5 = (bf16[16,464,128]{2,1,0:T(8,128)(2,1)S(1)}, bf16[16,464,128]{2,1,0:T(8,128)(2,1)}, u32[]{:S(2)}) copy-start(bf16[16,464,128]{2,1,0:T(8,128)(2,1)} %copy-done.4) | copy-start | bytes 5701636
  290.5 1.3 copy-start.9
  291.8 1.3 copy-start.11
  295.8 1.4 copy-start.2
  297.2 4.7 copy-start.1
  306.4 4.0 copy-start.17
  331.1 8.9 %copy-start.18 = (s32[3]{0:T(128)S(1)}, s32[3]{0:T(128)}, u32[]{:S(2)}) copy-start(s32[3]{0:T(128)} %dynamic-slice_reduce_fusion.1) | copy-start | bytes 40
  343.3 20.5 %collective-permute-start.5 = (s16[3,128,512]{2,1,0:T(8,128)(2,1)}, s16[3,128,512]{2,1,0:T(8,128)(2,1)S(1)}, u32[]{:S(2)}, u32[]{:S(2)}) collective-permute-start(s16[3,128,512]{2,1,0:T(8,128)(2,1)} %copy-done.16), channel_id=1, source_target_pairs={{0,32},{32,64},{64,96},{96,0},{1,33},{33,65},{65,97},{97,1},{2,34}... | collective-permute-start | bytes 1179656 | tf_op jit(solution)/shard_map/ppermute | solution.py:301
  343.3 20.5 %collective-permute-start.6 = (s16[3,128,512]{2,1,0:T(8,128)(2,1)S(1)}, s16[3,128,512]{2,1,0:T(8,128)(2,1)S(1)}, u32[]{:S(2)}, u32[]{:S(2)}) collective-permute-start(s16[3,128,512]{2,1,0:T(8,128)(2,1)S(1)} %get-tuple-element.70), channel_id=1, source_target_pairs={{0,64},{32,96},{64,0},{96,32},{1,65},{33,97},{65,1},{97,33},{2,66}... | collective-permute-start | bytes 1179656 | tf_op jit(solution)/shard_map/ppermute | solution.py:301
  345.8 18.4 %collective-permute-start.7 = (s16[3,128,512]{2,1,0:T(8,128)(2,1)S(1)}, s16[3,128,512]{2,1,0:T(8,128)(2,1)S(1)}, u32[]{:S(2)}, u32[]{:S(2)}) collective-permute-start(s16[3,128,512]{2,1,0:T(8,128)(2,1)S(1)} %get-tuple-element.71), channel_id=1, source_target_pairs={{0,96},{32,0},{64,32},{96,64},{1,97},{33,1},{65,33},{97,65},{2,98}... | collective-permute-start | bytes 1179656 | tf_op jit(solution)/shard_map/ppermute | solution.py:301
  364.8 1.7 copy-start.3
  (3 other events, 2.8 us)

commit v4 on v3

--- a/solution.py
+++ b/solution.py
@@ -13,7 +13,8 @@
 ALL = AA + BA
 LANES = 128
 TILES = BS // LANES
-UPPER = 3 * LANES
+HALF = BS // 2
+CHUNKS = (2, 1, 1)
 FIXED = 32000.0
 IDS = 16
 
@@ -55,19 +56,27 @@
 
 
 def pack_kernel(
-    me_ref, one_ref, two_ref, a_ref, b_ref, inv_a_ref, inv_b_ref, slots_ref, first_ref, second_ref
+    me_ref, one_ref, two_ref, a_ref, b_ref, inv_a_ref, inv_b_ref, slots_ref, *out_refs
 ):
     width, pairs = a_ref.shape[0], slots_ref.shape[1]
+    unit_b = (b_ref[...].astype(f32) * inv_b_ref[1:2, :]).astype(bf16)
     unit_a = (a_ref[...].astype(f32) * inv_a_ref[0:1, :]).astype(bf16)
-    first_ref[0, :, :BS] = (b_ref[...].astype(f32) * inv_b_ref[1:2, :]).astype(bf16)
-    first_ref[0, :, BS:] = unit_a[:, :UPPER]
-    second_ref[0, :width, :] = unit_a[:, UPPER:]
-    second_ref[0, width:, :] = jnp.zeros((IDS, LANES), bf16)
-    second_ref[0, width : width + 2, :pairs] = slots_ref[...].astype(f32).astype(bf16)
+    out_refs[0][0] = unit_b[:, :HALF]
+    out_refs[1][0] = unit_b[:, HALF:]
+    at = 0
+    for ref in out_refs[2:]:
+        lanes = ref.shape[2]
+        ref[0, :width, :] = unit_a[:, at : at + lanes]
+        at += lanes
+    last = out_refs[-1]
+    last[0, width:, :] = jnp.zeros((IDS, LANES), bf16)
+    last[0, width : width + 2, :pairs] = slots_ref[...].astype(f32).astype(bf16)
 
 
 def pack(me, one, two, a, b, inverse, slots):
     width, owners = a.shape[0], one.shape[0]
+    blocks = [(1, width, HALF)] * 2 + [(1, width, n * LANES) for n in CHUNKS]
+    blocks[-1] = (1, width + IDS, CHUNKS[-1] * LANES)
     spec = pltpu.PrefetchScalarGridSpec(
         num_scalar_prefetch=3,
         grid=(owners,),
@@ -78,48 +87,42 @@
             pl.BlockSpec((2, BS), lambda o, me, r1, r2: (0, r2[me[0], o])),
             pl.BlockSpec(slots.shape, lambda o, me, r1, r2: (0, 0)),
         ],
-        out_specs=[
-            pl.BlockSpec((1, width, BS + UPPER), lambda o, me, r1, r2: (o, 0, 0)),
-            pl.BlockSpec((1, width + IDS, LANES), lambda o, me, r1, r2: (o, 0, 0)),
-        ],
-    )
-    shape = [
-        jax.ShapeDtypeStruct((owners, width, BS + UPPER), bf16),
-        jax.ShapeDtypeStruct((owners, width + IDS, LANES), bf16),
-    ]
+        out_specs=[pl.BlockSpec(x, lambda o, me, r1, r2: (o, 0, 0)) for x in blocks],
+    )
+    shape = [jax.ShapeDtypeStruct((owners, *x[1:]), bf16) for x in blocks]
     size = owners * width * 2 * BS
     args = (me, one, two, a, b, inverse, inverse, slots)
     return call(pack_kernel, shape, spec, 2 * size, 4 * size, args)
 
 
-def cosine_kernel(core_ref, slots_ref, *refs):
-    out_ref, b_ref, tiles = refs[-1], refs[-2], refs[:-2]
-    for t, a_ref in enumerate(tiles):
-        partial = lax.dot_general(
-            a_ref[0], b_ref[0], (((0,), (0,)), ((), ())), preferred_element_type=f32
-        )
-        fixed = jnp.floor(partial * FIXED + 0.5).astype(i32).astype(i16)
-        out_ref[0, t * LANES : (t + 1) * LANES, :] = fixed
-
-
-def cosines(core, slots, a, tiles, b, width):
-    pairs = slots.shape[1] // 2
-
-    def tile(t):
-        return pl.BlockSpec((1, width, LANES), lambda q, c, s: (s[0, c[0] * pairs + q], 0, t))
-
-    rows = LANES * len(tiles)
-    spec = pltpu.PrefetchScalarGridSpec(
-        num_scalar_prefetch=2,
-        grid=(pairs,),
-        in_specs=[tile(t) for t in tiles]
-        + [pl.BlockSpec((1, width, BS), lambda q, c, s: (s[1, c[0] * pairs + q], 0, 0))],
-        out_specs=pl.BlockSpec((1, rows, BS), lambda q, c, s: (q, 0, 0)),
-    )
-    shape = jax.ShapeDtypeStruct((pairs, rows, BS), i16)
-    flops = 2 * pairs * rows * BS * width
-    moved = pairs * (width * (rows + BS) + rows * BS) * 2
-    return call(cosine_kernel, shape, spec, flops, moved, (core, slots, *([a] * len(tiles)), b))
+def cosine_kernel(core_ref, slots_ref, a_ref, low_ref, high_ref, out_ref):
+    pairs, width = out_ref.shape[0], low_ref.shape[1]
+
+    @pl.loop(0, pairs)
+    def _(q):
+        at = core_ref[0] * pairs + q
+        a = a_ref[slots_ref[0, at], :width, :].T
+        for i, ref in enumerate((low_ref, high_ref)):
+            partial = jnp.dot(a, ref[slots_ref[1, at]], preferred_element_type=f32)
+            fixed = jnp.floor(partial * FIXED + 0.5).astype(i32).astype(i16)
+            out_ref[q, :, i * HALF : (i + 1) * HALF] = fixed
+
+
+def cosines(core, slots, a, low, high):
+    pairs, rows = slots.shape[1] // 2, a.shape[2]
+    scalars = pl.BlockSpec(memory_space=pltpu.SMEM)
+    vectors = pl.BlockSpec(memory_space=pltpu.VMEM)
+    flops = 2 * pairs * rows * BS * low.shape[1]
+    return pl.pallas_call(
+        cosine_kernel,
+        out_shape=jax.ShapeDtypeStruct((pairs, rows, BS), i16),
+        in_specs=[scalars, scalars, vectors, vectors, vectors],
+        out_specs=vectors,
+        compiler_params=pltpu.CompilerParams(vmem_limit_bytes=24 * 2**20),
+        cost_estimate=pl.CostEstimate(
+            flops=flops, bytes_accessed=2 * a.size + 4 * low.size, transcendentals=0
+        ),
+    )(core, slots, a, low, high)
 
 
 def both_cores_kernel(x_ref, *refs):
@@ -204,8 +207,8 @@
     return rows
 
 
-def start_kernel(first_ref, second_ref, out_ref):
-    emit_rows(times_rows((first_ref, second_ref), None), out_ref)
+def start_kernel(*refs):
+    emit_rows(times_rows(refs[:-1], None), refs[-1])
 
 
 def totals_of(hot, got_ref):
@@ -213,10 +216,10 @@
     return jnp.dot(hot, got, preferred_element_type=f32)
 
 
-def step_kernel(got_ref, hot_ref, first_ref, second_ref, out_ref):
+def step_kernel(got_ref, hot_ref, *refs):
     scale = 1.0 / (1.0 + totals_of(hot_ref[...], got_ref))
     padded = jnp.concatenate([scale, jnp.zeros((LANES - scale.shape[0], LANES), f32)], axis=0)
-    emit_rows(times_rows((first_ref, second_ref), padded), out_ref)
+    emit_rows(times_rows(refs[:-1], padded), refs[-1])
 
 
 def log_kernel(row_got_ref, row_hot_ref, col_got_ref, col_hot_ref, row_log_ref, col_log_ref):
@@ -238,7 +241,7 @@
 def step(got, hot, mats, devices):
     rows = 2 * TILES * mats[0].shape[0]
     out = jax.ShapeDtypeStruct((devices, rows, LANES), bf16)
-    flops = 4 * mats[0].size
+    flops = 8 * mats[0].size
     if got is None:
         return on_chip(start_kernel, out, flops, tuple(mats))
     return on_chip(step_kernel, out, flops, (got, hot, *mats))
@@ -284,16 +287,18 @@
 
     slots = candidate_pair_slots[0].T
     pairs = slots.shape[1]
-    first, second = pack(at_column, route_one, route_two, one_t, two_t, inverse, slots)
-    first, second = tied((first, second))
-    first = lax.all_to_all(first, BA, 0, 0, tiled=True)
-    first, second = tied((first, second))
+    sent = pack(at_column, route_one, route_two, one_t, two_t, inverse, slots)
+    sent = tied(tuple(sent))
     swap = [(0, 1), (1, 0)]
-
-    def by_chip(a, tiles):
-        other = cosines(at_other, slots, a, tiles, first, width)
+    low, high = None, None
+
+    def gathered(x):
+        return lax.all_to_all(x, BA, 0, 0, tiled=True)
+
+    def by_chip(a):
+        other = cosines(at_other, slots, a, low, high)
         other = lax.ppermute(other, "aa_1", swap)
-        own = cosines(at_core, slots, a, tiles, first, width)
+        own = cosines(at_core, slots, a, low, high)
         return both_cores(at_chip, own, other)
 
     def to_chips(parts):
@@ -302,14 +307,18 @@
             for d in range(1, 4)
         ]
 
-    parts = by_chip(first, (4, 5, 6))
-    parts, second = tied((parts, second))
-    upper = to_chips(parts)
-    second = lax.all_to_all(second, BA, 0, 0, tiled=True)
-    parts, second = tied((by_chip(second, (0,)), second))
-    lower = to_chips(parts)
-    k_upper, t_upper = affinity(upper)
-    k_lower, t_lower = affinity(lower)
+    low, sent = tied((gathered(sent[0]), sent[1:]))
+    high, sent = tied((gathered(sent[0]), sent[1:]))
+    spread = []
+    for _ in range(len(CHUNKS)):
+        a = gathered(sent[0])
+        a, sent = tied((a, sent[1:]))
+        parts = by_chip(a)
+        parts, a, sent = tied((parts, a, sent))
+        spread.append(to_chips(parts))
+    second = a
+    met = [affinity(parts) for parts in spread[:-1]]
+    met.append(affinity(spread[-1]))
 
     def masks():
         every = second[:, width : width + 2, :pairs].astype(i32)
@@ -340,8 +349,8 @@
 
     hot = masks()
 
-    mats, hot = tied(((k_upper, k_lower, t_upper, t_lower), hot))
-    by_row, by_col = mats[2:], mats[:2]
+    met, hot = tied((met, hot))
+    by_row, by_col = [m[1] for m in met], [m[0] for m in met]
     got = exchanged(step(None, None, by_row, devices))
     for _ in range(SWEEPS - 1):
         got = exchanged(step(got, hot[0], by_col, devices))

time: 540 us -> 542 us (level)
  blocking collectives: 357 us -> 384 us
  local copies, waits for them, and re-layouts: 50.6 us -> 36.2 us
  waiting for transfers between devices: 62.3 us -> 54.1 us
    pallas_call x10 -> x8, Pallas kernels: 45.9 us -> 19 us  [call(): pl.pallas_call(kernel, out_shape=out_shape, grid_spec=grid_spec, compiler...]
    pallas_call x0 -> x6, Pallas kernels: none -> 26.5 us  [cosines(): pl.pallas_call(cosine_kernel, out_shape=jax.ShapeDtypeStruct((pairs, rows...]
    all_to_all x2 -> x5, blocking collectives: 181 us -> 207 us  [gathered(): return lax.all_to_all(x, BA, 0, 0, tiled=True)]
    ppermute x6 -> x9, waiting for transfers between devices: 61.9 us -> 53.4 us  [to_chips(): lax.ppermute(parts[d], 'aa_0', [(x, (x + d) % 4) for x in range(4)])]
    unnamed x38 -> x58, local copies, waits for them, and re-layouts: 17.1 us -> 21.5 us
  transfers between devices with their start and end apart: 8 -> 12, of which waited for: 4 -> 6; matrix products, arithmetic and copies ran while one was open for 1% -> 1% of each run, Pallas kernels for 3% -> 3%
where the time goes in v4:
time: 542 us; the launch traced here: 540 us
  blocking collectives  384 us (71%)
  waiting for transfers between devices  54.1 us (10%)
  Pallas kernels  52.3 us (10%)
  local copies, waits for them, and re-layouts  36.2 us (7%)
  starting transfers between devices  8.32 us (2%)
    all_to_all x5, blocking collectives, gathered(): return lax.all_to_all(x, BA, 0, 0, tiled=True)  207 us
    all_to_all x8, blocking collectives, exchanged(): return lax.all_to_all(x, ALL, 0, 0, tiled=True)  165 us
    ppermute x9, waiting for transfers between devices, to_chips(): lax.ppermute(parts[d], 'aa_0', [(x, (x + d) % 4) for x in range(4)])  53.4 us
    pallas_call x6, Pallas kernels, cosines(): pl.pallas_call(cosine_kernel, out_shape=jax.ShapeDtypeStruct((pairs, rows...  26.5 us
    unnamed x58, local copies, waits for them, and re-layouts  21.5 us
    pallas_call x8, Pallas kernels, call(): pl.pallas_call(kernel, out_shape=out_shape, grid_spec=grid_spec, compiler...  19 us
    all_to_all x1, blocking collectives, per_device(): sums = lax.all_to_all(sums, AA, 0, 0, tiled=True).sum(axis=0)  11.9 us
  transfers between devices with their start and end apart: 12, of which 6 were waited for; matrix products, arithmetic and copies ran while one was open for 1% of the time, Pallas kernels for 3%

profile of v4, /device:TPU:0, one launch (start us, length us, event | category | flops | bytes accessed | tf_op | source)
XLA Modules:
  0.0 539.7 jit_solution(12273883483990783389)
XLA Ops:
  0.7 6.4 %shard_map.68 = f32[8,2,4096]{2,1,0:T(2,128)} custom-call(bf16[448,4096]{1,0:T(8,128)(2,1)} %bitcast.32, bf16[448,4096]{1,0:T(8,128)(2,1)} %bitcast.34), custom_call_target="tpu_custom_call" | custom-call | flops 7340032 | bytes 14680064 | tf_op jit(solution)/shard_map/pallas_call | solution.py:29
  7.0 11.9 %all_to_all.70 = f32[8,2,4096]{2,1,0:T(2,128)S(1)} all-to-all(f32[8,2,4096]{2,1,0:T(2,128)} %shard_map.68), channel_id=1, replica_groups=mesh['aa_0'=4,'aa_1'=2,'ba_0'=4,'ba_1'=4] {'aa_0','aa_1'}, dimensions={0} | all-to-all | bytes 524288 | tf_op jit(solution)/shard_map/all_to_all | solution.py:285
  23.2 5.0 shard_map.69
  28.1 52.8 %all_to_all.71.low_ref = bf16[16,448,256]{2,1,0:T(8,128)(2,1)S(1)} all-to-all(bf16[16,448,256]{2,1,0:T(8,128)(2,1)S(1)} %get-tuple-element.78), channel_id=1, replica_groups=mesh['aa_0'=4,'aa_1'=2,'ba_0'=4,'ba_1'=4] {'ba_0','ba_1'}, dimensions={0} | all-to-all | bytes 7340032 | tf_op jit(solution)/shard_map/all_to_all | solution.py:296
  80.9 48.0 %all_to_all.72.high_ref = bf16[16,448,256]{2,1,0:T(8,128)(2,1)S(1)} all-to-all(bf16[16,448,256]{2,1,0:T(8,128)(2,1)S(1)} %get-tuple-element.83), channel_id=1, replica_groups=mesh['aa_0'=4,'aa_1'=2,'ba_0'=4,'ba_1'=4] {'ba_0','ba_1'}, dimensions={0} | all-to-all | bytes 7340032 | tf_op jit(solution)/shard_map/all_to_all | solution.py:296
  128.9 46.7 %all_to_all.73.a_ref = bf16[16,448,256]{2,1,0:T(8,128)(2,1)S(1)} all-to-all(bf16[16,448,256]{2,1,0:T(8,128)(2,1)S(1)} %get-tuple-element.87), channel_id=1, replica_groups=mesh['aa_0'=4,'aa_1'=2,'ba_0'=4,'ba_1'=4] {'ba_0','ba_1'}, dimensions={0} | all-to-all | bytes 7340032 | tf_op jit(solution)/shard_map/all_to_all | solution.py:296
  175.6 4.9 shard_map.71
  180.6 4.9 shard_map.70.refs_0_.refs_1_.refs_2_.refs_3_
  188.9 29.5 %all_to_all.74.a_ref = bf16[16,448,128]{2,1,0:T(8,128)(2,1)S(1)} all-to-all(bf16[16,448,128]{2,1,0:T(8,128)(2,1)S(1)} %get-tuple-element.106), channel_id=1, replica_groups=mesh['aa_0'=4,'aa_1'=2,'ba_0'=4,'ba_1'=4] {'ba_0','ba_1'}, dimensions={0} | all-to-all | bytes 3670016 | tf_op jit(solution)/shard_map/all_to_all | solution.py:296
  218.4 3.9 shard_map.75
  227.9 29.9 %all_to_all.75.a_ref = bf16[16,464,128]{2,1,0:T(8,128)(2,1)S(1)} all-to-all(bf16[16,464,128]{2,1,0:T(8,128)(2,1)S(1)} %get-tuple-element.120), channel_id=1, replica_groups=mesh['aa_0'=4,'aa_1'=2,'ba_0'=4,'ba_1'=4] {'ba_0','ba_1'}, dimensions={0} | all-to-all | bytes 3801088 | tf_op jit(solution)/shard_map/all_to_all | solution.py:296
  257.8 5.0 shard_map.79
  267.5 33.8 %collective-permute-done.1.b_ref = s16[3,256,512]{2,1,0:T(8,128)(2,1)S(1)} collective-permute-done((s16[3,256,512]{2,1,0:T(8,128)(2,1)S(1)}, s16[3,256,512]{2,1,0:T(8,128)(2,1)S(1)}, u32[]{:S(2)}, u32[]{:S(2)}) %collective-permute-start.1) | collective-permute-done | bytes 786464 | tf_op jit(solution)/shard_map/ppermute | solution.py:306
  326.3 3.9 shard_map.78.refs_0_.refs_1_.refs_2_.refs_3_
  351.6 8.4 %collective-permute-done.10.c_ref = s16[3,128,512]{2,1,0:T(8,128)(2,1)S(1)} collective-permute-done((s16[3,128,512]{2,1,0:T(8,128)(2,1)}, s16[3,128,512]{2,1,0:T(8,128)(2,1)S(1)}, u32[]{:S(2)}, u32[]{:S(2)}) %collective-permute-start.10) | collective-permute-done | bytes 393248 | tf_op jit(solution)/shard_map/ppermute | solution.py:306
  360.0 7.4 %collective-permute-done.11.d_ref = s16[3,128,512]{2,1,0:T(8,128)(2,1)S(1)} collective-permute-done((s16[3,128,512]{2,1,0:T(8,128)(2,1)}, s16[3,128,512]{2,1,0:T(8,128)(2,1)S(1)}, u32[]{:S(2)}, u32[]{:S(2)}) %collective-permute-start.11) | collective-permute-done | bytes 393248 | tf_op jit(solution)/shard_map/ppermute | solution.py:306
  368.3 21.8 %all_to_all.76.got_ref = bf16[128,24,128]{2,1,0:T(8,128)(2,1)S(1)} all-to-all(bf16[128,24,128]{2,1,0:T(8,128)(2,1)S(1)} %shard_map.82), channel_id=1, replica_groups=mesh['aa_0'=4,'aa_1'=2,'ba_0'=4,'ba_1'=4] {'aa_0','aa_1','ba_0','ba_1'}, dimensions={0} | all-to-all | bytes 1572864 | tf_op jit(solution)/shard_map/all_to_all | solution.py:251
  390.8 20.4 %all_to_all.77.got_ref = bf16[128,24,128]{2,1,0:T(8,128)(2,1)S(1)} all-to-all(bf16[128,24,128]{2,1,0:T(8,128)(2,1)S(1)} %shard_map.83), channel_id=1, replica_groups=mesh['aa_0'=4,'aa_1'=2,'ba_0'=4,'ba_1'=4] {'aa_0','aa_1','ba_0','ba_1'}, dimensions={0} | all-to-all | bytes 1572864 | tf_op jit(solution)/shard_map/all_to_all | solution.py:251
  412.1 20.4 %all_to_all.78.got_ref = bf16[128,24,128]{2,1,0:T(8,128)(2,1)S(1)} all-to-all(bf16[128,24,128]{2,1,0:T(8,128)(2,1)S(1)} %shard_map.84), channel_id=1, replica_groups=mesh['aa_0'=4,'aa_1'=2,'ba_0'=4,'ba_1'=4] {'aa_0','aa_1','ba_0','ba_1'}, dimensions={0} | all-to-all | bytes 1572864 | tf_op jit(solution)/shard_map/all_to_all | solution.py:251
  433.3 20.4 %all_to_all.79.got_ref = bf16[128,24,128]{2,1,0:T(8,128)(2,1)S(1)} all-to-all(bf16[128,24,128]{2,1,0:T(8,128)(2,1)S(1)} %shard_map.85), channel_id=1, replica_groups=mesh['aa_0'=4,'aa_1'=2,'ba_0'=4,'ba_1'=4] {'aa_0','aa_1','ba_0','ba_1'}, dimensions={0} | all-to-all | bytes 1572864 | tf_op jit(solution)/shard_map/all_to_all | solution.py:251
  454.6 20.4 %all_to_all.80.got_ref = bf16[128,24,128]{2,1,0:T(8,128)(2,1)S(1)} all-to-all(bf16[128,24,128]{2,1,0:T(8,128)(2,1)S(1)} %shard_map.86), channel_id=1, replica_groups=mesh['aa_0'=4,'aa_1'=2,'ba_0'=4,'ba_1'=4] {'aa_0','aa_1','ba_0','ba_1'}, dimensions={0} | all-to-all | bytes 1572864 | tf_op jit(solution)/shard_map/all_to_all | solution.py:251
  475.8 20.4 %all_to_all.81.got_ref = bf16[128,24,128]{2,1,0:T(8,128)(2,1)S(1)} all-to-all(bf16[128,24,128]{2,1,0:T(8,128)(2,1)S(1)} %shard_map.87), channel_id=1, replica_groups=mesh['aa_0'=4,'aa_1'=2,'ba_0'=4,'ba_1'=4] {'aa_0','aa_1','ba_0','ba_1'}, dimensions={0} | all-to-all | bytes 1572864 | tf_op jit(solution)/shard_map/all_to_all | solution.py:251
  497.1 20.4 %all_to_all.82.got_ref.row_got_ref = bf16[128,24,128]{2,1,0:T(8,128)(2,1)S(1)} all-to-all(bf16[128,24,128]{2,1,0:T(8,128)(2,1)S(1)} %shard_map.88), channel_id=1, replica_groups=mesh['aa_0'=4,'aa_1'=2,'ba_0'=4,'ba_1'=4] {'aa_0','aa_1','ba_0','ba_1'}, dimensions={0} | all-to-all | bytes 1572864 | tf_op jit(solution)/shard_map/all_to_all | solution.py:251
  518.3 20.4 %all_to_all.83.col_got_ref = bf16[128,24,128]{2,1,0:T(8,128)(2,1)S(1)} all-to-all(bf16[128,24,128]{2,1,0:T(8,128)(2,1)S(1)} %shard_map.89), channel_id=1, replica_groups=mesh['aa_0'=4,'aa_1'=2,'ba_0'=4,'ba_1'=4] {'aa_0','aa_1','ba_0','ba_1'}, dimensions={0} | all-to-all | bytes 1572864 | tf_op jit(solution)/shard_map/all_to_all | solution.py:251
  (142 shorter events, 71.5 us)
Async XLA Ops:
  0.6 18.4 %copy-start.22 = (s32[1,24,2]{1,2,0:T(2,128)S(1)}, s32[1,24,2]{1,2,0:T(2,128)}, u32[]{:S(2)}) copy-start(s32[1,24,2]{1,2,0:T(2,128)} %param.9) | copy-start | bytes 580
  0.7 18.4 %copy-start.23 = (s32[16,16]{1,0:T(8,128)S(1)}, s32[16,16]{1,0:T(8,128)}, u32[]{:S(2)}) copy-start(s32[16,16]{1,0:T(8,128)} %one_ref.1) | copy-start | bytes 3076
  0.7 18.4 %copy-start.24 = (s32[16,16]{1,0:T(8,128)S(1)}, s32[16,16]{1,0:T(8,128)}, u32[]{:S(2)}) copy-start(s32[16,16]{1,0:T(8,128)} %two_ref.1) | copy-start | bytes 3076
  19.1 2.0 copy-start.8
  80.9 176.9 %copy-start = (bf16[16,448,256]{2,1,0:T(8,128)(2,1)}, bf16[16,448,256]{2,1,0:T(8,128)(2,1)S(1)}, u32[]{:S(2)}) copy-start(bf16[16,448,256]{2,1,0:T(8,128)(2,1)S(1)} %all_to_all.71.low_ref) | copy-start | bytes 11010052
  128.9 128.9 %copy-start.2 = (bf16[16,448,256]{2,1,0:T(8,128)(2,1)}, bf16[16,448,256]{2,1,0:T(8,128)(2,1)S(1)}, u32[]{:S(2)}) copy-start(bf16[16,448,256]{2,1,0:T(8,128)(2,1)S(1)} %all_to_all.72.high_ref) | copy-start | bytes 11010052
  180.5 5.7 %collective-permute-start = (s16[12,256,512]{2,1,0:T(8,128)(2,1)S(1)}, s16[12,256,512]{2,1,0:T(8,128)(2,1)S(1)}, u32[]{:S(2)}, u32[]{:S(2)}) collective-permute-start(s16[12,256,512]{2,1,0:T(8,128)(2,1)S(1)} %shard_map.71), channel_id=1, source_target_pairs={{0,16},{16,0},{1,17},{17,1},{2,18},{18,2},{3,19},{19,3},{4,20},{20... | collective-permute-start | bytes 9437192 | tf_op jit(solution)/shard_map/ppermute | solution.py:300
  222.2 4.0 collective-permute-start.4
  257.8 5.1 copy-start.6
  262.8 67.4 %collective-permute-start.8 = (s16[12,128,512]{2,1,0:T(8,128)(2,1)}, s16[12,128,512]{2,1,0:T(8,128)(2,1)S(1)}, u32[]{:S(2)}, u32[]{:S(2)}) collective-permute-start(s16[12,128,512]{2,1,0:T(8,128)(2,1)} %shard_map.79), channel_id=1, source_target_pairs={{0,16},{16,0},{1,17},{17,1},{2,18},{18,2},{3,19},{19,3},{4,20},{20... | collective-permute-start | bytes 4718600 | tf_op jit(solution)/shard_map/ppermute | solution.py:300
  262.8 38.5 %collective-permute-start.1 = (s16[3,256,512]{2,1,0:T(8,128)(2,1)S(1)}, s16[3,256,512]{2,1,0:T(8,128)(2,1)S(1)}, u32[]{:S(2)}, u32[]{:S(2)}) collective-permute-start(s16[3,256,512]{2,1,0:T(8,128)(2,1)S(1)} %get-tuple-element.101), channel_id=1, source_target_pairs={{0,32},{32,64},{64,96},{96,0},{1,33},{33,65},{65,97},{97,1},{2,34}... | collective-permute-start | bytes 2359304 | tf_op jit(solution)/shard_map/ppermute | solution.py:306
  263.4 38.9 %collective-permute-start.2 = (s16[3,256,512]{2,1,0:T(8,128)(2,1)S(1)}, s16[3,256,512]{2,1,0:T(8,128)(2,1)S(1)}, u32[]{:S(2)}, u32[]{:S(2)}) collective-permute-start(s16[3,256,512]{2,1,0:T(8,128)(2,1)S(1)} %get-tuple-element.102), channel_id=1, source_target_pairs={{0,64},{32,96},{64,0},{96,32},{1,65},{33,97},{65,1},{97,33},{2,66}... | collective-permute-start | bytes 2359304 | tf_op jit(solution)/shard_map/ppermute | solution.py:306
  265.5 41.4 %collective-permute-start.3 = (s16[3,256,512]{2,1,0:T(8,128)(2,1)}, s16[3,256,512]{2,1,0:T(8,128)(2,1)S(1)}, u32[]{:S(2)}, u32[]{:S(2)}) collective-permute-start(s16[3,256,512]{2,1,0:T(8,128)(2,1)} %get-tuple-element.103), channel_id=1, source_target_pairs={{0,96},{32,0},{64,32},{96,64},{1,97},{33,1},{65,33},{97,65},{2,98}... | collective-permute-start | bytes 2359304 | tf_op jit(solution)/shard_map/ppermute | solution.py:306
  266.8 51.0 %collective-permute-start.5 = (s16[3,128,512]{2,1,0:T(8,128)(2,1)}, s16[3,128,512]{2,1,0:T(8,128)(2,1)}, u32[]{:S(2)}, u32[]{:S(2)}) collective-permute-start(s16[3,128,512]{2,1,0:T(8,128)(2,1)} %get-tuple-element.115), channel_id=1, source_target_pairs={{0,32},{32,64},{64,96},{96,0},{1,33},{33,65},{65,97},{97,1},{2,34}... | collective-permute-start | bytes 1179656 | tf_op jit(solution)/shard_map/ppermute | solution.py:306
  302.3 15.5 %collective-permute-start.6 = (s16[3,128,512]{2,1,0:T(8,128)(2,1)}, s16[3,128,512]{2,1,0:T(8,128)(2,1)}, u32[]{:S(2)}, u32[]{:S(2)}) collective-permute-start(s16[3,128,512]{2,1,0:T(8,128)(2,1)} %get-tuple-element.116), channel_id=1, source_target_pairs={{0,64},{32,96},{64,0},{96,32},{1,65},{33,97},{65,1},{97,33},{2,66}... | collective-permute-start | bytes 1179656 | tf_op jit(solution)/shard_map/ppermute | solution.py:306
  303.2 15.3 %collective-permute-start.7 = (s16[3,128,512]{2,1,0:T(8,128)(2,1)}, s16[3,128,512]{2,1,0:T(8,128)(2,1)}, u32[]{:S(2)}, u32[]{:S(2)}) collective-permute-start(s16[3,128,512]{2,1,0:T(8,128)(2,1)} %get-tuple-element.117), channel_id=1, source_target_pairs={{0,96},{32,0},{64,32},{96,64},{1,97},{33,1},{65,33},{97,65},{2,98}... | collective-permute-start | bytes 1179656 | tf_op jit(solution)/shard_map/ppermute | solution.py:306
  306.9 15.9 %copy-start.1 = (bf16[16,448,256]{2,1,0:T(8,128)(2,1)S(1)}, bf16[16,448,256]{2,1,0:T(8,128)(2,1)}, u32[]{:S(2)}) copy-start(bf16[16,448,256]{2,1,0:T(8,128)(2,1)} %copy-done) | copy-start | bytes 11010052
  330.2 2.8 copy-start.28
  337.3 30.7 %copy-start.5 = (f32[3,512,256]{2,1,0:T(8,128)S(1)}, f32[3,512,256]{2,1,0:T(8,128)}, u32[]{:S(2)}) copy-start(f32[3,512,256]{2,1,0:T(8,128)} %copy-done.4) | copy-start | bytes 4718596
  346.3 21.7 %copy-start.13 = (f32[3,512,128]{2,1,0:T(8,128)S(1)}, f32[3,512,128]{2,1,0:T(8,128)}, u32[]{:S(2)}) copy-start(f32[3,512,128]{2,1,0:T(8,128)} %copy-done.12) | copy-start | bytes 2359300
  346.3 13.7 %collective-permute-start.10 = (s16[3,128,512]{2,1,0:T(8,128)(2,1)}, s16[3,128,512]{2,1,0:T(8,128)(2,1)S(1)}, u32[]{:S(2)}, u32[]{:S(2)}) collective-permute-start(s16[3,128,512]{2,1,0:T(8,128)(2,1)} %copy-done.27), channel_id=1, source_target_pairs={{0,64},{32,96},{64,0},{96,32},{1,65},{33,97},{65,1},{97,33},{2,66}... | collective-permute-start | bytes 1179656 | tf_op jit(solution)/shard_map/ppermute | solution.py:306
  347.6 19.8 %collective-permute-start.11 = (s16[3,128,512]{2,1,0:T(8,128)(2,1)}, s16[3,128,512]{2,1,0:T(8,128)(2,1)S(1)}, u32[]{:S(2)}, u32[]{:S(2)}) collective-permute-start(s16[3,128,512]{2,1,0:T(8,128)(2,1)} %copy-done.26), channel_id=1, source_target_pairs={{0,96},{32,0},{64,32},{96,64},{1,97},{33,1},{65,33},{97,65},{2,98}... | collective-permute-start | bytes 1179656 | tf_op jit(solution)/shard_map/ppermute | solution.py:306
  349.6 17.8 %collective-permute-start.9 = (s16[3,128,512]{2,1,0:T(8,128)(2,1)}, s16[3,128,512]{2,1,0:T(8,128)(2,1)S(1)}, u32[]{:S(2)}, u32[]{:S(2)}) collective-permute-start(s16[3,128,512]{2,1,0:T(8,128)(2,1)} %copy-done.25), channel_id=1, source_target_pairs={{0,32},{32,64},{64,96},{96,0},{1,33},{33,65},{65,97},{97,1},{2,34}... | collective-permute-start | bytes 1179656 | tf_op jit(solution)/shard_map/ppermute | solution.py:306
  368.0 22.0 %copy-start.11 = (f32[3,128,512]{2,1,0:T(8,128)S(1)}, f32[3,128,512]{2,1,0:T(8,128)}, u32[]{:S(2)}) copy-start(f32[3,128,512]{2,1,0:T(8,128)} %copy-done.10) | copy-start | bytes 2359300
  (17 other events, 19.5 us)

commit v5 on v4

--- a/solution.py
+++ b/solution.py
@@ -1,3 +1,5 @@
+import functools
+
 import jax
 import jax.numpy as jnp
 from jax import lax
@@ -14,7 +16,7 @@
 LANES = 128
 TILES = BS // LANES
 HALF = BS // 2
-CHUNKS = (2, 1, 1)
+CHUNKS = (3, 1)
 FIXED = 32000.0
 IDS = 16
 
@@ -59,15 +61,10 @@
     me_ref, one_ref, two_ref, a_ref, b_ref, inv_a_ref, inv_b_ref, slots_ref, *out_refs
 ):
     width, pairs = a_ref.shape[0], slots_ref.shape[1]
-    unit_b = (b_ref[...].astype(f32) * inv_b_ref[1:2, :]).astype(bf16)
     unit_a = (a_ref[...].astype(f32) * inv_a_ref[0:1, :]).astype(bf16)
-    out_refs[0][0] = unit_b[:, :HALF]
-    out_refs[1][0] = unit_b[:, HALF:]
-    at = 0
-    for ref in out_refs[2:]:
-        lanes = ref.shape[2]
-        ref[0, :width, :] = unit_a[:, at : at + lanes]
-        at += lanes
+    out_refs[0][0, :, :BS] = (b_ref[...].astype(f32) * inv_b_ref[1:2, :]).astype(bf16)
+    out_refs[0][0, :, BS:] = unit_a[:, : CHUNKS[0] * LANES]
+    out_refs[1][0, :width, :] = unit_a[:, CHUNKS[0] * LANES :]
     last = out_refs[-1]
     last[0, width:, :] = jnp.zeros((IDS, LANES), bf16)
     last[0, width : width + 2, :pairs] = slots_ref[...].astype(f32).astype(bf16)
@@ -75,8 +72,10 @@
 
 def pack(me, one, two, a, b, inverse, slots):
     width, owners = a.shape[0], one.shape[0]
-    blocks = [(1, width, HALF)] * 2 + [(1, width, n * LANES) for n in CHUNKS]
-    blocks[-1] = (1, width + IDS, CHUNKS[-1] * LANES)
+    blocks = [
+        (1, width, BS + CHUNKS[0] * LANES),
+        (1, width + IDS, CHUNKS[1] * LANES),
+    ]
     spec = pltpu.PrefetchScalarGridSpec(
         num_scalar_prefetch=3,
         grid=(owners,),
@@ -95,34 +94,39 @@
     return call(pack_kernel, shape, spec, 2 * size, 4 * size, args)
 
 
-def cosine_kernel(core_ref, slots_ref, a_ref, low_ref, high_ref, out_ref):
-    pairs, width = out_ref.shape[0], low_ref.shape[1]
-
-    @pl.loop(0, pairs)
-    def _(q):
-        at = core_ref[0] * pairs + q
-        a = a_ref[slots_ref[0, at], :width, :].T
-        for i, ref in enumerate((low_ref, high_ref)):
-            partial = jnp.dot(a, ref[slots_ref[1, at]], preferred_element_type=f32)
-            fixed = jnp.floor(partial * FIXED + 0.5).astype(i32).astype(i16)
-            out_ref[q, :, i * HALF : (i + 1) * HALF] = fixed
-
-
-def cosines(core, slots, a, low, high):
-    pairs, rows = slots.shape[1] // 2, a.shape[2]
+def cosine_kernel(outputs, slots_ref, *refs):
+    core_refs, out_refs, refs = refs[:outputs], refs[-outputs:], refs[outputs:-outputs]
+    pairs, rows, _ = out_refs[0].shape
+    b_ref, a_ref = refs[0], refs[-1]
+    start, spare = (BS, 0) if len(refs) == 1 else (0, IDS)
+    width = a_ref.shape[1] - spare
+
+    for core_ref, out_ref in zip(core_refs, out_refs):
+
+        @pl.loop(0, pairs)
+        def _(q):
+            at = core_ref[0] * pairs + q
+            a = a_ref[slots_ref[0, at], :width, start : start + rows].T
+            for i in range(0, BS, HALF):
+                b = b_ref[slots_ref[1, at], :, i : i + HALF]
+                partial = jnp.dot(a, b, preferred_element_type=f32)
+                fixed = jnp.floor(partial * FIXED + 0.5).astype(i32).astype(i16)
+                out_ref[q, :, i : i + HALF] = fixed
+
+
+def cosines(cores, slots, rows, *arrays):
+    pairs, width = slots.shape[1] // 2, arrays[0].shape[1]
     scalars = pl.BlockSpec(memory_space=pltpu.SMEM)
     vectors = pl.BlockSpec(memory_space=pltpu.VMEM)
-    flops = 2 * pairs * rows * BS * low.shape[1]
+    flops = 2 * pairs * rows * BS * width * len(cores)
     return pl.pallas_call(
-        cosine_kernel,
-        out_shape=jax.ShapeDtypeStruct((pairs, rows, BS), i16),
-        in_specs=[scalars, scalars, vectors, vectors, vectors],
-        out_specs=vectors,
-        compiler_params=pltpu.CompilerParams(vmem_limit_bytes=24 * 2**20),
-        cost_estimate=pl.CostEstimate(
-            flops=flops, bytes_accessed=2 * a.size + 4 * low.size, transcendentals=0
-        ),
-    )(core, slots, a, low, high)
+        functools.partial(cosine_kernel, len(cores)),
+        out_shape=[jax.ShapeDtypeStruct((pairs, rows, BS), i16)] * len(cores),
+        in_specs=[scalars] * (1 + len(cores)) + [vectors] * len(arrays),
+        out_specs=[vectors] * len(cores),
+        compiler_params=pltpu.CompilerParams(vmem_limit_bytes=8 * 2**20),
+        cost_estimate=pl.CostEstimate(flops=flops, bytes_accessed=flops // 256, transcendentals=0),
+    )(slots, *cores, *arrays)
 
 
 def both_cores_kernel(x_ref, *refs):
@@ -290,15 +294,18 @@
     sent = pack(at_column, route_one, route_two, one_t, two_t, inverse, slots)
     sent = tied(tuple(sent))
     swap = [(0, 1), (1, 0)]
-    low, high = None, None
 
     def gathered(x):
         return lax.all_to_all(x, BA, 0, 0, tiled=True)
 
-    def by_chip(a):
-        other = cosines(at_other, slots, a, low, high)
-        other = lax.ppermute(other, "aa_1", swap)
-        own = cosines(at_core, slots, a, low, high)
+    def by_chip(rows, *arrays):
+        if len(arrays) == len(CHUNKS):
+            other, own = cosines((at_other, at_core), slots, rows, *arrays)
+            other = lax.ppermute(other, "aa_1", swap)
+        else:
+            (other,) = cosines((at_other,), slots, rows, *arrays)
+            other = lax.ppermute(other, "aa_1", swap)
+            (own,) = cosines((at_core,), slots, rows, *arrays)
         return both_cores(at_chip, own, other)
 
     def to_chips(parts):
@@ -307,13 +314,12 @@
             for d in range(1, 4)
         ]
 
-    low, sent = tied((gathered(sent[0]), sent[1:]))
-    high, sent = tied((gathered(sent[0]), sent[1:]))
-    spread = []
-    for _ in range(len(CHUNKS)):
+    spread, arrived = [], []
+    for tiles in CHUNKS:
         a = gathered(sent[0])
         a, sent = tied((a, sent[1:]))
-        parts = by_chip(a)
+        arrived.append(a)
+        parts = by_chip(tiles * LANES, *arrived)
         parts, a, sent = tied((parts, a, sent))
         spread.append(to_chips(parts))
     second = a

time: 542 us -> 533 us (0.983)
  blocking collectives: 384 us -> 357 us
  local copies, waits for them, and re-layouts: 36.2 us -> 47.3 us
  waiting for transfers between devices: 54.1 us -> 64 us
  Pallas kernels: 52.3 us -> 46.1 us
    all_to_all x5 -> x2, blocking collectives: 207 us -> 181 us  [gathered(): return lax.all_to_all(x, BA, 0, 0, tiled=True)]
    ppermute x9 -> x6, waiting for transfers between devices: 53.4 us -> 61.9 us  [to_chips(): lax.ppermute(parts[d], 'aa_0', [(x, (x + d) % 4) for x in range(4)])]
    unnamed x58 -> x34, local copies, waits for them, and re-layouts: 21.5 us -> 13.6 us
    pallas_call x6 -> x3, Pallas kernels: 26.5 us -> 19.8 us  [cosines(): pl.pallas_call(functools.partial(cosine_kernel, len(cores)), out_shape=[j...]
    pallas_call x8 -> x6, Pallas kernels: 19 us -> 19.6 us  [call(): pl.pallas_call(kernel, out_shape=out_shape, grid_spec=grid_spec, compiler...]
  transfers between devices with their start and end apart: 12 -> 8, of which waited for: 6 -> 4; matrix products, arithmetic and copies ran while one was open for 1% -> 1% of each run, Pallas kernels for 3% -> 2%
where the time goes in v5:
time: 533 us; the launch traced here: 530 us
  blocking collectives  357 us (67%)
  waiting for transfers between devices  64 us (12%)
  local copies, waits for them, and re-layouts  47.3 us (9%)
  Pallas kernels  46.1 us (9%)
  other arithmetic  8.27 us (2%)
  starting transfers between devices  6.83 us (1%)
    all_to_all x2, blocking collectives, gathered(): return lax.all_to_all(x, BA, 0, 0, tiled=True)  181 us
    all_to_all x8, blocking collectives, exchanged(): return lax.all_to_all(x, ALL, 0, 0, tiled=True)  164 us
    ppermute x6, waiting for transfers between devices, to_chips(): lax.ppermute(parts[d], 'aa_0', [(x, (x + d) % 4) for x in range(4)])  61.9 us
    pallas_call x3, Pallas kernels, cosines(): pl.pallas_call(functools.partial(cosine_kernel, len(cores)), out_shape=[j...  19.8 us
    pallas_call x6, Pallas kernels, call(): pl.pallas_call(kernel, out_shape=out_shape, grid_spec=grid_spec, compiler...  19.6 us
    unnamed x34, local copies, waits for them, and re-layouts  13.6 us
    all_to_all x1, blocking collectives, per_device(): sums = lax.all_to_all(sums, AA, 0, 0, tiled=True).sum(axis=0)  11.9 us
  transfers between devices with their start and end apart: 8, of which 4 were waited for; matrix products, arithmetic and copies ran while one was open for 1% of the time, Pallas kernels for 2%

profile of v5, /device:TPU:0, one launch (start us, length us, event | category | flops | bytes accessed | tf_op | source)
XLA Modules:
  0.0 530.2 jit_solution(15382553673939447518)
XLA Ops:
  0.7 6.4 %shard_map.68 = f32[8,2,4096]{2,1,0:T(2,128)} custom-call(bf16[448,4096]{1,0:T(8,128)(2,1)} %bitcast.32, bf16[448,4096]{1,0:T(8,128)(2,1)} %bitcast.34), custom_call_target="tpu_custom_call" | custom-call | flops 7340032 | bytes 14680064 | tf_op jit(solution)/shard_map/pallas_call | solution.py:31
  7.1 11.9 %all_to_all.55 = f32[8,2,4096]{2,1,0:T(2,128)S(1)} all-to-all(f32[8,2,4096]{2,1,0:T(2,128)} %shard_map.68), channel_id=1, replica_groups=mesh['aa_0'=4,'aa_1'=2,'ba_0'=4,'ba_1'=4] {'aa_0','aa_1'}, dimensions={0} | all-to-all | bytes 524288 | tf_op jit(solution)/shard_map/all_to_all | solution.py:289
  21.2 2.0 copy-done.5
  23.2 5.0 shard_map.69
  28.2 151.1 %all_to_all.56.refs_1_.refs_2_ = bf16[16,448,896]{2,1,0:T(8,128)(2,1)S(1)} all-to-all(bf16[16,448,896]{2,1,0:T(8,128)(2,1)S(1)} %get-tuple-element.51), channel_id=1, replica_groups=mesh['aa_0'=4,'aa_1'=2,'ba_0'=4,'ba_1'=4] {'ba_0','ba_1'}, dimensions={0} | all-to-all | bytes 25690112 | tf_op jit(solution)/shard_map/all_to_all | solution.py:299
  179.3 5.9 %shard_map.71 = s16[12,384,512]{2,1,0:T(8,128)(2,1)S(1)} custom-call(s32[2,24]{1,0:T(2,128)S(1)} %bitcast.39, s32[1]{0:T(128)} %bitcast.5.refs_0_, bf16[16,448,896]{2,1,0:T(8,128)(2,1)S(1)} %all_to_all.56.refs_1_.refs_2_), custom_call_target="tpu_custom_call" | custom-call | flops 2113929216 | bytes 8257536 | tf_op jit(solution)/shard_map/pallas_call | solution.py:122
  185.2 5.9 %shard_map.70.refs_0_.refs_1_.refs_2_.refs_3_ = s16[12,384,512]{2,1,0:T(8,128)(2,1)S(1)} custom-call(s32[2,24]{1,0:T(2,128)S(1)} %bitcast.40, s32[1]{0:T(128)} %bitcast.4.refs_0_.refs_1_, bf16[16,448,896]{2,1,0:T(8,128)(2,1)S(1)} %all_to_all.56.refs_1_.refs_2_), custom_call_target="tpu_custom_call" | custom-call | flops 2113929216 | bytes 8257536 | tf_op jit(solution)/shard_map/pallas_call | solution.py:122
  193.1 2.4 shard_map.72
  195.5 29.5 %all_to_all.57.refs_3_ = bf16[16,464,128]{2,1,0:T(8,128)(2,1)S(1)} all-to-all(bf16[16,464,128]{2,1,0:T(8,128)(2,1)S(1)} %get-tuple-element.66), channel_id=1, replica_groups=mesh['aa_0'=4,'aa_1'=2,'ba_0'=4,'ba_1'=4] {'ba_0','ba_1'}, dimensions={0} | all-to-all | bytes 3801088 | tf_op jit(solution)/shard_map/all_to_all | solution.py:299
  225.0 8.1 %shard_map.74 = (s16[12,128,512]{2,1,0:T(8,128)(2,1)}, s16[12,128,512]{2,1,0:T(8,128)(2,1)S(1)}) custom-call(s32[2,24]{1,0:T(2,128)S(1)} %bitcast.41, s32[1]{0:T(128)} %bitcast.5.refs_0_, s32[1]{0:T(128)} %bitcast.4.refs_0_.refs_1_, bf16[16,448,896]{2,1,0:T(8,128)(2,1)S(1)} %all_to_all.56.refs_1_.refs_2_, bf16[16,464,128]{2,1,0:T(8,128)(2,1)S(1)} %all_to_all.57.refs_3_), custom_call_target="tpu_custom_call" | custom-call | flops 1409286144 | bytes 5505024 | tf_op jit(solution)/shard_map/pallas_call | solution.py:122
  234.9 2.1 collective-permute-start.2
  243.3 46.1 %collective-permute-done.1.b_ref = s16[3,384,512]{2,1,0:T(8,128)(2,1)S(1)} collective-permute-done((s16[3,384,512]{2,1,0:T(8,128)(2,1)}, s16[3,384,512]{2,1,0:T(8,128)(2,1)S(1)}, u32[]{:S(2)}, u32[]{:S(2)}) %collective-permute-start.1) | collective-permute-done | bytes 1179680 | tf_op jit(solution)/shard_map/ppermute | solution.py:313
  293.9 2.7 shard_map.73
  298.1 2.5 shard_map.75
  335.9 2.5 collective-permute-start.6
  341.0 15.5 %collective-permute-done.5.b_ref = s16[3,128,512]{2,1,0:T(8,128)(2,1)S(1)} collective-permute-done((s16[3,128,512]{2,1,0:T(8,128)(2,1)}, s16[3,128,512]{2,1,0:T(8,128)(2,1)S(1)}, u32[]{:S(2)}, u32[]{:S(2)}) %collective-permute-start.5) | collective-permute-done | bytes 393248 | tf_op jit(solution)/shard_map/ppermute | solution.py:313
  359.3 21.4 %all_to_all.58.got_ref = bf16[128,24,128]{2,1,0:T(8,128)(2,1)S(1)} all-to-all(bf16[128,24,128]{2,1,0:T(8,128)(2,1)S(1)} %shard_map.77), channel_id=1, replica_groups=mesh['aa_0'=4,'aa_1'=2,'ba_0'=4,'ba_1'=4] {'aa_0','aa_1','ba_0','ba_1'}, dimensions={0} | all-to-all | bytes 1572864 | tf_op jit(solution)/shard_map/all_to_all | solution.py:255
  381.5 20.4 %all_to_all.59.got_ref = bf16[128,24,128]{2,1,0:T(8,128)(2,1)S(1)} all-to-all(bf16[128,24,128]{2,1,0:T(8,128)(2,1)S(1)} %shard_map.78), channel_id=1, replica_groups=mesh['aa_0'=4,'aa_1'=2,'ba_0'=4,'ba_1'=4] {'aa_0','aa_1','ba_0','ba_1'}, dimensions={0} | all-to-all | bytes 1572864 | tf_op jit(solution)/shard_map/all_to_all | solution.py:255
  402.7 20.4 %all_to_all.60.got_ref = bf16[128,24,128]{2,1,0:T(8,128)(2,1)S(1)} all-to-all(bf16[128,24,128]{2,1,0:T(8,128)(2,1)S(1)} %shard_map.79), channel_id=1, replica_groups=mesh['aa_0'=4,'aa_1'=2,'ba_0'=4,'ba_1'=4] {'aa_0','aa_1','ba_0','ba_1'}, dimensions={0} | all-to-all | bytes 1572864 | tf_op jit(solution)/shard_map/all_to_all | solution.py:255
  424.0 20.4 %all_to_all.61.got_ref = bf16[128,24,128]{2,1,0:T(8,128)(2,1)S(1)} all-to-all(bf16[128,24,128]{2,1,0:T(8,128)(2,1)S(1)} %shard_map.80), channel_id=1, replica_groups=mesh['aa_0'=4,'aa_1'=2,'ba_0'=4,'ba_1'=4] {'aa_0','aa_1','ba_0','ba_1'}, dimensions={0} | all-to-all | bytes 1572864 | tf_op jit(solution)/shard_map/all_to_all | solution.py:255
  445.2 20.4 %all_to_all.62.got_ref = bf16[128,24,128]{2,1,0:T(8,128)(2,1)S(1)} all-to-all(bf16[128,24,128]{2,1,0:T(8,128)(2,1)S(1)} %shard_map.81), channel_id=1, replica_groups=mesh['aa_0'=4,'aa_1'=2,'ba_0'=4,'ba_1'=4] {'aa_0','aa_1','ba_0','ba_1'}, dimensions={0} | all-to-all | bytes 1572864 | tf_op jit(solution)/shard_map/all_to_all | solution.py:255
  466.4 20.4 %all_to_all.63.got_ref = bf16[128,24,128]{2,1,0:T(8,128)(2,1)S(1)} all-to-all(bf16[128,24,128]{2,1,0:T(8,128)(2,1)S(1)} %shard_map.82), channel_id=1, replica_groups=mesh['aa_0'=4,'aa_1'=2,'ba_0'=4,'ba_1'=4] {'aa_0','aa_1','ba_0','ba_1'}, dimensions={0} | all-to-all | bytes 1572864 | tf_op jit(solution)/shard_map/all_to_all | solution.py:255
  487.6 20.4 %all_to_all.64.got_ref.row_got_ref = bf16[128,24,128]{2,1,0:T(8,128)(2,1)S(1)} all-to-all(bf16[128,24,128]{2,1,0:T(8,128)(2,1)S(1)} %shard_map.83), channel_id=1, replica_groups=mesh['aa_0'=4,'aa_1'=2,'ba_0'=4,'ba_1'=4] {'aa_0','aa_1','ba_0','ba_1'}, dimensions={0} | all-to-all | bytes 1572864 | tf_op jit(solution)/shard_map/all_to_all | solution.py:255
  508.8 20.4 %all_to_all.65.col_got_ref = bf16[128,24,128]{2,1,0:T(8,128)(2,1)S(1)} all-to-all(bf16[128,24,128]{2,1,0:T(8,128)(2,1)S(1)} %shard_map.84), channel_id=1, replica_groups=mesh['aa_0'=4,'aa_1'=2,'ba_0'=4,'ba_1'=4] {'aa_0','aa_1','ba_0','ba_1'}, dimensions={0} | all-to-all | bytes 1572864 | tf_op jit(solution)/shard_map/all_to_all | solution.py:255
  (102 shorter events, 65.4 us)
Async XLA Ops:
  0.6 18.5 %copy-start.11 = (s32[16,16]{1,0:T(8,128)S(1)}, s32[16,16]{1,0:T(8,128)}, u32[]{:S(2)}) copy-start(s32[16,16]{1,0:T(8,128)} %one_ref.1) | copy-start | bytes 3076
  0.6 18.5 %copy-start.12 = (s32[16,16]{1,0:T(8,128)S(1)}, s32[16,16]{1,0:T(8,128)}, u32[]{:S(2)}) copy-start(s32[16,16]{1,0:T(8,128)} %two_ref.1) | copy-start | bytes 3076
  0.7 18.5 %copy-start.13 = (s32[1,24,2]{1,2,0:T(2,128)S(1)}, s32[1,24,2]{1,2,0:T(2,128)}, u32[]{:S(2)}) copy-start(s32[1,24,2]{1,2,0:T(2,128)} %param.9) | copy-start | bytes 580
  19.1 2.0 copy-start.4
  21.2 2.0 copy-start.5
  185.1 8.0 %collective-permute-start = (s16[12,384,512]{2,1,0:T(8,128)(2,1)S(1)}, s16[12,384,512]{2,1,0:T(8,128)(2,1)S(1)}, u32[]{:S(2)}, u32[]{:S(2)}) collective-permute-start(s16[12,384,512]{2,1,0:T(8,128)(2,1)S(1)} %shard_map.71), channel_id=1, source_target_pairs={{0,16},{16,0},{1,17},{17,1},{2,18},{18,2},{3,19},{19,3},{4,20},{20... | collective-permute-start | bytes 14155784 | tf_op jit(solution)/shard_map/ppermute | solution.py:307
  225.0 8.1 %copy-start.6 = (bf16[16,464,128]{2,1,0:T(8,128)(2,1)}, bf16[16,464,128]{2,1,0:T(8,128)(2,1)S(1)}, u32[]{:S(2)}) copy-start(bf16[16,464,128]{2,1,0:T(8,128)(2,1)S(1)} %all_to_all.57.refs_3_) | copy-start | bytes 5701636
  233.1 1.2 copy-start.2
  234.3 63.8 %collective-permute-start.4 = (s16[12,128,512]{2,1,0:T(8,128)(2,1)}, s16[12,128,512]{2,1,0:T(8,128)(2,1)}, u32[]{:S(2)}, u32[]{:S(2)}) collective-permute-start(s16[12,128,512]{2,1,0:T(8,128)(2,1)} %get-tuple-element.68), channel_id=1, source_target_pairs={{0,16},{16,0},{1,17},{17,1},{2,18},{18,2},{3,19},{19,3},{4,20},{20... | collective-permute-start | bytes 4718600 | tf_op jit(solution)/shard_map/ppermute | solution.py:304
  234.3 55.1 %collective-permute-start.1 = (s16[3,384,512]{2,1,0:T(8,128)(2,1)}, s16[3,384,512]{2,1,0:T(8,128)(2,1)S(1)}, u32[]{:S(2)}, u32[]{:S(2)}) collective-permute-start(s16[3,384,512]{2,1,0:T(8,128)(2,1)} %get-tuple-element.61), channel_id=1, source_target_pairs={{0,32},{32,64},{64,96},{96,0},{1,33},{33,65},{65,97},{97,1},{2,34}... | collective-permute-start | bytes 3538952 | tf_op jit(solution)/shard_map/ppermute | solution.py:313
  234.9 55.5 %collective-permute-start.2 = (s16[3,384,512]{2,1,0:T(8,128)(2,1)}, s16[3,384,512]{2,1,0:T(8,128)(2,1)S(1)}, u32[]{:S(2)}, u32[]{:S(2)}) collective-permute-start(s16[3,384,512]{2,1,0:T(8,128)(2,1)} %get-tuple-element.62), channel_id=1, source_target_pairs={{0,64},{32,96},{64,0},{96,32},{1,65},{33,97},{65,1},{97,33},{2,66}... | collective-permute-start | bytes 3538952 | tf_op jit(solution)/shard_map/ppermute | solution.py:313
  236.9 54.5 %collective-permute-start.3 = (s16[3,384,512]{2,1,0:T(8,128)(2,1)}, s16[3,384,512]{2,1,0:T(8,128)(2,1)}, u32[]{:S(2)}, u32[]{:S(2)}) collective-permute-start(s16[3,384,512]{2,1,0:T(8,128)(2,1)} %get-tuple-element.63), channel_id=1, source_target_pairs={{0,96},{32,0},{64,32},{96,64},{1,97},{33,1},{65,33},{97,65},{2,98}... | collective-permute-start | bytes 3538952 | tf_op jit(solution)/shard_map/ppermute | solution.py:313
  243.3 54.8 %copy-start.3 = (s16[12,128,512]{2,1,0:T(8,128)(2,1)S(1)}, s16[12,128,512]{2,1,0:T(8,128)(2,1)}, u32[]{:S(2)}) copy-start(s16[12,128,512]{2,1,0:T(8,128)(2,1)} %copy-done.2) | copy-start | bytes 4718596
  289.4 1.0 copy-start.7
  290.4 1.0 copy-start.9
  291.4 1.3 copy-start.8
  292.7 1.3 copy-start.10
  296.7 1.4 copy-start
  298.1 4.7 copy-start.15
  323.5 9.0 %copy-start.16 = (s32[3]{0:T(128)S(1)}, s32[3]{0:T(128)}, u32[]{:S(2)}) copy-start(s32[3]{0:T(128)} %dynamic-slice_reduce_fusion.1) | copy-start | bytes 40
  335.9 20.5 %collective-permute-start.5 = (s16[3,128,512]{2,1,0:T(8,128)(2,1)}, s16[3,128,512]{2,1,0:T(8,128)(2,1)S(1)}, u32[]{:S(2)}, u32[]{:S(2)}) collective-permute-start(s16[3,128,512]{2,1,0:T(8,128)(2,1)} %copy-done.14), channel_id=1, source_target_pairs={{0,32},{32,64},{64,96},{96,0},{1,33},{33,65},{65,97},{97,1},{2,34}... | collective-permute-start | bytes 1179656 | tf_op jit(solution)/shard_map/ppermute | solution.py:313
  335.9 20.5 %collective-permute-start.6 = (s16[3,128,512]{2,1,0:T(8,128)(2,1)S(1)}, s16[3,128,512]{2,1,0:T(8,128)(2,1)S(1)}, u32[]{:S(2)}, u32[]{:S(2)}) collective-permute-start(s16[3,128,512]{2,1,0:T(8,128)(2,1)S(1)} %get-tuple-element.75), channel_id=1, source_target_pairs={{0,64},{32,96},{64,0},{96,32},{1,65},{33,97},{65,1},{97,33},{2,66}... | collective-permute-start | bytes 1179656 | tf_op jit(solution)/shard_map/ppermute | solution.py:313
  338.4 18.4 %collective-permute-start.7 = (s16[3,128,512]{2,1,0:T(8,128)(2,1)S(1)}, s16[3,128,512]{2,1,0:T(8,128)(2,1)S(1)}, u32[]{:S(2)}, u32[]{:S(2)}) collective-permute-start(s16[3,128,512]{2,1,0:T(8,128)(2,1)S(1)} %get-tuple-element.76), channel_id=1, source_target_pairs={{0,96},{32,0},{64,32},{96,64},{1,97},{33,1},{65,33},{97,65},{2,98}... | collective-permute-start | bytes 1179656 | tf_op jit(solution)/shard_map/ppermute | solution.py:313
  357.4 1.7 copy-start.1
  (1 other events, 0.7 us)

commit v6 on v5

--- a/solution.py
+++ b/solution.py
@@ -40,18 +40,24 @@
 
 
 def squares_kernel(one_ref, two_ref, sums_ref):
+    @pl.when(pl.program_id(0) == 0)
+    def _():
+        sums_ref[...] = jnp.zeros_like(sums_ref)
+
     for i, ref in enumerate((one_ref, two_ref)):
         total = jnp.sum(jnp.square(ref[...].astype(f32)), axis=0, keepdims=True)
-        sums_ref[:, i : i + 1, :] = jnp.broadcast_to(total[None], (sums_ref.shape[0], 1, BS))
+        sums_ref[:, i : i + 1, :] += jnp.broadcast_to(
+            total[None], (sums_ref.shape[0], 1, ref.shape[1])
+        )
 
 
 def squares(one, two, depth):
     width, rows = one.shape
-    block = pl.BlockSpec((width, BS), lambda k: (0, k))
+    block = pl.BlockSpec((64, rows), lambda k: (k, 0))
     spec = pl.GridSpec(
-        grid=(rows // BS,),
+        grid=(width // 64,),
         in_specs=[block, block],
-        out_specs=pl.BlockSpec((depth, 2, BS), lambda k: (0, 0, k)),
+        out_specs=pl.BlockSpec((depth, 2, rows), lambda k: (0, 0, 0)),
     )
     shape = jax.ShapeDtypeStruct((depth, 2, rows), f32)
     return call(squares_kernel, shape, spec, 4 * one.size, 8 * one.size, (one, two), 60)
@@ -184,7 +190,10 @@
 
 def emit_rows(rows, out_ref):
     high = [r.astype(bf16).astype(f32) for r in rows]
+    spare = out_ref.shape[1] - len(rows)
     low = [r - h for r, h in zip(rows, high)]
+    if spare < len(rows):
+        low = [jnp.zeros((spare, LANES), f32)]
     tile = jnp.concatenate(high + low, axis=0).astype(bf16)
     out_ref[...] = jnp.broadcast_to(tile[None], out_ref.shape)
 
@@ -242,8 +251,9 @@
     )(*args)
 
 
-def step(got, hot, mats, devices):
-    rows = 2 * TILES * mats[0].shape[0]
+def step(got, hot, mats, devices, fine=True):
+    pairs = mats[0].shape[0]
+    rows = TILES * (2 * pairs if fine else pairs + 1)
     out = jax.ShapeDtypeStruct((devices, rows, LANES), bf16)
     flops = 8 * mats[0].size
     if got is None:
@@ -255,9 +265,11 @@
     return lax.all_to_all(x, ALL, 0, 0, tiled=True)
 
 
-def hot_rows(wanted, present):
+def hot_rows(wanted, present, fine=True):
     devices, pairs = present.shape
-    shape = (devices, 2, pairs, TILES)
+    if not fine:
+        present = jnp.concatenate([present, jnp.full((devices, 1), -1, i32)], axis=1)
+    shape = (devices, 2, pairs, TILES) if fine else (devices, 1, pairs + 1, TILES)
     col_id = jnp.broadcast_to(present[:, None, :, None], shape).reshape(1, -1)
     col_tile = lax.broadcasted_iota(i32, shape, 3).reshape(1, -1)
     row_id = jnp.repeat(wanted, TILES)[:, None]
@@ -351,14 +363,18 @@
             hot_rows(my_cols, col_dev),
             hot_rows(own_blocks, row_dev),
             hot_rows(own_blocks, col_dev),
+            hot_rows(my_rows, row_dev, False),
+            hot_rows(my_cols, col_dev, False),
         ]
 
     hot = masks()
 
     met, hot = tied((met, hot))
     by_row, by_col = [m[1] for m in met], [m[0] for m in met]
-    got = exchanged(step(None, None, by_row, devices))
-    for _ in range(SWEEPS - 1):
+    got = exchanged(step(None, None, by_row, devices, False))
+    got = exchanged(step(got, hot[4], by_col, devices, False))
+    got = exchanged(step(got, hot[5], by_row, devices))
+    for _ in range(SWEEPS - 2):
         got = exchanged(step(got, hot[0], by_col, devices))
         got = exchanged(step(got, hot[1], by_row, devices))
     last = exchanged(step(got, hot[0], by_col, devices))

time: 533 us -> 531 us (level)
  local copies, waits for them, and re-layouts: 47.3 us -> 53.2 us
    eq x8 -> x11, local copies, waits for them, and re-layouts: 8.42 us -> 13.8 us  [hot_rows(): return ((row_id == col_id) & (row_tile == col_tile)).astype(bf16)]
  transfers between devices with their start and end apart: 8 -> 8, of which waited for: 4 -> 4; matrix products, arithmetic and copies ran while one was open for 1% -> 2% of each run, Pallas kernels for 2% -> 2%
where the time goes in v6:
time: 531 us; the launch traced here: 528 us
  blocking collectives  352 us (66%)
  waiting for transfers between devices  60.5 us (11%)
  local copies, waits for them, and re-layouts  53.2 us (10%)
  Pallas kernels  45.9 us (9%)
  other arithmetic  9.04 us (2%)
  starting transfers between devices  6.86 us (1%)
    all_to_all x2, blocking collectives, gathered(): return lax.all_to_all(x, BA, 0, 0, tiled=True)  181 us
    all_to_all x8, blocking collectives, exchanged(): return lax.all_to_all(x, ALL, 0, 0, tiled=True)  159 us
    ppermute x6, waiting for transfers between devices, to_chips(): lax.ppermute(parts[d], 'aa_0', [(x, (x + d) % 4) for x in range(4)])  58.5 us
    pallas_call x3, Pallas kernels, cosines(): pl.pallas_call(functools.partial(cosine_kernel, len(cores)), out_shape=[j...  19.9 us
    pallas_call x6, Pallas kernels, call(): pl.pallas_call(kernel, out_shape=out_shape, grid_spec=grid_spec, compiler...  19.5 us
    eq x11, local copies, waits for them, and re-layouts, hot_rows(): return ((row_id == col_id) & (row_tile == col_tile)).astype(bf16)  13.8 us
    unnamed x34, local copies, waits for them, and re-layouts  12 us
    all_to_all x1, blocking collectives, per_device(): sums = lax.all_to_all(sums, AA, 0, 0, tiled=True).sum(axis=0)  11.9 us
  transfers between devices with their start and end apart: 8, of which 4 were waited for; matrix products, arithmetic and copies ran while one was open for 2% of the time, Pallas kernels for 2%

profile of v6, /device:TPU:0, one launch (start us, length us, event | category | flops | bytes accessed | tf_op | source)
XLA Modules:
  0.0 528.2 jit_solution(2323266676765583442)
XLA Ops:
  0.7 6.3 %shard_map.68 = f32[8,2,4096]{2,1,0:T(2,128)} custom-call(bf16[448,4096]{1,0:T(8,128)(2,1)} %bitcast.38, bf16[448,4096]{1,0:T(8,128)(2,1)} %bitcast.40), custom_call_target="tpu_custom_call" | custom-call | flops 7340032 | bytes 14680064 | tf_op jit(solution)/shard_map/pallas_call | solution.py:31
  6.9 11.9 %all_to_all.55 = f32[8,2,4096]{2,1,0:T(2,128)S(1)} all-to-all(f32[8,2,4096]{2,1,0:T(2,128)} %shard_map.68), channel_id=1, replica_groups=mesh['aa_0'=4,'aa_1'=2,'ba_0'=4,'ba_1'=4] {'aa_0','aa_1'}, dimensions={0} | all-to-all | bytes 524288 | tf_op jit(solution)/shard_map/all_to_all | solution.py:301
  21.1 2.0 copy-done.5
  23.1 5.0 shard_map.69
  28.1 151.1 %all_to_all.56.refs_1_.refs_2_ = bf16[16,448,896]{2,1,0:T(8,128)(2,1)S(1)} all-to-all(bf16[16,448,896]{2,1,0:T(8,128)(2,1)S(1)} %get-tuple-element.53), channel_id=1, replica_groups=mesh['aa_0'=4,'aa_1'=2,'ba_0'=4,'ba_1'=4] {'ba_0','ba_1'}, dimensions={0} | all-to-all | bytes 25690112 | tf_op jit(solution)/shard_map/all_to_all | solution.py:311
  179.2 5.9 %shard_map.71 = s16[12,384,512]{2,1,0:T(8,128)(2,1)S(1)} custom-call(s32[2,24]{1,0:T(2,128)S(1)} %bitcast.45, s32[1]{0:T(128)} %bitcast.5.refs_0_, bf16[16,448,896]{2,1,0:T(8,128)(2,1)S(1)} %all_to_all.56.refs_1_.refs_2_), custom_call_target="tpu_custom_call" | custom-call | flops 2113929216 | bytes 8257536 | tf_op jit(solution)/shard_map/pallas_call | solution.py:128
  185.1 5.9 %shard_map.70.refs_0_.refs_1_.refs_2_.refs_3_ = s16[12,384,512]{2,1,0:T(8,128)(2,1)S(1)} custom-call(s32[2,24]{1,0:T(2,128)S(1)} %bitcast.46, s32[1]{0:T(128)} %bitcast.4.refs_0_.refs_1_, bf16[16,448,896]{2,1,0:T(8,128)(2,1)S(1)} %all_to_all.56.refs_1_.refs_2_), custom_call_target="tpu_custom_call" | custom-call | flops 2113929216 | bytes 8257536 | tf_op jit(solution)/shard_map/pallas_call | solution.py:128
  193.0 2.5 shard_map.72
  195.5 29.5 %all_to_all.57.refs_3_ = bf16[16,464,128]{2,1,0:T(8,128)(2,1)S(1)} all-to-all(bf16[16,464,128]{2,1,0:T(8,128)(2,1)S(1)} %get-tuple-element.68), channel_id=1, replica_groups=mesh['aa_0'=4,'aa_1'=2,'ba_0'=4,'ba_1'=4] {'ba_0','ba_1'}, dimensions={0} | all-to-all | bytes 3801088 | tf_op jit(solution)/shard_map/all_to_all | solution.py:311
  224.9 8.2 %shard_map.74 = (s16[12,128,512]{2,1,0:T(8,128)(2,1)}, s16[12,128,512]{2,1,0:T(8,128)(2,1)S(1)}) custom-call(s32[2,24]{1,0:T(2,128)S(1)} %bitcast.47, s32[1]{0:T(128)} %bitcast.5.refs_0_, s32[1]{0:T(128)} %bitcast.4.refs_0_.refs_1_, bf16[16,448,896]{2,1,0:T(8,128)(2,1)S(1)} %all_to_all.56.refs_1_.refs_2_, bf16[16,464,128]{2,1,0:T(8,128)(2,1)S(1)} %all_to_all.57.refs_3_), custom_call_target="tpu_custom_call" | custom-call | flops 1409286144 | bytes 5505024 | tf_op jit(solution)/shard_map/pallas_call | solution.py:128
  234.8 2.1 collective-permute-start.2
  245.8 43.5 %collective-permute-done.1.b_ref = s16[3,384,512]{2,1,0:T(8,128)(2,1)S(1)} collective-permute-done((s16[3,384,512]{2,1,0:T(8,128)(2,1)}, s16[3,384,512]{2,1,0:T(8,128)(2,1)S(1)}, u32[]{:S(2)}, u32[]{:S(2)}) %collective-permute-start.1) | collective-permute-done | bytes 1179680 | tf_op jit(solution)/shard_map/ppermute | solution.py:325
  293.9 2.7 shard_map.73
  298.1 2.5 shard_map.75
  340.9 2.5 collective-permute-start.6
  346.8 14.6 %collective-permute-done.5.b_ref = s16[3,128,512]{2,1,0:T(8,128)(2,1)S(1)} collective-permute-done((s16[3,128,512]{2,1,0:T(8,128)(2,1)}, s16[3,128,512]{2,1,0:T(8,128)(2,1)S(1)}, u32[]{:S(2)}, u32[]{:S(2)}) %collective-permute-start.5) | collective-permute-done | bytes 393248 | tf_op jit(solution)/shard_map/ppermute | solution.py:325
  362.5 18.7 %all_to_all.58.got_ref = bf16[128,16,128]{2,1,0:T(8,128)(2,1)S(1)} all-to-all(bf16[128,16,128]{2,1,0:T(8,128)(2,1)S(1)} %shard_map.77), channel_id=1, replica_groups=mesh['aa_0'=4,'aa_1'=2,'ba_0'=4,'ba_1'=4] {'aa_0','aa_1','ba_0','ba_1'}, dimensions={0} | all-to-all | bytes 1048576 | tf_op jit(solution)/shard_map/all_to_all | solution.py:265
  382.0 17.8 %all_to_all.59.got_ref = bf16[128,16,128]{2,1,0:T(8,128)(2,1)S(1)} all-to-all(bf16[128,16,128]{2,1,0:T(8,128)(2,1)S(1)} %shard_map.78), channel_id=1, replica_groups=mesh['aa_0'=4,'aa_1'=2,'ba_0'=4,'ba_1'=4] {'aa_0','aa_1','ba_0','ba_1'}, dimensions={0} | all-to-all | bytes 1048576 | tf_op jit(solution)/shard_map/all_to_all | solution.py:265
  400.6 20.6 %all_to_all.60.got_ref = bf16[128,24,128]{2,1,0:T(8,128)(2,1)S(1)} all-to-all(bf16[128,24,128]{2,1,0:T(8,128)(2,1)S(1)} %shard_map.79), channel_id=1, replica_groups=mesh['aa_0'=4,'aa_1'=2,'ba_0'=4,'ba_1'=4] {'aa_0','aa_1','ba_0','ba_1'}, dimensions={0} | all-to-all | bytes 1572864 | tf_op jit(solution)/shard_map/all_to_all | solution.py:265
  421.9 20.4 %all_to_all.61.got_ref = bf16[128,24,128]{2,1,0:T(8,128)(2,1)S(1)} all-to-all(bf16[128,24,128]{2,1,0:T(8,128)(2,1)S(1)} %shard_map.80), channel_id=1, replica_groups=mesh['aa_0'=4,'aa_1'=2,'ba_0'=4,'ba_1'=4] {'aa_0','aa_1','ba_0','ba_1'}, dimensions={0} | all-to-all | bytes 1572864 | tf_op jit(solution)/shard_map/all_to_all | solution.py:265
  443.1 20.4 %all_to_all.62.got_ref = bf16[128,24,128]{2,1,0:T(8,128)(2,1)S(1)} all-to-all(bf16[128,24,128]{2,1,0:T(8,128)(2,1)S(1)} %shard_map.81), channel_id=1, replica_groups=mesh['aa_0'=4,'aa_1'=2,'ba_0'=4,'ba_1'=4] {'aa_0','aa_1','ba_0','ba_1'}, dimensions={0} | all-to-all | bytes 1572864 | tf_op jit(solution)/shard_map/all_to_all | solution.py:265
  464.3 20.4 %all_to_all.63.got_ref = bf16[128,24,128]{2,1,0:T(8,128)(2,1)S(1)} all-to-all(bf16[128,24,128]{2,1,0:T(8,128)(2,1)S(1)} %shard_map.82), channel_id=1, replica_groups=mesh['aa_0'=4,'aa_1'=2,'ba_0'=4,'ba_1'=4] {'aa_0','aa_1','ba_0','ba_1'}, dimensions={0} | all-to-all | bytes 1572864 | tf_op jit(solution)/shard_map/all_to_all | solution.py:265
  485.6 20.4 %all_to_all.64.got_ref.row_got_ref = bf16[128,24,128]{2,1,0:T(8,128)(2,1)S(1)} all-to-all(bf16[128,24,128]{2,1,0:T(8,128)(2,1)S(1)} %shard_map.83), channel_id=1, replica_groups=mesh['aa_0'=4,'aa_1'=2,'ba_0'=4,'ba_1'=4] {'aa_0','aa_1','ba_0','ba_1'}, dimensions={0} | all-to-all | bytes 1572864 | tf_op jit(solution)/shard_map/all_to_all | solution.py:265
  506.8 20.4 %all_to_all.65.col_got_ref = bf16[128,24,128]{2,1,0:T(8,128)(2,1)S(1)} all-to-all(bf16[128,24,128]{2,1,0:T(8,128)(2,1)S(1)} %shard_map.84), channel_id=1, replica_groups=mesh['aa_0'=4,'aa_1'=2,'ba_0'=4,'ba_1'=4] {'aa_0','aa_1','ba_0','ba_1'}, dimensions={0} | all-to-all | bytes 1572864 | tf_op jit(solution)/shard_map/all_to_all | solution.py:265
  (111 shorter events, 72.0 us)
Async XLA Ops:
  0.6 18.4 %copy-start.11 = (s32[16,16]{1,0:T(8,128)S(1)}, s32[16,16]{1,0:T(8,128)}, u32[]{:S(2)}) copy-start(s32[16,16]{1,0:T(8,128)} %one_ref.1) | copy-start | bytes 3076
  0.6 18.4 %copy-start.12 = (s32[16,16]{1,0:T(8,128)S(1)}, s32[16,16]{1,0:T(8,128)}, u32[]{:S(2)}) copy-start(s32[16,16]{1,0:T(8,128)} %two_ref.1) | copy-start | bytes 3076
  0.7 18.4 %copy-start.13 = (s32[1,24,2]{1,2,0:T(2,128)S(1)}, s32[1,24,2]{1,2,0:T(2,128)}, u32[]{:S(2)}) copy-start(s32[1,24,2]{1,2,0:T(2,128)} %param.9) | copy-start | bytes 580
  19.0 2.0 copy-start.4
  21.1 2.0 copy-start.5
  185.0 8.0 %collective-permute-start = (s16[12,384,512]{2,1,0:T(8,128)(2,1)S(1)}, s16[12,384,512]{2,1,0:T(8,128)(2,1)S(1)}, u32[]{:S(2)}, u32[]{:S(2)}) collective-permute-start(s16[12,384,512]{2,1,0:T(8,128)(2,1)S(1)} %shard_map.71), channel_id=1, source_target_pairs={{0,16},{16,0},{1,17},{17,1},{2,18},{18,2},{3,19},{19,3},{4,20},{20... | collective-permute-start | bytes 14155784 | tf_op jit(solution)/shard_map/ppermute | solution.py:319
  224.9 8.2 %copy-start.6 = (bf16[16,464,128]{2,1,0:T(8,128)(2,1)}, bf16[16,464,128]{2,1,0:T(8,128)(2,1)S(1)}, u32[]{:S(2)}) copy-start(bf16[16,464,128]{2,1,0:T(8,128)(2,1)S(1)} %all_to_all.57.refs_3_) | copy-start | bytes 5701636
  233.1 1.1 copy-start.2
  234.2 63.8 %collective-permute-start.4 = (s16[12,128,512]{2,1,0:T(8,128)(2,1)}, s16[12,128,512]{2,1,0:T(8,128)(2,1)}, u32[]{:S(2)}, u32[]{:S(2)}) collective-permute-start(s16[12,128,512]{2,1,0:T(8,128)(2,1)} %get-tuple-element.70), channel_id=1, source_target_pairs={{0,16},{16,0},{1,17},{17,1},{2,18},{18,2},{3,19},{19,3},{4,20},{20... | collective-permute-start | bytes 4718600 | tf_op jit(solution)/shard_map/ppermute | solution.py:316
  234.2 55.1 %collective-permute-start.1 = (s16[3,384,512]{2,1,0:T(8,128)(2,1)}, s16[3,384,512]{2,1,0:T(8,128)(2,1)S(1)}, u32[]{:S(2)}, u32[]{:S(2)}) collective-permute-start(s16[3,384,512]{2,1,0:T(8,128)(2,1)} %get-tuple-element.63), channel_id=1, source_target_pairs={{0,32},{32,64},{64,96},{96,0},{1,33},{33,65},{65,97},{97,1},{2,34}... | collective-permute-start | bytes 3538952 | tf_op jit(solution)/shard_map/ppermute | solution.py:325
  234.8 55.5 %collective-permute-start.2 = (s16[3,384,512]{2,1,0:T(8,128)(2,1)}, s16[3,384,512]{2,1,0:T(8,128)(2,1)S(1)}, u32[]{:S(2)}, u32[]{:S(2)}) collective-permute-start(s16[3,384,512]{2,1,0:T(8,128)(2,1)} %get-tuple-element.64), channel_id=1, source_target_pairs={{0,64},{32,96},{64,0},{96,32},{1,65},{33,97},{65,1},{97,33},{2,66}... | collective-permute-start | bytes 3538952 | tf_op jit(solution)/shard_map/ppermute | solution.py:325
  236.9 54.5 %collective-permute-start.3 = (s16[3,384,512]{2,1,0:T(8,128)(2,1)}, s16[3,384,512]{2,1,0:T(8,128)(2,1)}, u32[]{:S(2)}, u32[]{:S(2)}) collective-permute-start(s16[3,384,512]{2,1,0:T(8,128)(2,1)} %get-tuple-element.65), channel_id=1, source_target_pairs={{0,96},{32,0},{64,32},{96,64},{1,97},{33,1},{65,33},{97,65},{2,98}... | collective-permute-start | bytes 3538952 | tf_op jit(solution)/shard_map/ppermute | solution.py:325
  245.8 52.3 %copy-start.3 = (s16[12,128,512]{2,1,0:T(8,128)(2,1)S(1)}, s16[12,128,512]{2,1,0:T(8,128)(2,1)}, u32[]{:S(2)}) copy-start(s16[12,128,512]{2,1,0:T(8,128)(2,1)} %copy-done.2) | copy-start | bytes 4718596
  289.3 1.0 copy-start.7
  290.3 1.0 copy-start.9
  291.4 1.3 copy-start.8
  292.6 1.3 copy-start.10
  296.6 1.4 copy-start
  298.1 4.7 copy-start.15
  329.8 15.3 %copy-start.16 = (s32[16]{0:T(128)S(1)}, s32[16]{0:T(128)}, u32[]{:S(2)}) copy-start(s32[16]{0:T(128)} %eq.226) | copy-start | bytes 196
  340.9 21.5 %copy-start.1 = (f32[3,512,384]{2,1,0:T(8,128)S(1)}, f32[3,512,384]{2,1,0:T(8,128)}, u32[]{:S(2)}) copy-start(f32[3,512,384]{2,1,0:T(8,128)} %copy-done) | copy-start | bytes 7077892
  340.9 20.5 %collective-permute-start.5 = (s16[3,128,512]{2,1,0:T(8,128)(2,1)}, s16[3,128,512]{2,1,0:T(8,128)(2,1)S(1)}, u32[]{:S(2)}, u32[]{:S(2)}) collective-permute-start(s16[3,128,512]{2,1,0:T(8,128)(2,1)} %copy-done.14), channel_id=1, source_target_pairs={{0,32},{32,64},{64,96},{96,0},{1,33},{33,65},{65,97},{97,1},{2,34}... | collective-permute-start | bytes 1179656 | tf_op jit(solution)/shard_map/ppermute | solution.py:325
  340.9 20.5 %collective-permute-start.6 = (s16[3,128,512]{2,1,0:T(8,128)(2,1)S(1)}, s16[3,128,512]{2,1,0:T(8,128)(2,1)S(1)}, u32[]{:S(2)}, u32[]{:S(2)}) collective-permute-start(s16[3,128,512]{2,1,0:T(8,128)(2,1)S(1)} %get-tuple-element.77), channel_id=1, source_target_pairs={{0,64},{32,96},{64,0},{96,32},{1,65},{33,97},{65,1},{97,33},{2,66}... | collective-permute-start | bytes 1179656 | tf_op jit(solution)/shard_map/ppermute | solution.py:325
  343.4 18.4 %collective-permute-start.7 = (s16[3,128,512]{2,1,0:T(8,128)(2,1)S(1)}, s16[3,128,512]{2,1,0:T(8,128)(2,1)S(1)}, u32[]{:S(2)}, u32[]{:S(2)}) collective-permute-start(s16[3,128,512]{2,1,0:T(8,128)(2,1)S(1)} %get-tuple-element.78), channel_id=1, source_target_pairs={{0,96},{32,0},{64,32},{96,64},{1,97},{33,1},{65,33},{97,65},{2,98}... | collective-permute-start | bytes 1179656 | tf_op jit(solution)/shard_map/ppermute | solution.py:325
  (1 other events, 0.8 us)

commit v7 on v6

--- a/solution.py
+++ b/solution.py
@@ -12,7 +12,8 @@
 SWEEPS = 4
 BA = ("ba_0", "ba_1")
 AA = ("aa_0", "aa_1")
-ALL = AA + BA
+CROSSED = ("ba_1", "ba_0")
+ALL = ("ba_0", "ba_1", "aa_1", "aa_0")
 LANES = 128
 TILES = BS // LANES
 HALF = BS // 2
@@ -25,6 +26,10 @@
 norm_floor = 1e-06
 
 f32, bf16, i16, i32 = jnp.float32, jnp.bfloat16, jnp.int16, jnp.int32
+
+
+def crossed(owner):
+    return lax.rem(owner, 4) * 4 + lax.div(owner, 4)
 
 
 def call(kernel, out_shape, grid_spec, flops, bytes_accessed, args, mebibytes=8):
@@ -60,7 +65,7 @@
         out_specs=pl.BlockSpec((depth, 2, rows), lambda k: (0, 0, 0)),
     )
     shape = jax.ShapeDtypeStruct((depth, 2, rows), f32)
-    return call(squares_kernel, shape, spec, 4 * one.size, 8 * one.size, (one, two), 60)
+    return call(squares_kernel, shape, spec, 4 * one.size, 8 * one.size, (one, two), 52)
 
 
 def pack_kernel(
@@ -86,10 +91,10 @@
         num_scalar_prefetch=3,
         grid=(owners,),
         in_specs=[
-            pl.BlockSpec((width, BS), lambda o, me, r1, r2: (0, r1[me[0], o])),
-            pl.BlockSpec((width, BS), lambda o, me, r1, r2: (0, r2[me[0], o])),
-            pl.BlockSpec((2, BS), lambda o, me, r1, r2: (0, r1[me[0], o])),
-            pl.BlockSpec((2, BS), lambda o, me, r1, r2: (0, r2[me[0], o])),
+            pl.BlockSpec((width, BS), lambda o, me, r1, r2: (0, r1[me[0], crossed(o)])),
+            pl.BlockSpec((width, BS), lambda o, me, r1, r2: (0, r2[me[0], crossed(o)])),
+            pl.BlockSpec((2, BS), lambda o, me, r1, r2: (0, r1[me[0], crossed(o)])),
+            pl.BlockSpec((2, BS), lambda o, me, r1, r2: (0, r2[me[0], crossed(o)])),
             pl.BlockSpec(slots.shape, lambda o, me, r1, r2: (0, 0)),
         ],
         out_specs=[pl.BlockSpec(x, lambda o, me, r1, r2: (o, 0, 0)) for x in blocks],
@@ -112,9 +117,9 @@
         @pl.loop(0, pairs)
         def _(q):
             at = core_ref[0] * pairs + q
-            a = a_ref[slots_ref[0, at], :width, start : start + rows].T
+            a = a_ref[crossed(slots_ref[0, at]), :width, start : start + rows].T
             for i in range(0, BS, HALF):
-                b = b_ref[slots_ref[1, at], :, i : i + HALF]
+                b = b_ref[crossed(slots_ref[1, at]), :, i : i + HALF]
                 partial = jnp.dot(a, b, preferred_element_type=f32)
                 fixed = jnp.floor(partial * FIXED + 0.5).astype(i32).astype(i16)
                 out_ref[q, :, i : i + HALF] = fixed
@@ -308,7 +313,7 @@
     swap = [(0, 1), (1, 0)]
 
     def gathered(x):
-        return lax.all_to_all(x, BA, 0, 0, tiled=True)
+        return lax.all_to_all(x, CROSSED, 0, 0, tiled=True)
 
     def by_chip(rows, *arrays):
         if len(arrays) == len(CHUNKS):
@@ -340,6 +345,7 @@
 
     def masks():
         every = second[:, width : width + 2, :pairs].astype(i32)
+        every = every.reshape(4, 4, 2, pairs).swapaxes(0, 1).reshape(owners, 2, pairs)
         s_all, r_all = every[:, 0], every[:, 1]
 
         def block_of(source, route):
@@ -349,11 +355,10 @@
         each = pairs // depth
 
         def by_device(x):
-            x = x.reshape(owners, 2, 4, each)
-            return x.transpose(2, 1, 0, 3).reshape(devices, each)
+            return x.reshape(devices, each)
 
         row_dev, col_dev = by_device(block_of(s_all, route_one)), by_device(block_of(r_all, route_two))
-        me = (chip * 2 + core) * owners + column
+        me = (column * 2 + core) * 4 + chip
         pad = jnp.full((4 - each,), -2, i32)
         my_rows = jnp.concatenate([lax.dynamic_index_in_dim(row_dev, me, 0, False), pad])
         my_cols = jnp.concatenate([lax.dynamic_index_in_dim(col_dev, me, 0, False), pad])

time: 531 us -> 517 us (0.974)
  local copies, waits for them, and re-layouts: 53.2 us -> 44 us
    unnamed x34 -> x40, local copies, waits for them, and re-layouts: 12 us -> 12 us
where the time goes in v7:
time: 517 us; the launch traced here: 515 us
  blocking collectives  350 us (68%)
  waiting for transfers between devices  57.5 us (11%)
  Pallas kernels  45.5 us (9%)
  local copies, waits for them, and re-layouts  44 us (9%)
  starting transfers between devices  9.42 us (2%)
  other arithmetic  6.72 us (1%)
    all_to_all x2, blocking collectives, gathered(): return lax.all_to_all(x, CROSSED, 0, 0, tiled=True)  181 us
    all_to_all x8, blocking collectives, exchanged(): return lax.all_to_all(x, ALL, 0, 0, tiled=True)  158 us
    ppermute x6, waiting for transfers between devices, to_chips(): lax.ppermute(parts[d], 'aa_0', [(x, (x + d) % 4) for x in range(4)])  55.6 us
    pallas_call x3, Pallas kernels, cosines(): pl.pallas_call(functools.partial(cosine_kernel, len(cores)), out_shape=[j...  20 us
    pallas_call x6, Pallas kernels, call(): pl.pallas_call(kernel, out_shape=out_shape, grid_spec=grid_spec, compiler...  19 us
    eq x11, local copies, waits for them, and re-layouts, hot_rows(): return ((row_id == col_id) & (row_tile == col_tile)).astype(bf16)  13.5 us
    unnamed x40, local copies, waits for them, and re-layouts  12 us
    all_to_all x1, blocking collectives, per_device(): sums = lax.all_to_all(sums, AA, 0, 0, tiled=True).sum(axis=0)  11.7 us
  transfers between devices with their start and end apart: 8, of which 4 were waited for; matrix products, arithmetic and copies ran while one was open for 2% of the time, Pallas kernels for 2%

profile of v7, /device:TPU:0, one launch (start us, length us, event | category | flops | bytes accessed | tf_op | source)
XLA Modules:
  0.0 514.5 jit_solution(12597227843296217538)
XLA Ops:
  0.7 5.6 %shard_map.68 = f32[8,2,4096]{2,1,0:T(2,128)S(1)} custom-call(bf16[448,4096]{1,0:T(8,128)(2,1)} %bitcast.36, bf16[448,4096]{1,0:T(8,128)(2,1)} %bitcast.38), custom_call_target="tpu_custom_call" | custom-call | flops 7340032 | bytes 14680064 | tf_op jit(solution)/shard_map/pallas_call | solution.py:36
  6.3 11.7 %all_to_all.55 = f32[8,2,4096]{2,1,0:T(2,128)S(1)} all-to-all(f32[8,2,4096]{2,1,0:T(2,128)S(1)} %shard_map.68), channel_id=1, replica_groups=mesh['aa_0'=4,'aa_1'=2,'ba_0'=4,'ba_1'=4] {'aa_0','aa_1'}, dimensions={0} | all-to-all | bytes 524288 | tf_op jit(solution)/shard_map/all_to_all | solution.py:306
  22.2 5.1 shard_map.69
  27.4 150.8 %all_to_all.56.refs_1_.refs_2_ = bf16[16,448,896]{2,1,0:T(8,128)(2,1)S(1)} all-to-all(bf16[16,448,896]{2,1,0:T(8,128)(2,1)S(1)} %get-tuple-element.53), channel_id=1, replica_groups=mesh['aa_0'=4,'aa_1'=2,'ba_0'=4,'ba_1'=4] {'ba_1','ba_0'}, dimensions={0} | all-to-all | bytes 25690112 | tf_op jit(solution)/shard_map/all_to_all | solution.py:316
  178.2 5.9 %shard_map.71 = s16[12,384,512]{2,1,0:T(8,128)(2,1)S(1)} custom-call(s32[2,24]{1,0:T(2,128)S(1)} %bitcast.43, s32[1]{0:T(128)} %bitcast.5.refs_0_, bf16[16,448,896]{2,1,0:T(8,128)(2,1)S(1)} %all_to_all.56.refs_1_.refs_2_), custom_call_target="tpu_custom_call" | custom-call | flops 2113929216 | bytes 8257536 | tf_op jit(solution)/shard_map/pallas_call | solution.py:133
  184.2 5.9 %shard_map.70.refs_0_.refs_1_.refs_2_.refs_3_ = s16[12,384,512]{2,1,0:T(8,128)(2,1)S(1)} custom-call(s32[2,24]{1,0:T(2,128)S(1)} %bitcast.44, s32[1]{0:T(128)} %bitcast.4.refs_0_.refs_1_, bf16[16,448,896]{2,1,0:T(8,128)(2,1)S(1)} %all_to_all.56.refs_1_.refs_2_), custom_call_target="tpu_custom_call" | custom-call | flops 2113929216 | bytes 8257536 | tf_op jit(solution)/shard_map/pallas_call | solution.py:133
  192.1 2.4 shard_map.72
  194.5 30.0 %all_to_all.57.refs_3_ = bf16[16,464,128]{2,1,0:T(8,128)(2,1)S(1)} all-to-all(bf16[16,464,128]{2,1,0:T(8,128)(2,1)S(1)} %get-tuple-element.68), channel_id=1, replica_groups=mesh['aa_0'=4,'aa_1'=2,'ba_0'=4,'ba_1'=4] {'ba_1','ba_0'}, dimensions={0} | all-to-all | bytes 3801088 | tf_op jit(solution)/shard_map/all_to_all | solution.py:316
  224.5 8.1 %shard_map.74 = (s16[12,128,512]{2,1,0:T(8,128)(2,1)}, s16[12,128,512]{2,1,0:T(8,128)(2,1)S(1)}) custom-call(s32[2,24]{1,0:T(2,128)S(1)} %bitcast.45, s32[1]{0:T(128)} %bitcast.5.refs_0_, s32[1]{0:T(128)} %bitcast.4.refs_0_.refs_1_, bf16[16,448,896]{2,1,0:T(8,128)(2,1)S(1)} %all_to_all.56.refs_1_.refs_2_, bf16[16,464,128]{2,1,0:T(8,128)(2,1)S(1)} %all_to_all.57.refs_3_), custom_call_target="tpu_custom_call" | custom-call | flops 1409286144 | bytes 5505024 | tf_op jit(solution)/shard_map/pallas_call | solution.py:133
  236.5 2.6 collective-permute-start.3
  247.0 41.9 %collective-permute-done.1.b_ref = s16[3,384,512]{2,1,0:T(8,128)(2,1)S(1)} collective-permute-done((s16[3,384,512]{2,1,0:T(8,128)(2,1)}, s16[3,384,512]{2,1,0:T(8,128)(2,1)S(1)}, u32[]{:S(2)}, u32[]{:S(2)}) %collective-permute-start.1) | collective-permute-done | bytes 1179680 | tf_op jit(solution)/shard_map/ppermute | solution.py:330
  293.5 2.7 shard_map.73
  297.6 2.5 shard_map.75
  329.5 2.4 collective-permute-start.6
  335.8 4.4 collective-permute-done.5.b_ref
  340.2 9.3 %collective-permute-done.6.c_ref = s16[3,128,512]{2,1,0:T(8,128)(2,1)S(1)} collective-permute-done((s16[3,128,512]{2,1,0:T(8,128)(2,1)S(1)}, s16[3,128,512]{2,1,0:T(8,128)(2,1)S(1)}, u32[]{:S(2)}, u32[]{:S(2)}) %collective-permute-start.6) | collective-permute-done | bytes 393248 | tf_op jit(solution)/shard_map/ppermute | solution.py:330
  350.2 18.8 %all_to_all.58.got_ref = bf16[128,16,128]{2,1,0:T(8,128)(2,1)S(1)} all-to-all(bf16[128,16,128]{2,1,0:T(8,128)(2,1)S(1)} %shard_map.77), channel_id=1, replica_groups=mesh['aa_0'=4,'aa_1'=2,'ba_0'=4,'ba_1'=4] {'ba_0','ba_1','aa_1','aa_0'}, dimensions={0} | all-to-all | bytes 1048576 | tf_op jit(solution)/shard_map/all_to_all | solution.py:270
  369.8 17.6 %all_to_all.59.got_ref = bf16[128,16,128]{2,1,0:T(8,128)(2,1)S(1)} all-to-all(bf16[128,16,128]{2,1,0:T(8,128)(2,1)S(1)} %shard_map.78), channel_id=1, replica_groups=mesh['aa_0'=4,'aa_1'=2,'ba_0'=4,'ba_1'=4] {'ba_0','ba_1','aa_1','aa_0'}, dimensions={0} | all-to-all | bytes 1048576 | tf_op jit(solution)/shard_map/all_to_all | solution.py:270
  388.1 20.4 %all_to_all.60.got_ref = bf16[128,24,128]{2,1,0:T(8,128)(2,1)S(1)} all-to-all(bf16[128,24,128]{2,1,0:T(8,128)(2,1)S(1)} %shard_map.79), channel_id=1, replica_groups=mesh['aa_0'=4,'aa_1'=2,'ba_0'=4,'ba_1'=4] {'ba_0','ba_1','aa_1','aa_0'}, dimensions={0} | all-to-all | bytes 1572864 | tf_op jit(solution)/shard_map/all_to_all | solution.py:270
  409.3 20.2 %all_to_all.61.got_ref = bf16[128,24,128]{2,1,0:T(8,128)(2,1)S(1)} all-to-all(bf16[128,24,128]{2,1,0:T(8,128)(2,1)S(1)} %shard_map.80), channel_id=1, replica_groups=mesh['aa_0'=4,'aa_1'=2,'ba_0'=4,'ba_1'=4] {'ba_0','ba_1','aa_1','aa_0'}, dimensions={0} | all-to-all | bytes 1572864 | tf_op jit(solution)/shard_map/all_to_all | solution.py:270
  430.3 20.2 %all_to_all.62.got_ref = bf16[128,24,128]{2,1,0:T(8,128)(2,1)S(1)} all-to-all(bf16[128,24,128]{2,1,0:T(8,128)(2,1)S(1)} %shard_map.81), channel_id=1, replica_groups=mesh['aa_0'=4,'aa_1'=2,'ba_0'=4,'ba_1'=4] {'ba_0','ba_1','aa_1','aa_0'}, dimensions={0} | all-to-all | bytes 1572864 | tf_op jit(solution)/shard_map/all_to_all | solution.py:270
  451.3 20.2 %all_to_all.63.got_ref = bf16[128,24,128]{2,1,0:T(8,128)(2,1)S(1)} all-to-all(bf16[128,24,128]{2,1,0:T(8,128)(2,1)S(1)} %shard_map.82), channel_id=1, replica_groups=mesh['aa_0'=4,'aa_1'=2,'ba_0'=4,'ba_1'=4] {'ba_0','ba_1','aa_1','aa_0'}, dimensions={0} | all-to-all | bytes 1572864 | tf_op jit(solution)/shard_map/all_to_all | solution.py:270
  472.3 20.2 %all_to_all.64.got_ref.row_got_ref = bf16[128,24,128]{2,1,0:T(8,128)(2,1)S(1)} all-to-all(bf16[128,24,128]{2,1,0:T(8,128)(2,1)S(1)} %shard_map.83), channel_id=1, replica_groups=mesh['aa_0'=4,'aa_1'=2,'ba_0'=4,'ba_1'=4] {'ba_0','ba_1','aa_1','aa_0'}, dimensions={0} | all-to-all | bytes 1572864 | tf_op jit(solution)/shard_map/all_to_all | solution.py:270
  493.3 20.2 %all_to_all.65.col_got_ref = bf16[128,24,128]{2,1,0:T(8,128)(2,1)S(1)} all-to-all(bf16[128,24,128]{2,1,0:T(8,128)(2,1)S(1)} %shard_map.84), channel_id=1, replica_groups=mesh['aa_0'=4,'aa_1'=2,'ba_0'=4,'ba_1'=4] {'ba_0','ba_1','aa_1','aa_0'}, dimensions={0} | all-to-all | bytes 1572864 | tf_op jit(solution)/shard_map/all_to_all | solution.py:270
  (108 shorter events, 64.2 us)
Async XLA Ops:
  0.6 17.5 %copy-start.11 = (s32[16,16]{1,0:T(8,128)S(1)}, s32[16,16]{1,0:T(8,128)}, u32[]{:S(2)}) copy-start(s32[16,16]{1,0:T(8,128)} %one_ref.1) | copy-start | bytes 3076
  0.6 17.5 %copy-start.12 = (s32[16,16]{1,0:T(8,128)S(1)}, s32[16,16]{1,0:T(8,128)}, u32[]{:S(2)}) copy-start(s32[16,16]{1,0:T(8,128)} %two_ref.1) | copy-start | bytes 3076
  0.7 17.5 %copy-start.13 = (s32[1,24,2]{1,2,0:T(2,128)S(1)}, s32[1,24,2]{1,2,0:T(2,128)}, u32[]{:S(2)}) copy-start(s32[1,24,2]{1,2,0:T(2,128)} %param.9) | copy-start | bytes 580
  18.1 2.0 copy-start.4
  20.2 2.0 copy-start.5
  184.1 8.0 %collective-permute-start = (s16[12,384,512]{2,1,0:T(8,128)(2,1)S(1)}, s16[12,384,512]{2,1,0:T(8,128)(2,1)S(1)}, u32[]{:S(2)}, u32[]{:S(2)}) collective-permute-start(s16[12,384,512]{2,1,0:T(8,128)(2,1)S(1)} %shard_map.71), channel_id=1, source_target_pairs={{0,16},{16,0},{1,17},{17,1},{2,18},{18,2},{3,19},{19,3},{4,20},{20... | collective-permute-start | bytes 14155784 | tf_op jit(solution)/shard_map/ppermute | solution.py:324
  224.5 8.1 %copy-start.6 = (bf16[16,464,128]{2,1,0:T(8,128)(2,1)}, bf16[16,464,128]{2,1,0:T(8,128)(2,1)S(1)}, u32[]{:S(2)}) copy-start(bf16[16,464,128]{2,1,0:T(8,128)(2,1)S(1)} %all_to_all.57.refs_3_) | copy-start | bytes 5701636
  232.7 1.1 copy-start.2
  233.8 63.8 %collective-permute-start.4 = (s16[12,128,512]{2,1,0:T(8,128)(2,1)}, s16[12,128,512]{2,1,0:T(8,128)(2,1)}, u32[]{:S(2)}, u32[]{:S(2)}) collective-permute-start(s16[12,128,512]{2,1,0:T(8,128)(2,1)} %get-tuple-element.70), channel_id=1, source_target_pairs={{0,16},{16,0},{1,17},{17,1},{2,18},{18,2},{3,19},{19,3},{4,20},{20... | collective-permute-start | bytes 4718600 | tf_op jit(solution)/shard_map/ppermute | solution.py:321
  233.8 55.1 %collective-permute-start.1 = (s16[3,384,512]{2,1,0:T(8,128)(2,1)}, s16[3,384,512]{2,1,0:T(8,128)(2,1)S(1)}, u32[]{:S(2)}, u32[]{:S(2)}) collective-permute-start(s16[3,384,512]{2,1,0:T(8,128)(2,1)} %get-tuple-element.63), channel_id=1, source_target_pairs={{0,32},{32,64},{64,96},{96,0},{1,33},{33,65},{65,97},{97,1},{2,34}... | collective-permute-start | bytes 3538952 | tf_op jit(solution)/shard_map/ppermute | solution.py:330
  234.4 55.5 %collective-permute-start.2 = (s16[3,384,512]{2,1,0:T(8,128)(2,1)}, s16[3,384,512]{2,1,0:T(8,128)(2,1)S(1)}, u32[]{:S(2)}, u32[]{:S(2)}) collective-permute-start(s16[3,384,512]{2,1,0:T(8,128)(2,1)} %get-tuple-element.64), channel_id=1, source_target_pairs={{0,64},{32,96},{64,0},{96,32},{1,65},{33,97},{65,1},{97,33},{2,66}... | collective-permute-start | bytes 3538952 | tf_op jit(solution)/shard_map/ppermute | solution.py:330
  236.5 54.5 %collective-permute-start.3 = (s16[3,384,512]{2,1,0:T(8,128)(2,1)}, s16[3,384,512]{2,1,0:T(8,128)(2,1)}, u32[]{:S(2)}, u32[]{:S(2)}) collective-permute-start(s16[3,384,512]{2,1,0:T(8,128)(2,1)} %get-tuple-element.65), channel_id=1, source_target_pairs={{0,96},{32,0},{64,32},{96,64},{1,97},{33,1},{65,33},{97,65},{2,98}... | collective-permute-start | bytes 3538952 | tf_op jit(solution)/shard_map/ppermute | solution.py:330
  247.0 50.6 %copy-start.3 = (s16[12,128,512]{2,1,0:T(8,128)(2,1)S(1)}, s16[12,128,512]{2,1,0:T(8,128)(2,1)}, u32[]{:S(2)}) copy-start(s16[12,128,512]{2,1,0:T(8,128)(2,1)} %copy-done.2) | copy-start | bytes 4718596
  289.9 1.0 copy-start.9
  290.9 1.3 copy-start.8
  292.2 1.3 copy-start.10
  296.2 1.4 copy-start
  297.6 4.7 copy-start.17
  297.6 4.7 copy-start.18
  321.5 12.6 %copy-start.19 = (s32[16]{0:T(128)S(1)}, s32[16]{0:T(128)}, u32[]{:S(2)}) copy-start(s32[16]{0:T(128)} %eq.226) | copy-start | bytes 196
  329.1 21.0 %copy-start.1 = (f32[3,512,384]{2,1,0:T(8,128)S(1)}, f32[3,512,384]{2,1,0:T(8,128)}, u32[]{:S(2)}) copy-start(f32[3,512,384]{2,1,0:T(8,128)} %copy-done) | copy-start | bytes 7077892
  329.1 11.1 %collective-permute-start.5 = (s16[3,128,512]{2,1,0:T(8,128)(2,1)}, s16[3,128,512]{2,1,0:T(8,128)(2,1)S(1)}, u32[]{:S(2)}, u32[]{:S(2)}) collective-permute-start(s16[3,128,512]{2,1,0:T(8,128)(2,1)} %copy-done.14), channel_id=1, source_target_pairs={{0,32},{32,64},{64,96},{96,0},{1,33},{33,65},{65,97},{97,1},{2,34}... | collective-permute-start | bytes 1179656 | tf_op jit(solution)/shard_map/ppermute | solution.py:330
  329.5 20.0 %collective-permute-start.6 = (s16[3,128,512]{2,1,0:T(8,128)(2,1)S(1)}, s16[3,128,512]{2,1,0:T(8,128)(2,1)S(1)}, u32[]{:S(2)}, u32[]{:S(2)}) collective-permute-start(s16[3,128,512]{2,1,0:T(8,128)(2,1)S(1)} %get-tuple-element.77), channel_id=1, source_target_pairs={{0,64},{32,96},{64,0},{96,32},{1,65},{33,97},{65,1},{97,33},{2,66}... | collective-permute-start | bytes 1179656 | tf_op jit(solution)/shard_map/ppermute | solution.py:330
  331.8 17.6 %collective-permute-start.7 = (s16[3,128,512]{2,1,0:T(8,128)(2,1)S(1)}, s16[3,128,512]{2,1,0:T(8,128)(2,1)S(1)}, u32[]{:S(2)}, u32[]{:S(2)}) collective-permute-start(s16[3,128,512]{2,1,0:T(8,128)(2,1)S(1)} %get-tuple-element.78), channel_id=1, source_target_pairs={{0,96},{32,0},{64,32},{96,64},{1,97},{33,1},{65,33},{97,65},{2,98}... | collective-permute-start | bytes 1179656 | tf_op jit(solution)/shard_map/ppermute | solution.py:330
  (4 other events, 3.1 us)

commit v8 on v7

--- a/solution.py
+++ b/solution.py
@@ -240,6 +240,39 @@
     emit_rows(times_rows(refs[:-1], padded), refs[-1])
 
 
+def last_kernel(core_ref, chip_ref, slots_ref, got_ref, hot_ref, *refs):
+    mats, out_ref = refs[:-1], refs[-1]
+    scale = 1.0 / (1.0 + totals_of(hot_ref[...], got_ref))
+    padded = jnp.concatenate([scale, jnp.zeros((LANES - scale.shape[0], LANES), f32)], axis=0)
+    rows = times_rows(mats, padded)
+    each = mats[0].shape[0]
+    totals = [jnp.concatenate(rows[TILES * k : TILES * (k + 1)], axis=0) for k in range(each)]
+    first = core_ref[0] * (slots_ref.shape[1] // 2) + chip_ref[0] * each
+    depth = 2 * 4
+    for source in range(out_ref.shape[0] // depth):
+        total = jnp.zeros_like(totals[0])
+        for k in range(each):
+            total = total + jnp.where(slots_ref[1, first + k] == source, totals[k], 0.0)
+        high = total.astype(bf16).astype(f32)
+        tile = jnp.concatenate([high, total - high], axis=0).astype(bf16)
+        out_ref[source * depth : (source + 1) * depth] = jnp.broadcast_to(
+            tile[None], (depth, *tile.shape)
+        )
+
+
+def last_step(core, chip, slots, got, hot, mats, devices):
+    out = jax.ShapeDtypeStruct((devices, 2 * TILES, LANES), bf16)
+    scalars = pl.BlockSpec(memory_space=pltpu.SMEM)
+    vectors = pl.BlockSpec(memory_space=pltpu.VMEM)
+    return pl.pallas_call(
+        last_kernel,
+        out_shape=out,
+        in_specs=[scalars] * 3 + [vectors] * (2 + len(mats)),
+        out_specs=vectors,
+        compiler_params=pltpu.CompilerParams(vmem_limit_bytes=8 * 2**20),
+    )(core, chip, slots, got, hot, *mats)
+
+
 def log_kernel(row_got_ref, row_hot_ref, col_got_ref, col_hot_ref, row_log_ref, col_log_ref):
     row_log_ref[...] = jnp.log(1.0 / (1.0 + totals_of(row_hot_ref[...], row_got_ref)))
     col_log_ref[...] = jnp.log(1.0 / (1.0 + totals_of(col_hot_ref[...], col_got_ref)))
@@ -363,11 +396,12 @@
         my_rows = jnp.concatenate([lax.dynamic_index_in_dim(row_dev, me, 0, False), pad])
         my_cols = jnp.concatenate([lax.dynamic_index_in_dim(col_dev, me, 0, False), pad])
         own_blocks = column * blocks_dev + jnp.arange(blocks_dev)
+        own_route = lax.dynamic_index_in_dim(route_two, column, 0, False)
         return [
             hot_rows(my_rows, row_dev),
             hot_rows(my_cols, col_dev),
             hot_rows(own_blocks, row_dev),
-            hot_rows(own_blocks, col_dev),
+            hot_rows(jnp.arange(blocks_dev), jnp.repeat(own_route, depth)[:, None]),
             hot_rows(my_rows, row_dev, False),
             hot_rows(my_cols, col_dev, False),
         ]
@@ -382,7 +416,7 @@
     for _ in range(SWEEPS - 2):
         got = exchanged(step(got, hot[0], by_col, devices))
         got = exchanged(step(got, hot[1], by_row, devices))
-    last = exchanged(step(got, hot[0], by_col, devices))
+    last = exchanged(last_step(at_core, at_chip, slots, got, hot[0], by_col, devices))
     got, last = tied((got, last))
     logs = [jax.ShapeDtypeStruct((blocks_dev * TILES, LANES), f32)] * 2
     row_log, col_log = on_chip(log_kernel, logs, 2**20, (got, hot[2], last, hot[3]))

time: 517 us -> 494 us (0.956)
  waiting for transfers between devices: 57.5 us -> 37.2 us
    ppermute x6, waiting for transfers between devices: 55.6 us -> 35.2 us  [to_chips(): lax.ppermute(parts[d], 'aa_0', [(x, (x + d) % 4) for x in range(4)])]
    all_to_all x8, blocking collectives: 158 us -> 153 us  [exchanged(): return lax.all_to_all(x, ALL, 0, 0, tiled=True)]
    eq x11 -> x14, local copies, waits for them, and re-layouts: 13.5 us -> 17.1 us  [hot_rows(): return ((row_id == col_id) & (row_tile == col_tile)).astype(bf16)]
    unnamed x40 -> x44, local copies, waits for them, and re-layouts: 12 us -> 14.5 us
  transfers between devices with their start and end apart: 8 -> 8, of which waited for: 4 -> 2; matrix products, arithmetic and copies ran while one was open for 2% -> 7% of each run, Pallas kernels for 2% -> 2%
where the time goes in v8:
time: 494 us; the launch traced here: 492 us
  blocking collectives  345 us (70%)
  Pallas kernels  48.2 us (10%)
  local copies, waits for them, and re-layouts  45.8 us (9%)
  waiting for transfers between devices  37.2 us (8%)
  starting transfers between devices  9.44 us (2%)
  other arithmetic  5.06 us (1%)
    all_to_all x2, blocking collectives, gathered(): return lax.all_to_all(x, CROSSED, 0, 0, tiled=True)  181 us
    all_to_all x8, blocking collectives, exchanged(): return lax.all_to_all(x, ALL, 0, 0, tiled=True)  153 us
    ppermute x6, waiting for transfers between devices, to_chips(): lax.ppermute(parts[d], 'aa_0', [(x, (x + d) % 4) for x in range(4)])  35.2 us
    pallas_call x6, Pallas kernels, call(): pl.pallas_call(kernel, out_shape=out_shape, grid_spec=grid_spec, compiler...  21.3 us
    pallas_call x3, Pallas kernels, cosines(): pl.pallas_call(functools.partial(cosine_kernel, len(cores)), out_shape=[j...  19.9 us
    eq x14, local copies, waits for them, and re-layouts, hot_rows(): return ((row_id == col_id) & (row_tile == col_tile)).astype(bf16)  17.1 us
    unnamed x44, local copies, waits for them, and re-layouts  14.5 us
    all_to_all x1, blocking collectives, per_device(): sums = lax.all_to_all(sums, AA, 0, 0, tiled=True).sum(axis=0)  11.7 us
  transfers between devices with their start and end apart: 8, of which 2 were waited for; matrix products, arithmetic and copies ran while one was open for 7% of the time, Pallas kernels for 2%

profile of v8, /device:TPU:0, one launch (start us, length us, event | category | flops | bytes accessed | tf_op | source)
XLA Modules:
  0.0 491.8 jit_solution(8060945610335179187)
XLA Ops:
  0.7 5.6 %shard_map.68 = f32[8,2,4096]{2,1,0:T(2,128)S(1)} custom-call(bf16[448,4096]{1,0:T(8,128)(2,1)} %bitcast.42, bf16[448,4096]{1,0:T(8,128)(2,1)} %bitcast.44), custom_call_target="tpu_custom_call" | custom-call | flops 7340032 | bytes 14680064 | tf_op jit(solution)/shard_map/pallas_call | solution.py:36
  6.3 11.7 %all_to_all.55 = f32[8,2,4096]{2,1,0:T(2,128)S(1)} all-to-all(f32[8,2,4096]{2,1,0:T(2,128)S(1)} %shard_map.68), channel_id=1, replica_groups=mesh['aa_0'=4,'aa_1'=2,'ba_0'=4,'ba_1'=4] {'aa_0','aa_1'}, dimensions={0} | all-to-all | bytes 524288 | tf_op jit(solution)/shard_map/all_to_all | solution.py:339
  22.2 5.1 %shard_map.69 = (bf16[16,448,896]{2,1,0:T(8,128)(2,1)S(1)}, bf16[16,464,128]{2,1,0:T(8,128)(2,1)S(1)}) custom-call(s32[1]{0:T(128)} %bitcast.2.me_ref, s32[16,16]{1,0:T(8,128)S(1)} %copy-done.12, s32[16,16]{1,0:T(8,128)S(1)} %copy-done.13, bf16[448,4096]{1,0:T(8,128)(2,1)S(1)} %bitcast.43, bf16[448,4096]{1,0:T(8,128)(2,1)S(1)} %bitcast.45, ...), custom_call_target="tpu_custom_call" | custom-call | flops 14680064 | bytes 29360128 | tf_op jit(solution)/shard_map/pallas_call | solution.py:36
  27.4 150.8 %all_to_all.56.refs_1_.refs_2_ = bf16[16,448,896]{2,1,0:T(8,128)(2,1)S(1)} all-to-all(bf16[16,448,896]{2,1,0:T(8,128)(2,1)S(1)} %get-tuple-element.53), channel_id=1, replica_groups=mesh['aa_0'=4,'aa_1'=2,'ba_0'=4,'ba_1'=4] {'ba_1','ba_0'}, dimensions={0} | all-to-all | bytes 25690112 | tf_op jit(solution)/shard_map/all_to_all | solution.py:349
  178.2 5.9 %shard_map.71 = s16[12,384,512]{2,1,0:T(8,128)(2,1)S(1)} custom-call(s32[2,24]{1,0:T(2,128)S(1)} %bitcast.49, s32[1]{0:T(128)} %bitcast.5.refs_0_, bf16[16,448,896]{2,1,0:T(8,128)(2,1)S(1)} %all_to_all.56.refs_1_.refs_2_), custom_call_target="tpu_custom_call" | custom-call | flops 2113929216 | bytes 8257536 | tf_op jit(solution)/shard_map/pallas_call | solution.py:133
  184.2 5.9 %shard_map.70.refs_0_.refs_1_.refs_2_.refs_3_ = s16[12,384,512]{2,1,0:T(8,128)(2,1)S(1)} custom-call(s32[2,24]{1,0:T(2,128)S(1)} %bitcast.50, s32[1]{0:T(128)} %bitcast.4.refs_0_.refs_1_.core_ref, bf16[16,448,896]{2,1,0:T(8,128)(2,1)S(1)} %all_to_all.56.refs_1_.refs_2_), custom_call_target="tpu_custom_call" | custom-call | flops 2113929216 | bytes 8257536 | tf_op jit(solution)/shard_map/pallas_call | solution.py:133
  192.1 2.5 shard_map.72
  194.6 30.0 %all_to_all.57.refs_3_ = bf16[16,464,128]{2,1,0:T(8,128)(2,1)S(1)} all-to-all(bf16[16,464,128]{2,1,0:T(8,128)(2,1)S(1)} %get-tuple-element.68), channel_id=1, replica_groups=mesh['aa_0'=4,'aa_1'=2,'ba_0'=4,'ba_1'=4] {'ba_1','ba_0'}, dimensions={0} | all-to-all | bytes 3801088 | tf_op jit(solution)/shard_map/all_to_all | solution.py:349
  224.6 8.1 %shard_map.74 = (s16[12,128,512]{2,1,0:T(8,128)(2,1)}, s16[12,128,512]{2,1,0:T(8,128)(2,1)S(1)}) custom-call(s32[2,24]{1,0:T(2,128)S(1)} %bitcast.51, s32[1]{0:T(128)} %bitcast.5.refs_0_, s32[1]{0:T(128)} %bitcast.4.refs_0_.refs_1_.core_ref, bf16[16,448,896]{2,1,0:T(8,128)(2,1)S(1)} %all_to_all.56.refs_1_.refs_2_, bf16[16,464,128]{2,1,0:T(8,128)(2,1)S(1)} %all_to_all.57.refs_3_), custom_call_target="tpu_custom_call" | custom-call | flops 1409286144 | bytes 5505024 | tf_op jit(solution)/shard_map/pallas_call | solution.py:133
  234.5 2.1 collective-permute-start.2
  236.6 2.6 collective-permute-start.3
  253.8 35.2 %collective-permute-done.1.b_ref = s16[3,384,512]{2,1,0:T(8,128)(2,1)S(1)} collective-permute-done((s16[3,384,512]{2,1,0:T(8,128)(2,1)}, s16[3,384,512]{2,1,0:T(8,128)(2,1)S(1)}, u32[]{:S(2)}, u32[]{:S(2)}) %collective-permute-start.1) | collective-permute-done | bytes 1179680 | tf_op jit(solution)/shard_map/ppermute | solution.py:363
  293.6 2.7 shard_map.73
  297.8 3.2 shard_map.75
  306.0 2.4 collective-permute-start.6
  328.4 2.2 shard_map.76
  332.4 18.8 %all_to_all.58.got_ref = bf16[128,16,128]{2,1,0:T(8,128)(2,1)S(1)} all-to-all(bf16[128,16,128]{2,1,0:T(8,128)(2,1)S(1)} %shard_map.77), channel_id=1, replica_groups=mesh['aa_0'=4,'aa_1'=2,'ba_0'=4,'ba_1'=4] {'ba_0','ba_1','aa_1','aa_0'}, dimensions={0} | all-to-all | bytes 1048576 | tf_op jit(solution)/shard_map/all_to_all | solution.py:303
  351.9 17.6 %all_to_all.59.got_ref = bf16[128,16,128]{2,1,0:T(8,128)(2,1)S(1)} all-to-all(bf16[128,16,128]{2,1,0:T(8,128)(2,1)S(1)} %shard_map.78), channel_id=1, replica_groups=mesh['aa_0'=4,'aa_1'=2,'ba_0'=4,'ba_1'=4] {'ba_0','ba_1','aa_1','aa_0'}, dimensions={0} | all-to-all | bytes 1048576 | tf_op jit(solution)/shard_map/all_to_all | solution.py:303
  370.3 20.4 %all_to_all.60.got_ref = bf16[128,24,128]{2,1,0:T(8,128)(2,1)S(1)} all-to-all(bf16[128,24,128]{2,1,0:T(8,128)(2,1)S(1)} %shard_map.79), channel_id=1, replica_groups=mesh['aa_0'=4,'aa_1'=2,'ba_0'=4,'ba_1'=4] {'ba_0','ba_1','aa_1','aa_0'}, dimensions={0} | all-to-all | bytes 1572864 | tf_op jit(solution)/shard_map/all_to_all | solution.py:303
  391.4 20.2 %all_to_all.61.got_ref = bf16[128,24,128]{2,1,0:T(8,128)(2,1)S(1)} all-to-all(bf16[128,24,128]{2,1,0:T(8,128)(2,1)S(1)} %shard_map.80), channel_id=1, replica_groups=mesh['aa_0'=4,'aa_1'=2,'ba_0'=4,'ba_1'=4] {'ba_0','ba_1','aa_1','aa_0'}, dimensions={0} | all-to-all | bytes 1572864 | tf_op jit(solution)/shard_map/all_to_all | solution.py:303
  412.4 20.2 %all_to_all.62.got_ref = bf16[128,24,128]{2,1,0:T(8,128)(2,1)S(1)} all-to-all(bf16[128,24,128]{2,1,0:T(8,128)(2,1)S(1)} %shard_map.81), channel_id=1, replica_groups=mesh['aa_0'=4,'aa_1'=2,'ba_0'=4,'ba_1'=4] {'ba_0','ba_1','aa_1','aa_0'}, dimensions={0} | all-to-all | bytes 1572864 | tf_op jit(solution)/shard_map/all_to_all | solution.py:303
  433.4 20.2 %all_to_all.63.got_ref = bf16[128,24,128]{2,1,0:T(8,128)(2,1)S(1)} all-to-all(bf16[128,24,128]{2,1,0:T(8,128)(2,1)S(1)} %shard_map.82), channel_id=1, replica_groups=mesh['aa_0'=4,'aa_1'=2,'ba_0'=4,'ba_1'=4] {'ba_0','ba_1','aa_1','aa_0'}, dimensions={0} | all-to-all | bytes 1572864 | tf_op jit(solution)/shard_map/all_to_all | solution.py:303
  454.5 20.2 %all_to_all.64.got_ref.row_got_ref = bf16[128,24,128]{2,1,0:T(8,128)(2,1)S(1)} all-to-all(bf16[128,24,128]{2,1,0:T(8,128)(2,1)S(1)} %shard_map.83), channel_id=1, replica_groups=mesh['aa_0'=4,'aa_1'=2,'ba_0'=4,'ba_1'=4] {'ba_0','ba_1','aa_1','aa_0'}, dimensions={0} | all-to-all | bytes 1572864 | tf_op jit(solution)/shard_map/all_to_all | solution.py:303
  476.0 14.9 %all_to_all.65.col_got_ref = bf16[128,8,128]{2,1,0:T(8,128)(2,1)S(1)} all-to-all(bf16[128,8,128]{2,1,0:T(8,128)(2,1)S(1)} %shard_map.84), channel_id=1, replica_groups=mesh['aa_0'=4,'aa_1'=2,'ba_0'=4,'ba_1'=4] {'ba_0','ba_1','aa_1','aa_0'}, dimensions={0} | all-to-all | bytes 524288 | tf_op jit(solution)/shard_map/all_to_all | solution.py:303
  (122 shorter events, 62.2 us)
Async XLA Ops:
  0.6 17.5 %copy-start.12 = (s32[16,16]{1,0:T(8,128)S(1)}, s32[16,16]{1,0:T(8,128)}, u32[]{:S(2)}) copy-start(s32[16,16]{1,0:T(8,128)} %one_ref.1) | copy-start | bytes 3076
  0.6 17.5 %copy-start.13 = (s32[16,16]{1,0:T(8,128)S(1)}, s32[16,16]{1,0:T(8,128)}, u32[]{:S(2)}) copy-start(s32[16,16]{1,0:T(8,128)} %two_ref.1) | copy-start | bytes 3076
  0.7 17.5 %copy-start.14 = (s32[1,24,2]{1,2,0:T(2,128)S(1)}, s32[1,24,2]{1,2,0:T(2,128)}, u32[]{:S(2)}) copy-start(s32[1,24,2]{1,2,0:T(2,128)} %param.9) | copy-start | bytes 580
  18.2 2.0 copy-start.4
  20.2 2.0 copy-start.5
  184.1 8.0 %collective-permute-start = (s16[12,384,512]{2,1,0:T(8,128)(2,1)S(1)}, s16[12,384,512]{2,1,0:T(8,128)(2,1)S(1)}, u32[]{:S(2)}, u32[]{:S(2)}) collective-permute-start(s16[12,384,512]{2,1,0:T(8,128)(2,1)S(1)} %shard_map.71), channel_id=1, source_target_pairs={{0,16},{16,0},{1,17},{17,1},{2,18},{18,2},{3,19},{19,3},{4,20},{20... | collective-permute-start | bytes 14155784 | tf_op jit(solution)/shard_map/ppermute | solution.py:357
  224.6 8.1 %copy-start.6 = (bf16[16,464,128]{2,1,0:T(8,128)(2,1)}, bf16[16,464,128]{2,1,0:T(8,128)(2,1)S(1)}, u32[]{:S(2)}) copy-start(bf16[16,464,128]{2,1,0:T(8,128)(2,1)S(1)} %all_to_all.57.refs_3_) | copy-start | bytes 5701636
  233.9 63.8 %collective-permute-start.4 = (s16[12,128,512]{2,1,0:T(8,128)(2,1)}, s16[12,128,512]{2,1,0:T(8,128)(2,1)}, u32[]{:S(2)}, u32[]{:S(2)}) collective-permute-start(s16[12,128,512]{2,1,0:T(8,128)(2,1)} %get-tuple-element.70), channel_id=1, source_target_pairs={{0,16},{16,0},{1,17},{17,1},{2,18},{18,2},{3,19},{19,3},{4,20},{20... | collective-permute-start | bytes 4718600 | tf_op jit(solution)/shard_map/ppermute | solution.py:354
  233.9 55.1 %collective-permute-start.1 = (s16[3,384,512]{2,1,0:T(8,128)(2,1)}, s16[3,384,512]{2,1,0:T(8,128)(2,1)S(1)}, u32[]{:S(2)}, u32[]{:S(2)}) collective-permute-start(s16[3,384,512]{2,1,0:T(8,128)(2,1)} %get-tuple-element.63), channel_id=1, source_target_pairs={{0,32},{32,64},{64,96},{96,0},{1,33},{33,65},{65,97},{97,1},{2,34}... | collective-permute-start | bytes 3538952 | tf_op jit(solution)/shard_map/ppermute | solution.py:363
  234.5 55.5 %collective-permute-start.2 = (s16[3,384,512]{2,1,0:T(8,128)(2,1)}, s16[3,384,512]{2,1,0:T(8,128)(2,1)S(1)}, u32[]{:S(2)}, u32[]{:S(2)}) collective-permute-start(s16[3,384,512]{2,1,0:T(8,128)(2,1)} %get-tuple-element.64), channel_id=1, source_target_pairs={{0,64},{32,96},{64,0},{96,32},{1,65},{33,97},{65,1},{97,33},{2,66}... | collective-permute-start | bytes 3538952 | tf_op jit(solution)/shard_map/ppermute | solution.py:363
  236.6 54.5 %collective-permute-start.3 = (s16[3,384,512]{2,1,0:T(8,128)(2,1)}, s16[3,384,512]{2,1,0:T(8,128)(2,1)}, u32[]{:S(2)}, u32[]{:S(2)}) collective-permute-start(s16[3,384,512]{2,1,0:T(8,128)(2,1)} %get-tuple-element.65), channel_id=1, source_target_pairs={{0,96},{32,0},{64,32},{96,64},{1,97},{33,1},{65,33},{97,65},{2,98}... | collective-permute-start | bytes 3538952 | tf_op jit(solution)/shard_map/ppermute | solution.py:363
  253.8 44.0 %copy-start.3 = (s16[12,128,512]{2,1,0:T(8,128)(2,1)S(1)}, s16[12,128,512]{2,1,0:T(8,128)(2,1)}, u32[]{:S(2)}) copy-start(s16[12,128,512]{2,1,0:T(8,128)(2,1)} %copy-done.2) | copy-start | bytes 4718596
  291.1 1.3 copy-start.8
  296.3 1.4 copy-start
  297.8 5.6 %copy-start.20 = (s32[16,16]{1,0:T(8,128)S(1)}, s32[16,16]{1,0:T(8,128)}, u32[]{:S(2)}) copy-start(s32[16,16]{1,0:T(8,128)} %copy.14) | copy-start | bytes 3076
  297.8 5.6 %copy-start.21 = (s32[16,16]{1,0:T(8,128)S(1)}, s32[16,16]{1,0:T(8,128)}, u32[]{:S(2)}) copy-start(s32[16,16]{1,0:T(8,128)} %copy.13) | copy-start | bytes 3076
  303.8 1.8 copy-start.18
  303.8 21.9 %copy-start.19 = (s32[3072]{0:T(1024)S(1)}, s32[3072]{0:T(1024)}, u32[]{:S(2)}) copy-start(s32[3072]{0:T(1024)} %eq.239) | copy-start | bytes 36868
  305.7 22.7 %collective-permute-start.5 = (s16[3,128,512]{2,1,0:T(8,128)(2,1)}, s16[3,128,512]{2,1,0:T(8,128)(2,1)S(1)}, u32[]{:S(2)}, u32[]{:S(2)}) collective-permute-start(s16[3,128,512]{2,1,0:T(8,128)(2,1)} %get-tuple-element.76), channel_id=1, source_target_pairs={{0,32},{32,64},{64,96},{96,0},{1,33},{33,65},{65,97},{97,1},{2,34}... | collective-permute-start | bytes 1179656 | tf_op jit(solution)/shard_map/ppermute | solution.py:363
  306.0 22.3 %collective-permute-start.6 = (s16[3,128,512]{2,1,0:T(8,128)(2,1)}, s16[3,128,512]{2,1,0:T(8,128)(2,1)S(1)}, u32[]{:S(2)}, u32[]{:S(2)}) collective-permute-start(s16[3,128,512]{2,1,0:T(8,128)(2,1)} %copy-done.17), channel_id=1, source_target_pairs={{0,64},{32,96},{64,0},{96,32},{1,65},{33,97},{65,1},{97,33},{2,66}... | collective-permute-start | bytes 1179656 | tf_op jit(solution)/shard_map/ppermute | solution.py:363
  308.4 19.9 %collective-permute-start.7 = (s16[3,128,512]{2,1,0:T(8,128)(2,1)}, s16[3,128,512]{2,1,0:T(8,128)(2,1)}, u32[]{:S(2)}, u32[]{:S(2)}) collective-permute-start(s16[3,128,512]{2,1,0:T(8,128)(2,1)} %copy-done.16), channel_id=1, source_target_pairs={{0,96},{32,0},{64,32},{96,64},{1,97},{33,1},{65,33},{97,65},{2,98}... | collective-permute-start | bytes 1179656 | tf_op jit(solution)/shard_map/ppermute | solution.py:363
  330.6 1.7 copy-start.1
  453.7 21.0 %copy-start.15 = (s32[1,24,2]{1,2,0:T(2,128)S(1)}, s32[1,24,2]{1,2,0:T(2,128)}, u32[]{:S(2)}) copy-start(s32[1,24,2]{1,2,0:T(2,128)} %param.9) | copy-start | bytes 580
  474.7 16.2 %copy-start.11 = (bf16[32,1024]{1,0:T(8,128)(2,1)S(1)}, bf16[32,1024]{1,0:T(8,128)(2,1)}, u32[]{:S(2)}) copy-start(bf16[32,1024]{1,0:T(8,128)(2,1)} %and_convert_fusion.1.col_hot_ref) | copy-start | bytes 196612
  (6 other events, 6.1 us)

commit v9 on v8

--- a/solution.py
+++ b/solution.py
@@ -58,9 +58,9 @@
 
 def squares(one, two, depth):
     width, rows = one.shape
-    block = pl.BlockSpec((64, rows), lambda k: (k, 0))
+    block = pl.BlockSpec((32, rows), lambda k: (k, 0))
     spec = pl.GridSpec(
-        grid=(width // 64,),
+        grid=(width // 32,),
         in_specs=[block, block],
         out_specs=pl.BlockSpec((depth, 2, rows), lambda k: (0, 0, 0)),
     )
@@ -361,7 +361,7 @@
     def to_chips(parts):
         return [parts[0]] + [
             lax.ppermute(parts[d], "aa_0", [(x, (x + d) % 4) for x in range(4)])
-            for d in range(1, 4)
+            for d in (2, 1, 3)
         ]
 
     spread, arrived = [], []

time: 494 us -> 496 us (level)
  transfers between devices with their start and end apart: 8 -> 8, of which waited for: 2 -> 3; matrix products, arithmetic and copies ran while one was open for 7% -> 7% of each run, Pallas kernels for 2% -> 2%
where the time goes in v9:
time: 496 us; the launch traced here: 494 us
  blocking collectives  344 us (69%)
  Pallas kernels  51.2 us (10%)
  local copies, waits for them, and re-layouts  45.8 us (9%)
  waiting for transfers between devices  35.9 us (7%)
  starting transfers between devices  10.9 us (2%)
  other arithmetic  5.06 us (1%)
    all_to_all x2, blocking collectives, gathered(): return lax.all_to_all(x, CROSSED, 0, 0, tiled=True)  181 us
    all_to_all x8, blocking collectives, exchanged(): return lax.all_to_all(x, ALL, 0, 0, tiled=True)  151 us
    ppermute x6, waiting for transfers between devices, to_chips(): lax.ppermute(parts[d], 'aa_0', [(x, (x + d) % 4) for x in range(4)])  33.9 us
    pallas_call x6, Pallas kernels, call(): pl.pallas_call(kernel, out_shape=out_shape, grid_spec=grid_spec, compiler...  24.2 us
    pallas_call x3, Pallas kernels, cosines(): pl.pallas_call(functools.partial(cosine_kernel, len(cores)), out_shape=[j...  19.9 us
    eq x14, local copies, waits for them, and re-layouts, hot_rows(): return ((row_id == col_id) & (row_tile == col_tile)).astype(bf16)  17.1 us
    unnamed x44, local copies, waits for them, and re-layouts  14.5 us
    all_to_all x1, blocking collectives, per_device(): sums = lax.all_to_all(sums, AA, 0, 0, tiled=True).sum(axis=0)  11.7 us
  transfers between devices with their start and end apart: 8, of which 3 were waited for; matrix products, arithmetic and copies ran while one was open for 7% of the time, Pallas kernels for 2%

profile of v9, /device:TPU:0, one launch (start us, length us, event | category | flops | bytes accessed | tf_op | source)
XLA Modules:
  0.0 493.8 jit_solution(15781530637085359278)
XLA Ops:
  0.7 8.6 %shard_map.68 = f32[8,2,4096]{2,1,0:T(2,128)S(1)} custom-call(bf16[448,4096]{1,0:T(8,128)(2,1)} %bitcast.42, bf16[448,4096]{1,0:T(8,128)(2,1)} %bitcast.44), custom_call_target="tpu_custom_call" | custom-call | flops 7340032 | bytes 14680064 | tf_op jit(solution)/shard_map/pallas_call | solution.py:36
  9.2 11.7 %all_to_all.55 = f32[8,2,4096]{2,1,0:T(2,128)S(1)} all-to-all(f32[8,2,4096]{2,1,0:T(2,128)S(1)} %shard_map.68), channel_id=1, replica_groups=mesh['aa_0'=4,'aa_1'=2,'ba_0'=4,'ba_1'=4] {'aa_0','aa_1'}, dimensions={0} | all-to-all | bytes 524288 | tf_op jit(solution)/shard_map/all_to_all | solution.py:339
  25.2 5.1 %shard_map.69 = (bf16[16,448,896]{2,1,0:T(8,128)(2,1)S(1)}, bf16[16,464,128]{2,1,0:T(8,128)(2,1)S(1)}) custom-call(s32[1]{0:T(128)} %bitcast.2.me_ref, s32[16,16]{1,0:T(8,128)S(1)} %copy-done.12, s32[16,16]{1,0:T(8,128)S(1)} %copy-done.13, bf16[448,4096]{1,0:T(8,128)(2,1)S(1)} %bitcast.43, bf16[448,4096]{1,0:T(8,128)(2,1)S(1)} %bitcast.45, ...), custom_call_target="tpu_custom_call" | custom-call | flops 14680064 | bytes 29360128 | tf_op jit(solution)/shard_map/pallas_call | solution.py:36
  30.3 150.8 %all_to_all.56.refs_1_.refs_2_ = bf16[16,448,896]{2,1,0:T(8,128)(2,1)S(1)} all-to-all(bf16[16,448,896]{2,1,0:T(8,128)(2,1)S(1)} %get-tuple-element.53), channel_id=1, replica_groups=mesh['aa_0'=4,'aa_1'=2,'ba_0'=4,'ba_1'=4] {'ba_1','ba_0'}, dimensions={0} | all-to-all | bytes 25690112 | tf_op jit(solution)/shard_map/all_to_all | solution.py:349
  181.1 5.9 %shard_map.71 = s16[12,384,512]{2,1,0:T(8,128)(2,1)S(1)} custom-call(s32[2,24]{1,0:T(2,128)S(1)} %bitcast.49, s32[1]{0:T(128)} %bitcast.5.refs_0_, bf16[16,448,896]{2,1,0:T(8,128)(2,1)S(1)} %all_to_all.56.refs_1_.refs_2_), custom_call_target="tpu_custom_call" | custom-call | flops 2113929216 | bytes 8257536 | tf_op jit(solution)/shard_map/pallas_call | solution.py:133
  187.2 5.9 %shard_map.70.refs_0_.refs_1_.refs_2_.refs_3_ = s16[12,384,512]{2,1,0:T(8,128)(2,1)S(1)} custom-call(s32[2,24]{1,0:T(2,128)S(1)} %bitcast.50, s32[1]{0:T(128)} %bitcast.4.refs_0_.refs_1_.core_ref, bf16[16,448,896]{2,1,0:T(8,128)(2,1)S(1)} %all_to_all.56.refs_1_.refs_2_), custom_call_target="tpu_custom_call" | custom-call | flops 2113929216 | bytes 8257536 | tf_op jit(solution)/shard_map/pallas_call | solution.py:133
  195.0 2.5 shard_map.72
  197.5 30.0 %all_to_all.57.refs_3_ = bf16[16,464,128]{2,1,0:T(8,128)(2,1)S(1)} all-to-all(bf16[16,464,128]{2,1,0:T(8,128)(2,1)S(1)} %get-tuple-element.68), channel_id=1, replica_groups=mesh['aa_0'=4,'aa_1'=2,'ba_0'=4,'ba_1'=4] {'ba_1','ba_0'}, dimensions={0} | all-to-all | bytes 3801088 | tf_op jit(solution)/shard_map/all_to_all | solution.py:349
  227.5 8.1 %shard_map.74 = (s16[12,128,512]{2,1,0:T(8,128)(2,1)}, s16[12,128,512]{2,1,0:T(8,128)(2,1)S(1)}) custom-call(s32[2,24]{1,0:T(2,128)S(1)} %bitcast.51, s32[1]{0:T(128)} %bitcast.5.refs_0_, s32[1]{0:T(128)} %bitcast.4.refs_0_.refs_1_.core_ref, bf16[16,448,896]{2,1,0:T(8,128)(2,1)S(1)} %all_to_all.56.refs_1_.refs_2_, bf16[16,464,128]{2,1,0:T(8,128)(2,1)S(1)} %all_to_all.57.refs_3_), custom_call_target="tpu_custom_call" | custom-call | flops 1409286144 | bytes 5505024 | tf_op jit(solution)/shard_map/pallas_call | solution.py:133
  236.9 2.6 collective-permute-start.1
  239.5 3.2 collective-permute-start.3
  257.3 10.1 %collective-permute-done.1.b_ref = s16[3,384,512]{2,1,0:T(8,128)(2,1)S(1)} collective-permute-done((s16[3,384,512]{2,1,0:T(8,128)(2,1)}, s16[3,384,512]{2,1,0:T(8,128)(2,1)S(1)}, u32[]{:S(2)}, u32[]{:S(2)}) %collective-permute-start.1) | collective-permute-done | bytes 1179680 | tf_op jit(solution)/shard_map/ppermute | solution.py:363
  268.5 23.8 %collective-permute-done.2.c_ref = s16[3,384,512]{2,1,0:T(8,128)(2,1)S(1)} collective-permute-done((s16[3,384,512]{2,1,0:T(8,128)(2,1)}, s16[3,384,512]{2,1,0:T(8,128)(2,1)S(1)}, u32[]{:S(2)}, u32[]{:S(2)}) %collective-permute-start.2) | collective-permute-done | bytes 1179680 | tf_op jit(solution)/shard_map/ppermute | solution.py:363
  295.8 2.7 shard_map.73
  300.0 3.2 shard_map.75
  309.7 3.2 collective-permute-start.7
  335.6 17.6 %all_to_all.58.got_ref = bf16[128,16,128]{2,1,0:T(8,128)(2,1)S(1)} all-to-all(bf16[128,16,128]{2,1,0:T(8,128)(2,1)S(1)} %shard_map.77), channel_id=1, replica_groups=mesh['aa_0'=4,'aa_1'=2,'ba_0'=4,'ba_1'=4] {'ba_0','ba_1','aa_1','aa_0'}, dimensions={0} | all-to-all | bytes 1048576 | tf_op jit(solution)/shard_map/all_to_all | solution.py:303
  353.9 17.6 %all_to_all.59.got_ref = bf16[128,16,128]{2,1,0:T(8,128)(2,1)S(1)} all-to-all(bf16[128,16,128]{2,1,0:T(8,128)(2,1)S(1)} %shard_map.78), channel_id=1, replica_groups=mesh['aa_0'=4,'aa_1'=2,'ba_0'=4,'ba_1'=4] {'ba_0','ba_1','aa_1','aa_0'}, dimensions={0} | all-to-all | bytes 1048576 | tf_op jit(solution)/shard_map/all_to_all | solution.py:303
  372.2 20.4 %all_to_all.60.got_ref = bf16[128,24,128]{2,1,0:T(8,128)(2,1)S(1)} all-to-all(bf16[128,24,128]{2,1,0:T(8,128)(2,1)S(1)} %shard_map.79), channel_id=1, replica_groups=mesh['aa_0'=4,'aa_1'=2,'ba_0'=4,'ba_1'=4] {'ba_0','ba_1','aa_1','aa_0'}, dimensions={0} | all-to-all | bytes 1572864 | tf_op jit(solution)/shard_map/all_to_all | solution.py:303
  393.4 20.2 %all_to_all.61.got_ref = bf16[128,24,128]{2,1,0:T(8,128)(2,1)S(1)} all-to-all(bf16[128,24,128]{2,1,0:T(8,128)(2,1)S(1)} %shard_map.80), channel_id=1, replica_groups=mesh['aa_0'=4,'aa_1'=2,'ba_0'=4,'ba_1'=4] {'ba_0','ba_1','aa_1','aa_0'}, dimensions={0} | all-to-all | bytes 1572864 | tf_op jit(solution)/shard_map/all_to_all | solution.py:303
  414.4 20.2 %all_to_all.62.got_ref = bf16[128,24,128]{2,1,0:T(8,128)(2,1)S(1)} all-to-all(bf16[128,24,128]{2,1,0:T(8,128)(2,1)S(1)} %shard_map.81), channel_id=1, replica_groups=mesh['aa_0'=4,'aa_1'=2,'ba_0'=4,'ba_1'=4] {'ba_0','ba_1','aa_1','aa_0'}, dimensions={0} | all-to-all | bytes 1572864 | tf_op jit(solution)/shard_map/all_to_all | solution.py:303
  435.4 20.2 %all_to_all.63.got_ref = bf16[128,24,128]{2,1,0:T(8,128)(2,1)S(1)} all-to-all(bf16[128,24,128]{2,1,0:T(8,128)(2,1)S(1)} %shard_map.82), channel_id=1, replica_groups=mesh['aa_0'=4,'aa_1'=2,'ba_0'=4,'ba_1'=4] {'ba_0','ba_1','aa_1','aa_0'}, dimensions={0} | all-to-all | bytes 1572864 | tf_op jit(solution)/shard_map/all_to_all | solution.py:303
  456.4 20.2 %all_to_all.64.got_ref.row_got_ref = bf16[128,24,128]{2,1,0:T(8,128)(2,1)S(1)} all-to-all(bf16[128,24,128]{2,1,0:T(8,128)(2,1)S(1)} %shard_map.83), channel_id=1, replica_groups=mesh['aa_0'=4,'aa_1'=2,'ba_0'=4,'ba_1'=4] {'ba_0','ba_1','aa_1','aa_0'}, dimensions={0} | all-to-all | bytes 1572864 | tf_op jit(solution)/shard_map/all_to_all | solution.py:303
  478.0 14.9 %all_to_all.65.col_got_ref = bf16[128,8,128]{2,1,0:T(8,128)(2,1)S(1)} all-to-all(bf16[128,8,128]{2,1,0:T(8,128)(2,1)S(1)} %shard_map.84), channel_id=1, replica_groups=mesh['aa_0'=4,'aa_1'=2,'ba_0'=4,'ba_1'=4] {'ba_0','ba_1','aa_1','aa_0'}, dimensions={0} | all-to-all | bytes 524288 | tf_op jit(solution)/shard_map/all_to_all | solution.py:303
  (122 shorter events, 63.9 us)
Async XLA Ops:
  0.6 20.4 %copy-start.12 = (s32[16,16]{1,0:T(8,128)S(1)}, s32[16,16]{1,0:T(8,128)}, u32[]{:S(2)}) copy-start(s32[16,16]{1,0:T(8,128)} %one_ref.1) | copy-start | bytes 3076
  0.6 20.4 %copy-start.13 = (s32[16,16]{1,0:T(8,128)S(1)}, s32[16,16]{1,0:T(8,128)}, u32[]{:S(2)}) copy-start(s32[16,16]{1,0:T(8,128)} %two_ref.1) | copy-start | bytes 3076
  0.7 20.4 %copy-start.14 = (s32[1,24,2]{1,2,0:T(2,128)S(1)}, s32[1,24,2]{1,2,0:T(2,128)}, u32[]{:S(2)}) copy-start(s32[1,24,2]{1,2,0:T(2,128)} %param.9) | copy-start | bytes 580
  21.1 2.0 copy-start.4
  23.2 2.0 copy-start.5
  187.1 8.0 %collective-permute-start = (s16[12,384,512]{2,1,0:T(8,128)(2,1)S(1)}, s16[12,384,512]{2,1,0:T(8,128)(2,1)S(1)}, u32[]{:S(2)}, u32[]{:S(2)}) collective-permute-start(s16[12,384,512]{2,1,0:T(8,128)(2,1)S(1)} %shard_map.71), channel_id=1, source_target_pairs={{0,16},{16,0},{1,17},{17,1},{2,18},{18,2},{3,19},{19,3},{4,20},{20... | collective-permute-start | bytes 14155784 | tf_op jit(solution)/shard_map/ppermute | solution.py:357
  227.5 8.1 %copy-start.6 = (bf16[16,464,128]{2,1,0:T(8,128)(2,1)}, bf16[16,464,128]{2,1,0:T(8,128)(2,1)S(1)}, u32[]{:S(2)}) copy-start(bf16[16,464,128]{2,1,0:T(8,128)(2,1)S(1)} %all_to_all.57.refs_3_) | copy-start | bytes 5701636
  236.9 63.1 %collective-permute-start.4 = (s16[12,128,512]{2,1,0:T(8,128)(2,1)}, s16[12,128,512]{2,1,0:T(8,128)(2,1)}, u32[]{:S(2)}, u32[]{:S(2)}) collective-permute-start(s16[12,128,512]{2,1,0:T(8,128)(2,1)} %get-tuple-element.70), channel_id=1, source_target_pairs={{0,16},{16,0},{1,17},{17,1},{2,18},{18,2},{3,19},{19,3},{4,20},{20... | collective-permute-start | bytes 4718600 | tf_op jit(solution)/shard_map/ppermute | solution.py:354
  236.9 30.6 %collective-permute-start.1 = (s16[3,384,512]{2,1,0:T(8,128)(2,1)}, s16[3,384,512]{2,1,0:T(8,128)(2,1)S(1)}, u32[]{:S(2)}, u32[]{:S(2)}) collective-permute-start(s16[3,384,512]{2,1,0:T(8,128)(2,1)} %get-tuple-element.63), channel_id=1, source_target_pairs={{0,64},{32,96},{64,0},{96,32},{1,65},{33,97},{65,1},{97,33},{2,66}... | collective-permute-start | bytes 3538952 | tf_op jit(solution)/shard_map/ppermute | solution.py:363
  239.5 52.7 %collective-permute-start.2 = (s16[3,384,512]{2,1,0:T(8,128)(2,1)}, s16[3,384,512]{2,1,0:T(8,128)(2,1)S(1)}, u32[]{:S(2)}, u32[]{:S(2)}) collective-permute-start(s16[3,384,512]{2,1,0:T(8,128)(2,1)} %get-tuple-element.64), channel_id=1, source_target_pairs={{0,32},{32,64},{64,96},{96,0},{1,33},{33,65},{65,97},{97,1},{2,34}... | collective-permute-start | bytes 3538952 | tf_op jit(solution)/shard_map/ppermute | solution.py:363
  239.5 53.8 %collective-permute-start.3 = (s16[3,384,512]{2,1,0:T(8,128)(2,1)}, s16[3,384,512]{2,1,0:T(8,128)(2,1)}, u32[]{:S(2)}, u32[]{:S(2)}) collective-permute-start(s16[3,384,512]{2,1,0:T(8,128)(2,1)} %get-tuple-element.65), channel_id=1, source_target_pairs={{0,96},{32,0},{64,32},{96,64},{1,97},{33,1},{65,33},{97,65},{2,98}... | collective-permute-start | bytes 3538952 | tf_op jit(solution)/shard_map/ppermute | solution.py:363
  257.3 42.7 %copy-start.3 = (s16[12,128,512]{2,1,0:T(8,128)(2,1)S(1)}, s16[12,128,512]{2,1,0:T(8,128)(2,1)}, u32[]{:S(2)}) copy-start(s16[12,128,512]{2,1,0:T(8,128)(2,1)} %copy-done.2) | copy-start | bytes 4718596
  293.3 1.3 copy-start.8
  298.6 1.4 copy-start
  300.0 5.6 %copy-start.20 = (s32[16,16]{1,0:T(8,128)S(1)}, s32[16,16]{1,0:T(8,128)}, u32[]{:S(2)}) copy-start(s32[16,16]{1,0:T(8,128)} %copy.14) | copy-start | bytes 3076
  300.0 5.6 %copy-start.21 = (s32[16,16]{1,0:T(8,128)S(1)}, s32[16,16]{1,0:T(8,128)}, u32[]{:S(2)}) copy-start(s32[16,16]{1,0:T(8,128)} %copy.13) | copy-start | bytes 3076
  306.1 1.8 copy-start.18
  306.1 22.8 %copy-start.19 = (s32[3072]{0:T(1024)S(1)}, s32[3072]{0:T(1024)}, u32[]{:S(2)}) copy-start(s32[3072]{0:T(1024)} %eq.239) | copy-start | bytes 36868
  307.9 23.6 %collective-permute-start.5 = (s16[3,128,512]{2,1,0:T(8,128)(2,1)}, s16[3,128,512]{2,1,0:T(8,128)(2,1)S(1)}, u32[]{:S(2)}, u32[]{:S(2)}) collective-permute-start(s16[3,128,512]{2,1,0:T(8,128)(2,1)} %get-tuple-element.76), channel_id=1, source_target_pairs={{0,64},{32,96},{64,0},{96,32},{1,65},{33,97},{65,1},{97,33},{2,66}... | collective-permute-start | bytes 1179656 | tf_op jit(solution)/shard_map/ppermute | solution.py:363
  309.7 21.8 %collective-permute-start.6 = (s16[3,128,512]{2,1,0:T(8,128)(2,1)}, s16[3,128,512]{2,1,0:T(8,128)(2,1)S(1)}, u32[]{:S(2)}, u32[]{:S(2)}) collective-permute-start(s16[3,128,512]{2,1,0:T(8,128)(2,1)} %copy-done.17), channel_id=1, source_target_pairs={{0,32},{32,64},{64,96},{96,0},{1,33},{33,65},{65,97},{97,1},{2,34}... | collective-permute-start | bytes 1179656 | tf_op jit(solution)/shard_map/ppermute | solution.py:363
  309.7 21.8 %collective-permute-start.7 = (s16[3,128,512]{2,1,0:T(8,128)(2,1)}, s16[3,128,512]{2,1,0:T(8,128)(2,1)}, u32[]{:S(2)}, u32[]{:S(2)}) collective-permute-start(s16[3,128,512]{2,1,0:T(8,128)(2,1)} %copy-done.16), channel_id=1, source_target_pairs={{0,96},{32,0},{64,32},{96,64},{1,97},{33,1},{65,33},{97,65},{2,98}... | collective-permute-start | bytes 1179656 | tf_op jit(solution)/shard_map/ppermute | solution.py:363
  333.7 1.7 copy-start.1
  455.6 21.0 %copy-start.15 = (s32[1,24,2]{1,2,0:T(2,128)S(1)}, s32[1,24,2]{1,2,0:T(2,128)}, u32[]{:S(2)}) copy-start(s32[1,24,2]{1,2,0:T(2,128)} %param.9) | copy-start | bytes 580
  476.6 16.2 %copy-start.11 = (bf16[32,1024]{1,0:T(8,128)(2,1)S(1)}, bf16[32,1024]{1,0:T(8,128)(2,1)}, u32[]{:S(2)}) copy-start(bf16[32,1024]{1,0:T(8,128)(2,1)} %and_convert_fusion.1.col_hot_ref) | copy-start | bytes 196612
  (6 other events, 6.1 us)
